TPU v7x, 32 devices: a 4x4x1 block of a 4x4x8 slice. The times are simulated.
32 devices in a mesh: dp: 1 (over z), tp: 4 (over y), ep: 8 (over x, core).
Axes of the slice: x: 4, y: 4, z: 1, core: 2. Of those that a mesh axis runs over, the one named last changes fastest.
The devices are a block of a 4x4x8 slice.
Arguments:
- hidden_in: bfloat16 [1024, 2048], P(('dp', 'ep'))
- positions: int32 [1024], P(('dp', 'ep'))
- expert_ids: int32 [1024, 2], P(('dp', 'ep'))
- k_cache: bfloat16 [1024, 64, 4, 128], P(('dp', 'ep'), None, 'tp')
- v_cache: bfloat16 [1024, 64, 4, 128], P(('dp', 'ep'), None, 'tp')
- norm_in: bfloat16 [2048], replicated
- norm_res: bfloat16 [2048], replicated
- norm_post: bfloat16 [2048], replicated
- w_q: bfloat16 [2048, 4096], P(None, 'tp')
- w_k: bfloat16 [2048, 512], P(None, 'tp')
- w_v: bfloat16 [2048, 512], P(None, 'tp')
- w_o: bfloat16 [4096, 2048], P('tp')
- w_gate: bfloat16 [2048, 6144], P(None, 'tp')
- w_up: bfloat16 [2048, 6144], P(None, 'tp')
- w_down: bfloat16 [6144, 2048], P('tp')
- w_router: bfloat16 [2048, 128], replicated
- e_gate: bfloat16 [128, 2048, 768], P('ep', None, 'tp')
- e_up: bfloat16 [128, 2048, 768], P('ep', None, 'tp')
- e_down: bfloat16 [128, 768, 2048], P('ep', 'tp')
Outputs:
- output 1: bfloat16 [1024, 2048], P(('dp', 'ep'))
- output 2: bfloat16 [1024, 64, 4, 128], P(('dp', 'ep'), None, 'tp')
- output 3: bfloat16 [1024, 64, 4, 128], P(('dp', 'ep'), None, 'tp')
All inputs are finite; a program needn't handle non-finite values.
Results may differ from a plain program's by a relative error of at most 0.0136629.
Values are sent between devices in bfloat16 or wider.
A program may use at most 768 MiB of HBM per device.

v0:
```python
import jax
import jax.numpy as jnp
from jax import lax
from jax.sharding import PartitionSpec as P

NORM_EPS = 1e-5
ROPE_BASE = 10000.0


def rms_norm(values, gain_vec):
    wide_vals = values.astype(jnp.float32)
    inv_rms = lax.rsqrt(jnp.mean(wide_vals * wide_vals, axis=-1, keepdims=True) + NORM_EPS)
    return (wide_vals * inv_rms * gain_vec.astype(jnp.float32)).astype(jnp.bfloat16)


def rope_rotate(values, positions):
    half_dim = values.shape[-1] // 2
    inv_freq = 1.0 / (ROPE_BASE ** (jnp.arange(0, 2 * half_dim, 2, dtype=jnp.float32) / (2 * half_dim)))
    angles = positions.astype(jnp.float32)[:, None] * inv_freq[None, :]
    cosine = jnp.cos(angles)[:, None, :]
    sine_part = jnp.sin(angles)[:, None, :]
    first_half = values[..., :half_dim]
    second_half = values[..., half_dim:]
    return jnp.concatenate([first_half * cosine - second_half * sine_part, second_half * cosine + first_half * sine_part], axis=-1)


def attention_block(normed, positions, k_cache, v_cache, w_q, w_k, w_v):
    tokens = normed.shape[0]
    cache_len, kv_heads, head_dim = k_cache.shape[1], k_cache.shape[2], k_cache.shape[3]
    q_heads = w_q.shape[1] // head_dim
    group_size = q_heads // kv_heads
    q_proj = jnp.dot(normed, w_q, preferred_element_type=jnp.float32).reshape(tokens, q_heads, head_dim)
    k_proj = jnp.dot(normed, w_k, preferred_element_type=jnp.float32).reshape(tokens, kv_heads, head_dim)
    v_new = jnp.dot(normed, w_v, preferred_element_type=jnp.float32).astype(jnp.bfloat16).reshape(tokens, kv_heads, head_dim)
    q_rot = rope_rotate(q_proj, positions).astype(jnp.bfloat16).reshape(tokens, kv_heads, group_size, head_dim)
    k_rot = rope_rotate(k_proj, positions).astype(jnp.bfloat16)
    slot_hit = (jnp.arange(cache_len)[None, :] == positions[:, None])[:, :, None, None]
    k_out = jnp.where(slot_hit, k_rot[:, None], k_cache)
    v_out = jnp.where(slot_hit, v_new[:, None], v_cache)
    scores = jnp.einsum('bkgd,btkd->bkgt', q_rot, k_out, preferred_element_type=jnp.float32) * (head_dim ** -0.5)
    visible = jnp.arange(cache_len)[None, None, None, :] <= positions[:, None, None, None]
    attn_probs = jax.nn.softmax(jnp.where(visible, scores, -jnp.inf), axis=-1).astype(jnp.bfloat16)
    mixed_vals = jnp.einsum('bkgt,btkd->bkgd', attn_probs, v_out, preferred_element_type=jnp.float32)
    return mixed_vals.astype(jnp.bfloat16).reshape(tokens, q_heads * head_dim), k_out, v_out


def dense_block(hidden_mid, norm_res, w_gate, w_up, w_down):
    res_in = rms_norm(hidden_mid, norm_res)
    gate_val = jnp.dot(res_in, w_gate, preferred_element_type=jnp.float32)
    up_val = jnp.dot(res_in, w_up, preferred_element_type=jnp.float32)
    act_val = (jax.nn.silu(gate_val) * up_val).astype(jnp.bfloat16)
    return jnp.dot(act_val, w_down, preferred_element_type=jnp.float32)


def route_weights(moe_in, w_router, expert_ids):
    gate_probs = jax.nn.softmax(jnp.dot(moe_in, w_router, preferred_element_type=jnp.float32), axis=-1)
    picked = jnp.take_along_axis(gate_probs, expert_ids, axis=1)
    return picked / jnp.sum(picked, axis=1, keepdims=True)


def run_experts(slot_rows, slot_expert, e_gate, e_up, e_down):
    sort_order = jnp.argsort(slot_expert, stable=True)
    sorted_rows = slot_rows[sort_order]
    group_sizes = jnp.bincount(slot_expert, length=e_gate.shape[0]).astype(jnp.int32)
    gate_val = lax.ragged_dot(sorted_rows, e_gate, group_sizes, preferred_element_type=jnp.float32)
    up_val = lax.ragged_dot(sorted_rows, e_up, group_sizes, preferred_element_type=jnp.float32)
    act_val = (jax.nn.silu(gate_val) * up_val).astype(jnp.bfloat16)
    out_sorted = lax.ragged_dot(act_val, e_down, group_sizes, preferred_element_type=jnp.float32).astype(jnp.bfloat16)
    return out_sorted[jnp.argsort(sort_order)]


def solution(mesh):
    ep_size = mesh.shape['ep']
    row_spec = P(('dp', 'ep'), None)
    cache_spec = P(('dp', 'ep'), None, 'tp', None)
    col_split = P(None, 'tp')
    row_split = P('tp', None)
    in_specs = (row_spec, P(('dp', 'ep')), row_spec, cache_spec, cache_spec, P(None), P(None), P(None), col_split, col_split, col_split, row_split, col_split, col_split, row_split, P(None, None), P('ep', None, 'tp'), P('ep', None, 'tp'), P('ep', 'tp', None))
    out_specs = (row_spec, cache_spec, cache_spec)

    def local_layer(hidden_in, positions, expert_ids, k_cache, v_cache, norm_in, norm_res, norm_post, w_q, w_k, w_v, w_o, w_gate, w_up, w_down, w_router, e_gate, e_up, e_down):
        tokens, model_dim = hidden_in.shape
        local_experts = e_gate.shape[0]
        capacity = 4 * tokens // ep_size
        attn_mix, k_out, v_out = attention_block(rms_norm(hidden_in, norm_in), positions, k_cache, v_cache, w_q, w_k, w_v)
        attn_sum = lax.psum(jnp.dot(attn_mix, w_o, preferred_element_type=jnp.float32).astype(jnp.bfloat16), 'tp')
        hidden_mid = (hidden_in.astype(jnp.float32) + attn_sum.astype(jnp.float32)).astype(jnp.bfloat16)
        dense_sum = lax.psum(dense_block(hidden_mid, norm_res, w_gate, w_up, w_down).astype(jnp.bfloat16), 'tp')
        moe_in = rms_norm(hidden_in, norm_post)
        route_wts = route_weights(moe_in, w_router, expert_ids)
        flat_ids = expert_ids.reshape(-1)
        dest_shard = flat_ids // local_experts
        dest_hot = (dest_shard[:, None] == jnp.arange(ep_size)[None, :]).astype(jnp.int32)
        rank_in_dest = jnp.sum((jnp.cumsum(dest_hot, axis=0) - dest_hot) * dest_hot, axis=1)
        slot_index = dest_shard * capacity + rank_in_dest
        pair_token = jnp.arange(2 * tokens, dtype=jnp.int32) // 2
        send_token = jnp.full((ep_size * capacity,), tokens, jnp.int32).at[slot_index].set(pair_token)
        send_expert = jnp.zeros((ep_size * capacity,), jnp.int32).at[slot_index].set(flat_ids % local_experts)
        padded_rows = jnp.concatenate([moe_in, jnp.zeros((1, model_dim), jnp.bfloat16)], axis=0)
        send_rows = padded_rows[send_token]
        recv_rows = lax.all_to_all(send_rows, 'ep', 0, 0, tiled=True)
        recv_expert = lax.all_to_all(send_expert, 'ep', 0, 0, tiled=True)
        expert_part = run_experts(recv_rows, recv_expert, e_gate, e_up, e_down)
        expert_sum = lax.psum(expert_part, 'tp')
        returned = lax.all_to_all(expert_sum, 'ep', 0, 0, tiled=True)
        pair_out = returned[slot_index].reshape(tokens, 2, model_dim)
        moe_out = jnp.sum(route_wts[:, :, None] * pair_out, axis=1)
        hidden_out = (hidden_mid.astype(jnp.float32) + dense_sum.astype(jnp.float32) + moe_out).astype(jnp.bfloat16)
        return hidden_out, k_out, v_out

    return jax.shard_map(local_layer, mesh=mesh, in_specs=in_specs, out_specs=out_specs, check_vma=False)
```

profile of v0, /device:TPU:97, one launch (start us, length us, event | category | flops | bytes accessed | tf_op | source)
XLA Modules:
  0.0 312.1 jit_solution(17322326240815669850)
XLA Ops:
  7.3 0.8 convert_element_type.95
  8.1 0.7 iota_compare_fusion.1
  8.8 1.2 fusion.21
  10.0 0.7 convert_element_type.93
  11.0 1.6 convolution_bitcast_fusion.1
  13.0 0.4 convolution_convert_fusion.2
  13.4 3.1 convolution_bitcast_fusion
  16.9 1.2 copy-done.5
  18.1 2.6 broadcast_select_fusion.1
  20.7 1.3 copy-done.1
  22.0 1.2 fusion.13
  23.6 3.5 %fusion.16 = bf16[128,8,128]{2,1,0:T(8,128)(2,1)S(1)} fusion(bf16[128,64,1,128]{3,1,2,0:T(8,128)(2,1)} %get-tuple-element.33, f32[128,8]{1,0:T(8,128)S(1)} %fusion.68, f32[128,8,64]{2,1,0:T(8,128)S(1)} %fusion.13), kind=kOutput, calls=%fused_computation.33 | convolution fusion | flops 17105984 | bytes 2625536 | tf_op jit(solution)/shard_map/bkgt,btkd->bkgd/dot_general | solution.py:43
  27.1 3.7 %convolution_convert_fusion.1 = bf16[128,2048]{1,0:T(8,128)(2,1)} fusion(bf16[1024,2048]{1,0:T(8,128)(2,1)} %param.30, bf16[16,8,8,128]{3,2,1,0:T(8,128)(2,1)S(1)} %bitcast.61), kind=kOutput, calls=%fused_computation.12 | convolution fusion | flops 537133056 | bytes 4980736 | tf_op jit(solution)/shard_map/dot_general | solution.py:86
  31.5 0.6 reduce-window.6
  32.4 1.4 scatter_custom_fusion.1
  33.8 0.7 all_to_all.27
  34.5 6.0 %all-to-all-start.1 = ((s32[8,64,1]{1,2,0:T(1,128)}), s32[8,64,1]{1,2,0:T(1,128)S(1)}, u32[]{:S(2)}, u32[]{:S(2)}) async-start(s32[8,64,1]{1,2,0:T(1,128)} %bitcast.10), calls=%async_computation.1 | async-start | bytes 8192 | tf_op jit(solution)/shard_map/all_to_all | solution.py:102
  40.5 1.4 scatter_custom_fusion
  42.0 20.6 %copy.57 = bf16[16,2048,192]{2,1,0:T(8,128)(2,1)} copy(bf16[16,2048,192]{1,2,0:T(8,128)(2,1)} %param.35) | data formatting | bytes 25165824 | tf_op args[16]
  62.6 20.6 %copy.58 = bf16[16,2048,192]{2,1,0:T(8,128)(2,1)} copy(bf16[16,2048,192]{1,2,0:T(8,128)(2,1)} %param.36) | data formatting | bytes 25165824 | tf_op args[17]
  83.2 0.6 broadcast.437
  83.8 0.7 fusion.65
  84.6 4.7 %scatter_custom_fusion.2 = s32[16]{0:T(128)} fusion(s32[512]{0:T(512)S(1)} %reshape.479, s32[512]{0:T(512)S(1)} %broadcast.358, s32[]{:T(128)} %constant.89.clone.1), kind=kCustom, calls=%fused_computation.123 | custom fusion | flops 512 | bytes 68 | tf_op jit(solution)/shard_map/scatter-add | solution.py:64
  89.3 2.0 ragged-dot-metadata
  91.3 3.8 %sort.34 = (s32[512]{0:T(512)}, s32[512]{0:T(512)S(1)}) sort(s32[512]{0:T(512)S(1)} %all_to_all.29, s32[512]{0:T(512)S(1)} %iota.44), dimensions={0}, to_apply=%region_14.15 | sort | flops 4608 | bytes 8192 | tf_op jit(solution)/shard_map/jit(argsort)/sort | solution.py:62
  95.1 3.8 %sort.35 = (s32[512]{0:T(512)}, s32[512]{0:T(512)S(1)}) sort(s32[512]{0:T(512)S(1)} %get-tuple-element.5, s32[512]{0:T(512)S(1)} %iota.45), dimensions={0}, to_apply=%region_16.17 | sort | flops 4608 | bytes 8192 | tf_op jit(solution)/shard_map/jit(argsort)/sort | solution.py:69
  98.9 1.4 fusion.23
  100.4 3.3 %gather_fusion = bf16[512,2048]{1,0:T(8,128)(2,1)} fusion(bf16[129,2048]{1,0:T(8,128)(2,1)S(1)} %concatenate.27, s32[1024]{0:T(1024)S(1)} %pad_clamp_fusion.3), kind=kCustom, calls=%fused_computation | custom fusion | bytes 4196352 | tf_op jit(solution)/shard_map/gather | solution.py:100
  103.7 4.8 %all-to-all-start = ((bf16[8,64,2048]{2,1,0:T(8,128)(2,1)}), bf16[8,64,2048]{2,1,0:T(8,128)(2,1)S(1)}, u32[]{:S(2)}, u32[]{:S(2)}) async-start(bf16[8,64,2048]{2,1,0:T(8,128)(2,1)} %bitcast.59), calls=%async_computation | async-start | bytes 4194304 | tf_op jit(solution)/shard_map/all_to_all | solution.py:101
  108.5 4.7 %fusion.37 = f32[128,1536]{1,0:T(8,128)} fusion(bf16[2048,1536]{1,0:T(8,128)(2,1)} %param.31, bf16[128,2048]{1,0:T(8,128)(2,1)S(1)} %get-tuple-element.26, f32[2048]{0:T(1024)S(1)} %convert_element_type.103, f32[128]{0:T(128)S(1)} %add_rsqrt_fusion), kind=kOutput, calls=%fused_computation.56 | convolution fusion | flops 806354944 | bytes 7610880 | tf_op jit(solution)/shard_map/dot_general | solution.py:49
  113.3 7.7 %convolution_convert_fusion = bf16[128,2048]{1,0:T(8,128)(2,1)} fusion(bf16[1536,2048]{1,0:T(8,128)(2,1)} %param.33, bf16[2048,1536]{1,0:T(8,128)(2,1)} %param.32, f32[128,1536]{1,0:T(8,128)} %fusion.37, bf16[128,2048]{1,0:T(8,128)(2,1)S(1)} %get-tuple-element.26, f32[2048]{0:T(1024)S(1)} %convert_element_type.103, f32[128]{0:T(128)S(1)} %add_rsqrt_fusion), kind=kOutput, calls=%fused_computation.11 | convolution fusion | flops 1613103104 | bytes 14426624 | tf_op jit(solution)/shard_map/dot_general | solution.py:52
  120.9 13.6 %all-to-all-done = bf16[8,64,2048]{2,1,0:T(8,128)(2,1)S(1)} async-done(((bf16[8,64,2048]{2,1,0:T(8,128)(2,1)}), bf16[8,64,2048]{2,1,0:T(8,128)(2,1)S(1)}, u32[]{:S(2)}, u32[]{:S(2)}) %all-to-all-start) | async-done | bytes 2097184 | tf_op jit(solution)/shard_map/all_to_all | solution.py:101
  134.5 3.3 %gather_fusion.1 = bf16[512,2048]{1,0:T(8,128)(2,1)} fusion(bf16[512,2048]{1,0:T(8,128)(2,1)S(1)} %bitcast.56, s32[1024]{0:T(1024)S(1)} %pad_clamp_fusion.2), kind=kCustom, calls=%fused_computation.1 | custom fusion | bytes 4196352 | tf_op jit(solution)/shard_map/gather | solution.py:63
  137.8 18.6 %ragged-dot-none.2 = f32[512,192]{1,0:T(8,128)} custom-call(s32[1]{0:T(128)} %get-tuple-element.7, s32[17]{0:T(128)} %get-tuple-element.8, s32[17]{0:T(128)} %get-tuple-element.9, s32[17]{0:T(128)} %get-tuple-element.10, s32[1]{0:T(128)} %get-tuple-element.7, bf16[512,2048]{1,0:T(8,128)(2,1)} %gather_fusion.1, bf16[16,2048,192]{2,1,0:T(8,128)(2,1)} %copy.57), custom_call_target="tpu_custom_call" | custom-call | flops 402653184 | bytes 15073344 | tf_op jit(solution)/shard_map/ragged_dot_general/ragged-dot-none
  156.4 18.7 %ragged-dot-none.1 = f32[512,192]{1,0:T(8,128)} custom-call(s32[1]{0:T(128)} %get-tuple-element.7, s32[17]{0:T(128)} %get-tuple-element.8, s32[17]{0:T(128)} %get-tuple-element.9, s32[17]{0:T(128)} %get-tuple-element.10, s32[1]{0:T(128)} %get-tuple-element.7, bf16[512,2048]{1,0:T(8,128)(2,1)} %gather_fusion.1, bf16[16,2048,192]{2,1,0:T(8,128)(2,1)} %copy.58), custom_call_target="tpu_custom_call" | custom-call | flops 402653184 | bytes 15073344 | tf_op jit(solution)/shard_map/ragged_dot_general/ragged-dot-none
  175.1 1.9 multiply_convert_fusion
  177.0 18.2 %ragged-dot-none = f32[512,2048]{1,0:T(8,128)} custom-call(s32[1]{0:T(128)} %get-tuple-element.7, s32[17]{0:T(128)} %get-tuple-element.8, s32[17]{0:T(128)} %get-tuple-element.9, s32[17]{0:T(128)} %get-tuple-element.10, s32[1]{0:T(128)} %get-tuple-element.7, bf16[512,192]{1,0:T(8,128)(2,1)} %multiply_convert_fusion, bf16[16,192,2048]{2,1,0:T(8,128)(2,1)} %param.37), custom_call_target="tpu_custom_call" | custom-call | flops 402653184 | bytes 16973888 | tf_op jit(solution)/shard_map/ragged_dot_general/ragged-dot-none
  195.2 2.5 convert_element_type.113
  197.7 3.3 %gather_fusion.2 = bf16[512,2048]{1,0:T(8,128)(2,1)} fusion(bf16[512,2048]{1,0:T(8,128)(2,1)S(1)} %convert_element_type.113, s32[1024]{0:T(1024)S(1)} %pad_clamp_fusion.1), kind=kCustom, calls=%fused_computation.2 | custom fusion | bytes 4196352 | tf_op jit(solution)/shard_map/gather | solution.py:69
  201.0 64.1 %all-reduce.7.cloned.1.call-done = (bf16[8,64,2048]{2,1,0:T(8,128)(2,1)}, bf16[128,2048]{1,0:T(8,128)(2,1)}) async-done(((bf16[8,64,2048]{2,1,0:T(8,128)(2,1)}, bf16[128,2048]{1,0:T(8,128)(2,1)}), (bf16[8,64,2048]{2,1,0:T(8,128)(2,1)}, bf16[128,2048]{1,0:T(8,128)(2,1)})) %all-reduce.7.cloned.1.call-update) | async-done | bytes 2621456 | tf_op jit(solution)/shard_map/psum | solution.py:104
  265.1 5.2 %all-to-all-start.2 = ((bf16[8,64,2048]{2,1,0:T(8,128)(2,1)}), bf16[8,64,2048]{2,1,0:T(8,128)(2,1)S(1)}, u32[]{:S(2)}, u32[]{:S(2)}) async-start(bf16[8,64,2048]{2,1,0:T(8,128)(2,1)} %get-tuple-element.21), calls=%async_computation.2 | async-start | bytes 4194304 | tf_op jit(solution)/shard_map/all_to_all | solution.py:105
  270.6 1.4 fusion.69
  272.1 2.0 gather_fusion.4
  274.4 21.9 %all-to-all-done.2 = bf16[8,64,2048]{2,1,0:T(8,128)(2,1)S(1)} async-done(((bf16[8,64,2048]{2,1,0:T(8,128)(2,1)}), bf16[8,64,2048]{2,1,0:T(8,128)(2,1)S(1)}, u32[]{:S(2)}, u32[]{:S(2)}) %all-to-all-start.2) | async-done | bytes 2097184 | tf_op jit(solution)/shard_map/all_to_all | solution.py:105
  296.3 2.3 gather_fusion.3
  298.6 2.4 reshape.422
  301.0 3.2 %multiply_reduce_fusion = f32[128,2048]{1,0:T(8,128)S(1)} fusion(f32[128,2,2048]{2,1,0:T(2,128)S(1)} %reshape.422, f32[128,2]{1,0:T(8,128)S(1)} %copy.52), kind=kLoop, calls=%fused_computation.17 | loop fusion | flops 786432 | bytes 3146752 | tf_op jit(solution)/shard_map/reduce_sum | solution.py:107
  304.2 1.0 fusion.27
  (76 shorter events, 3.4 us)
Async XLA Ops:
  7.2 263.4 %copy-start = (bf16[2048,128]{1,0:T(8,128)(2,1)S(1)}, bf16[2048,128]{1,0:T(8,128)(2,1)}, u32[]{:S(2)}) copy-start(bf16[2048,128]{1,0:T(8,128)(2,1)} %param.34) | copy-start | bytes 1572868
  7.2 5.8 %copy-start.3 = (bf16[128,2048]{1,0:T(8,128)(2,1)S(1)}, bf16[128,2048]{1,0:T(8,128)(2,1)}, u32[]{:S(2)}) copy-start(bf16[128,2048]{1,0:T(8,128)(2,1)} %param.19) | copy-start | bytes 1572868
  7.2 5.8 %copy-start.11 = (bf16[2048,128]{1,0:T(8,128)(2,1)S(1)}, bf16[2048,128]{1,0:T(8,128)(2,1)}, u32[]{:S(2)}) copy-start(bf16[2048,128]{1,0:T(8,128)(2,1)} %param.29) | copy-start | bytes 1572868
  7.2 91.7 %all-reduce.5.cloned.1.call-start = ((), (), s32[]{:S(2)}) async-start(), calls=%async_computation.3 | async-start | bytes 1048576 | tf_op jit(solution)/shard_map/psum | solution.py:86
  13.4 3.5 %copy-start.6 = (bf16[128,64,1,128]{3,1,2,0:T(8,128)(2,1)S(1)}, bf16[128,64,1,128]{3,1,2,0:T(8,128)(2,1)}, u32[]{:S(2)}) copy-start(bf16[128,64,1,128]{3,1,2,0:T(8,128)(2,1)} %param.23) | copy-start | bytes 6291460
  16.5 1.6 copy-start.5
  20.7 1.3 copy-start.1
  27.1 3.8 %copy-start.8 = (s32[128,2]{0,1:T(2,128)S(1)}, s32[128,2]{0,1:T(2,128)}, u32[]{:S(2)}) copy-start(s32[128,2]{0,1:T(2,128)} %param.21) | copy-start | bytes 3076
  27.1 14.9 %copy-start.9 = (bf16[2048]{0:T(1024)(128)(2,1)S(1)}, bf16[2048]{0:T(1024)(128)(2,1)}, u32[]{:S(2)}) copy-start(bf16[2048]{0:T(1024)(128)(2,1)} %param.26) | copy-start | bytes 12292
  34.5 48.7 %all-to-all-start.1 = ((s32[8,64,1]{1,2,0:T(1,128)}), s32[8,64,1]{1,2,0:T(1,128)S(1)}, u32[]{:S(2)}, u32[]{:S(2)}) async-start(s32[8,64,1]{1,2,0:T(1,128)} %bitcast.10), calls=%async_computation.1 | async-start | bytes 8192 | tf_op jit(solution)/shard_map/all_to_all | solution.py:102
  62.6 20.6 %copy-start.10 = (bf16[2048]{0:T(1024)(128)(2,1)S(1)}, bf16[2048]{0:T(1024)(128)(2,1)}, u32[]{:S(2)}) copy-start(bf16[2048]{0:T(1024)(128)(2,1)} %param.25) | copy-start | bytes 12292
  100.3 3.4 %copy-start.2 = (bf16[128,2048]{1,0:T(8,128)(2,1)}, bf16[128,2048]{1,0:T(8,128)(2,1)S(1)}, u32[]{:S(2)}) copy-start(bf16[128,2048]{1,0:T(8,128)(2,1)S(1)} %get-tuple-element.29) | copy-start | bytes 1572868
  103.7 30.8 %all-to-all-start = ((bf16[8,64,2048]{2,1,0:T(8,128)(2,1)}), bf16[8,64,2048]{2,1,0:T(8,128)(2,1)S(1)}, u32[]{:S(2)}, u32[]{:S(2)}) async-start(bf16[8,64,2048]{2,1,0:T(8,128)(2,1)} %bitcast.59), calls=%async_computation | async-start | bytes 4194304 | tf_op jit(solution)/shard_map/all_to_all | solution.py:101
  108.5 156.6 %all-reduce.7.cloned.1.call-start = ((), (), s32[]{:S(2)}) async-start(), calls=%async_computation.4 | async-start | bytes 5242880 | tf_op jit(solution)/shard_map/psum | solution.py:104
  156.4 18.7 %copy-start.4 = (f32[512,192]{1,0:T(8,128)S(1)}, f32[512,192]{1,0:T(8,128)}, u32[]{:S(2)}) copy-start(f32[512,192]{1,0:T(8,128)} %ragged-dot-none.2) | copy-start | bytes 1179652
  265.1 31.2 %all-to-all-start.2 = ((bf16[8,64,2048]{2,1,0:T(8,128)(2,1)}), bf16[8,64,2048]{2,1,0:T(8,128)(2,1)S(1)}, u32[]{:S(2)}, u32[]{:S(2)}) async-start(bf16[8,64,2048]{2,1,0:T(8,128)(2,1)} %get-tuple-element.21), calls=%async_computation.2 | async-start | bytes 4194304 | tf_op jit(solution)/shard_map/all_to_all | solution.py:105
  301.0 3.2 %copy-start.7 = (bf16[128,2048]{1,0:T(8,128)(2,1)S(1)}, bf16[128,2048]{1,0:T(8,128)(2,1)}, u32[]{:S(2)}) copy-start(bf16[128,2048]{1,0:T(8,128)(2,1)} %get-tuple-element.22) | copy-start | bytes 1572868
Sparse Core Ops, SparseCore 0:
  31.0 39.5 all-reduce.4
  201.1 63.9 all-reduce.6
where the time goes:
time: 315 us; the launch traced here: 312 us
  waiting for transfers between devices  99.7 us (32%)
  local copies, waits for them, and re-layouts  66.1 us (21%)
  Pallas kernels  57.4 us (18%)
  other arithmetic  31 us (10%)
  matrix products  27.3 us (9%)
  starting transfers between devices  16.1 us (5%)
  between operations  14.5 us (5%)
    psum x1, waiting for transfers between devices, local_layer(): expert_sum = lax.psum(expert_part, 'tp')  64.1 us
    another operation x3, Pallas kernels  55.5 us
    unnamed x28, local copies, waits for them, and re-layouts  44 us
    all_to_all x1, waiting for transfers between devices, local_layer(): returned = lax.all_to_all(expert_sum, 'ep', 0, 0, tiled=True)  21.9 us
    all_to_all x1, waiting for transfers between devices, local_layer(): recv_rows = lax.all_to_all(send_rows, 'ep', 0, 0, tiled=True)  13.6 us
    dot_general x1, matrix products, dense_block(): return jnp.dot(act_val, w_down, preferred_element_type=jnp.float32)  7.67 us
  transfers between devices with their start and end apart: 5, of which 3 were waited for; matrix products, arithmetic and copies ran while one was open for 24% of the time, Pallas kernels for 1%

commit v1 on v0

v1 whole, which is shorter than its diff:
```python
import functools

import jax
import jax.numpy as jnp
import numpy as np
from jax import lax
from jax.experimental import pallas as pl
from jax.experimental.pallas import tpu as pltpu
from jax.sharding import PartitionSpec as P

NORM_EPS = 1e-5
ROPE_BASE = 10000.0
MESH = pl.DeviceIdType.MESH
F32 = jnp.float32
BF16 = jnp.bfloat16
WIN = 32
ALIGN = 16
CHUNK = 256
VMEM_LIMIT = 60 * 1024 * 1024

ANY = pl.BlockSpec(memory_space=pl.ANY)
VMEM = pl.BlockSpec(memory_space=pltpu.VMEM)
SMEM = pl.BlockSpec(memory_space=pltpu.SMEM)


def nt_dot(a, b):
    return lax.dot_general(a, b, (((1,), (1,)), ((), ())), preferred_element_type=F32)


def mm(a, b):
    return jnp.dot(a, b, preferred_element_type=F32)


def iota(shape, dim):
    return lax.broadcasted_iota(jnp.int32, shape, dim)


class Links:
    def __init__(self, send_sems, recv_sems):
        self.send_sems, self.recv_sems, self.started = send_sems, recv_sems, {}

    def send(self, i, src, dst, device):
        copy = pltpu.make_async_remote_copy(
            src_ref=src, dst_ref=dst, send_sem=self.send_sems.at[i], recv_sem=self.recv_sems.at[i],
            device_id=device, device_id_type=MESH)
        copy.start()
        self.started[i] = copy

    def recv(self, *ids):
        for i in ids:
            self.started[i].wait_recv()

    def drain(self):
        for copy in self.started.values():
            copy.wait_send()


class RowSum:
    sends = 12

    def __init__(self, links, base, part, relay, got, full, axis):
        self.links, self.base, self.part, self.relay, self.got, self.full = links, base, part, relay, got, full
        self.size = lax.axis_size(axis)
        self.me = lax.axis_index(axis)
        self.right = lax.rem(self.me + 1, self.size)
        self.left = lax.rem(self.me + self.size - 1, self.size)
        self.far = lax.rem(self.me + 2, self.size)
        self.to_right, self.to_left = {axis: self.right}, {axis: self.left}
        self.block = part.shape[0] // self.size
        self.half = self.block // 2

    def rows(self, rank, half):
        return pl.ds(pl.multiple_of(rank * self.block + half * self.half, self.half), self.half)

    def send(self, i, src, dst, device):
        self.links.send(self.base + i, src, dst, device)

    def recv(self, *ids):
        self.links.recv(*[self.base + i for i in ids])

    def start(self):
        part = self.part
        self.send(0, part.at[self.rows(self.far, 0)], self.relay.at[0], self.to_right)
        self.send(1, part.at[self.rows(self.far, 1)], self.relay.at[1], self.to_left)
        self.send(2, part.at[self.rows(self.right, 1)], self.got.at[0, 1], self.to_right)
        self.send(3, part.at[self.rows(self.left, 0)], self.got.at[1, 0], self.to_left)

    def pass_on(self):
        part, relay = self.part, self.relay
        self.recv(0)
        relay[2] = (part[self.rows(self.right, 0), :].astype(F32) + relay[0].astype(F32)).astype(BF16)
        self.send(4, relay.at[2], self.got.at[0, 0], self.to_right)
        self.recv(1)
        relay[3] = (part[self.rows(self.left, 1), :].astype(F32) + relay[1].astype(F32)).astype(BF16)
        self.send(5, relay.at[3], self.got.at[1, 1], self.to_left)

    def finish_sum(self, own, rest):
        full = self.full
        self.recv(2, 3, 4, 5)
        for half in (0, 1):
            at = self.rows(self.me, half)
            total = own[at, :] + self.got[0, half].astype(F32) + self.got[1, half].astype(F32)
            full[at, :] = (rest[at, :].astype(F32) + total).astype(BF16)
        self.send(6, full.at[self.rows(self.me, 0)], full.at[self.rows(self.me, 0)], self.to_right)
        self.send(7, full.at[self.rows(self.me, 1)], full.at[self.rows(self.me, 1)], self.to_left)
        self.send(8, full.at[self.rows(self.me, 1)], full.at[self.rows(self.me, 1)], self.to_right)
        self.send(9, full.at[self.rows(self.me, 0)], full.at[self.rows(self.me, 0)], self.to_left)

    def forward(self):
        full = self.full
        self.recv(6)
        self.send(10, full.at[self.rows(self.left, 0)], full.at[self.rows(self.left, 0)], self.to_right)
        self.recv(7)
        self.send(11, full.at[self.rows(self.right, 1)], full.at[self.rows(self.right, 1)], self.to_left)

    def finish(self):
        self.recv(8, 9, 10, 11)


def row_sum_scratch(rows, cols, tp):
    half = rows // tp // 2
    return [pltpu.VMEM((rows, cols), BF16), pltpu.VMEM((4, half, cols), BF16),
            pltpu.VMEM((2, 2, half, cols), BF16), pltpu.VMEM((rows, cols), BF16)]


def meet(ep_peers, tp_peers):
    barrier = pltpu.get_barrier_semaphore()
    for peer in ep_peers:
        pl.semaphore_signal(barrier, inc=1, device_id={"ep": peer}, device_id_type=MESH)
    for peer in tp_peers:
        pl.semaphore_signal(barrier, inc=1, device_id={"tp": peer}, device_id_type=MESH)
    pl.semaphore_wait(barrier, len(ep_peers) + len(tp_peers))


def ring_ids():
    ep = lax.axis_size("ep")
    me = lax.axis_index("ep")
    core = lax.rem(me, 2)
    partner = me + 1 - 2 * core
    return ep, me, core, partner, lax.rem(me + 2, ep), lax.rem(me + ep - 2, ep), lax.rem(me + 4, ep)


def front_kernel(x_ref, ids_ref, pos_ref, freq_ref, gains_ref, wr_ref, kc_hbm, vc_hbm, wq_hbm, wk_hbm, wv_hbm, wo_hbm,
                 h_ref, knew_ref, vnew_ref, meta_ref, mall_hbm,
                 mall, meta, a_s, q_s, o_s, k_s, v_s, pcol, kc, vc, wq, wk, wv, wo, own, part, relay, got, full,
                 send_sems, recv_sems, load_sems, out_sems):
    tokens, dim = x_ref.shape
    head = wk.shape[1]
    heads = wq.shape[1] // head
    slots = kc.shape[1]
    ep, me, core, partner, right, left, far = ring_ids()
    tp, mt = lax.axis_size("tp"), lax.axis_index("tp")
    loads = [pltpu.make_async_copy(s, d, load_sems.at[i]) for i, (s, d) in enumerate(
        [(wq_hbm, wq), (wk_hbm, wk), (wv_hbm, wv), (kc_hbm, kc), (vc_hbm, vc), (wo_hbm, wo)])]
    for load in loads:
        load.start()
    peers = [lax.rem(me + i, ep) for i in range(1, ep)]
    barrier = pltpu.get_barrier_semaphore()
    for peer in peers:
        pl.semaphore_signal(barrier, inc=1, device_id={"ep": peer}, device_id_type=MESH)
    for peer in (lax.rem(mt + 1, tp), lax.rem(mt + tp - 1, tp)):
        pl.semaphore_signal(barrier, inc=1, device_id={"tp": peer}, device_id_type=MESH)

    wide = x_ref[...].astype(F32)
    inv = lax.rsqrt(jnp.mean(wide * wide, axis=-1, keepdims=True) + NORM_EPS)
    mall[me] = (wide * inv * gains_ref[2:3, :]).astype(BF16)
    a_s[...] = (wide * inv * gains_ref[0:1, :]).astype(BF16)

    pl.semaphore_wait(barrier, len(peers) + 2)
    links = Links(send_sems, recv_sems)
    hrow = tokens // 2

    def half(i, h):
        return mall.at[i, pl.ds(h * hrow, hrow)]

    links.send(0, half(me, 0), half(me, 0), {"ep": right})
    links.send(1, half(me, 1), half(me, 1), {"ep": left})
    links.send(2, half(me, 1), half(me, 1), {"ep": right})
    links.send(3, half(me, 0), half(me, 0), {"ep": left})
    links.send(4, mall.at[me], mall.at[me], {"ep": partner})
    outs = []

    def put(i):
        copy = pltpu.make_async_copy(mall.at[i], mall_hbm.at[i], out_sems.at[len(outs)])
        copy.start()
        outs.append(copy)

    put(me)

    m_own = mall[me]
    logits = mm(m_own, wr_ref[...])
    probs = jnp.exp(logits - jnp.max(logits, axis=-1, keepdims=True))
    probs = probs / jnp.sum(probs, axis=-1, keepdims=True)
    experts = logits.shape[1]
    ids = ids_ref[...].astype(F32)
    lane = iota((tokens, experts), 1).astype(F32)
    picked = []
    for k in (0, 1):
        id_col = jnp.transpose(jnp.broadcast_to(ids[k:k + 1, :], (experts, tokens)))
        picked.append(jnp.sum(jnp.where(id_col == lane, probs, 0.0), axis=-1, keepdims=True))
    both = picked[0] + picked[1]
    wt_rows = [jnp.transpose(jnp.broadcast_to(p / both, (tokens, 128)))[0:8, :] for p in picked]
    sub = iota((8, tokens), 0)
    block = jnp.where(sub == 0, jnp.broadcast_to(ids[0:1, :], (8, tokens)),
                      jnp.where(sub == 1, jnp.broadcast_to(ids[1:2, :], (8, tokens)),
                                jnp.where(sub == 2, wt_rows[0], wt_rows[1])))
    meta[me] = block
    for n, peer in enumerate(peers):
        links.send(20 + n, meta.at[me], meta.at[me], {"ep": peer})

    def pos_body(g, carry):
        row = iota((8, head), 0)
        acc = jnp.zeros((8, head), jnp.int32)
        for j in range(8):
            acc = jnp.where(row == j, pos_ref[g * 8 + j], acc)
        pcol[pl.ds(pl.multiple_of(g * 8, 8), 8), :] = acc
        return carry

    lax.fori_loop(0, tokens // 8, pos_body, 0)
    angles = pcol[...].astype(F32) * freq_ref[...]
    cosine = jnp.cos(angles)
    sine = jnp.where(iota((tokens, head), 1) < head // 2, -jnp.sin(angles), jnp.sin(angles))

    def rope(v):
        return v * cosine + pltpu.roll(v, head // 2, 1) * sine

    for load in loads[:3]:
        load.wait()
    normed = a_s[...]
    k_s[...] = rope(mm(normed, wk[...])).astype(BF16).astype(F32)
    v_s[...] = mm(normed, wv[...]).astype(BF16).astype(F32)
    knew_ref[...] = k_s[...].astype(BF16)
    vnew_ref[...] = v_s[...].astype(BF16)
    for i in range(heads // 2):
        q2 = mm(normed, wq[:, i * 2 * head:(i + 1) * 2 * head])
        for j in (0, 1):
            q_s[2 * i + j] = rope(q2[:, j * head:(j + 1) * head]).astype(BF16).astype(F32)

    loads[3].wait()
    loads[4].wait()

    def attend(g, carry):
        base = pl.multiple_of(g * 8, 8)
        slot = iota((slots, head), 0)
        keys, vals = [], []
        for j in range(8):
            hit = slot == pos_ref[g * 8 + j]
            keys.append(jnp.where(hit, k_s[pl.ds(base + j, 1), :], kc[base + j].astype(F32)).astype(BF16))
            vals.append(jnp.where(hit, v_s[pl.ds(base + j, 1), :], vc[base + j].astype(F32)).astype(BF16))
        keys = jnp.concatenate(keys, axis=0)
        vals = jnp.concatenate(vals, axis=0)
        q8 = q_s[:, pl.ds(base, 8), :].reshape(heads * 8, head).astype(BF16)
        scores = nt_dot(q8, keys) * (head ** -0.5)
        col = iota((8, 8 * slots), 1)
        mask = jnp.zeros((8, 8 * slots), jnp.bool_)
        row_pos = jnp.concatenate([pcol[pl.ds(base, 8), :]] * (8 * slots // head), axis=1)
        mask = (col // slots == iota((8, 8 * slots), 0)) & (lax.rem(col, slots) <= row_pos)
        mask = jnp.broadcast_to(mask[None], (heads, 8, 8 * slots)).reshape(heads * 8, 8 * slots)
        scores = jnp.where(mask, scores, -1e30)
        e = jnp.exp(scores - jnp.max(scores, axis=-1, keepdims=True))
        p = (e / jnp.sum(e, axis=-1, keepdims=True)).astype(BF16)
        o8 = mm(p, vals)
        o_s[:, pl.ds(base, 8), :] = o8.reshape(heads, 8, head)
        return carry

    lax.fori_loop(0, tokens // 8, attend, 0)
    mix = jnp.concatenate([o_s[i].astype(BF16) for i in range(heads)], axis=1)
    loads[5].wait()
    for i in range(dim // 512):
        cols = slice(i * 512, (i + 1) * 512)
        piece = mm(mix, wo[:, cols])
        own[:, cols] = piece
        part[:, cols] = piece.astype(BF16)
    tp_sum = RowSum(links, 5, part, relay, got, full, "tp")
    tp_sum.start()

    links.recv(0)
    links.send(17, half(left, 0), half(left, 0), {"ep": right})
    links.send(27, half(left, 0), half(left, 0), {"ep": partner})
    links.recv(1)
    links.send(18, half(right, 1), half(right, 1), {"ep": left})
    links.send(28, half(right, 1), half(right, 1), {"ep": partner})
    tp_sum.pass_on()
    links.recv(4)
    put(partner)
    tp_sum.finish_sum(own, x_ref)
    links.recv(2)
    links.send(29, half(left, 1), half(left, 1), {"ep": partner})
    put(left)
    links.recv(3)
    links.send(30, half(right, 0), half(right, 0), {"ep": partner})
    put(right)
    tp_sum.forward()
    tp_sum.finish()
    h_ref[...] = full[...]
    links.recv(*range(20, 20 + len(peers)))
    meta_ref[...] = meta[...]
    links.recv(17)
    links.send(31, half(far, 0), half(far, 0), {"ep": partner})
    links.recv(18)
    links.send(32, half(far, 1), half(far, 1), {"ep": partner})
    put(far)

    def twin(i):
        return i + 1 - 2 * lax.rem(i, 2)

    links.recv(27, 29)
    links.recv(28, 30)
    put(twin(left))
    put(twin(right))
    links.recv(31, 32)
    put(twin(far))
    links.drain()
    for copy in outs:
        copy.wait()


def front(x, ids_t, pos, freq, gains, w_router, kc, vc, w_q, w_k, w_v, w_o, ep, tp):
    tokens, dim = x.shape
    head = w_k.shape[1]
    heads = w_q.shape[1] // head
    slots = kc.shape[1]
    shape = jax.ShapeDtypeStruct
    return pl.pallas_call(
        front_kernel,
        name="front",
        out_shape=(shape((tokens, dim), BF16), shape((tokens, head), BF16), shape((tokens, head), BF16),
                   shape((ep, 8, tokens), F32), shape((ep, tokens, dim), BF16)),
        in_specs=[VMEM, VMEM, SMEM, VMEM, VMEM, VMEM] + [ANY] * 6,
        out_specs=(VMEM, VMEM, VMEM, VMEM, ANY),
        scratch_shapes=[
            pltpu.VMEM((ep, tokens, dim), BF16), pltpu.VMEM((ep, 8, tokens), F32), pltpu.VMEM((tokens, dim), BF16),
            pltpu.VMEM((heads, tokens, head), F32), pltpu.VMEM((heads, tokens, head), F32),
            pltpu.VMEM((tokens, head), F32), pltpu.VMEM((tokens, head), F32), pltpu.VMEM((tokens, head), jnp.int32),
            pltpu.VMEM(kc.shape, BF16), pltpu.VMEM(vc.shape, BF16), pltpu.VMEM(w_q.shape, BF16),
            pltpu.VMEM(w_k.shape, BF16), pltpu.VMEM(w_v.shape, BF16), pltpu.VMEM(w_o.shape, BF16),
            pltpu.VMEM((tokens, dim), F32), *row_sum_scratch(tokens, dim, tp),
            pltpu.SemaphoreType.DMA((33,)), pltpu.SemaphoreType.DMA((33,)),
            pltpu.SemaphoreType.DMA((6,)), pltpu.SemaphoreType.DMA((8,))],
        compiler_params=pltpu.CompilerParams(collective_id=0, has_side_effects=True, vmem_limit_bytes=VMEM_LIMIT),
    )(x, ids_t, pos, freq, gains, w_router, kc, vc, w_q, w_k, w_v, w_o)


def expert_kernel(meta_ref, mall_hbm, eg_hbm, eu_hbm, ed_hbm, out_hbm,
                  rows, sorted_in, sorted_out, pos_row, pos_col, wt_row, wt_slot, plan, plan_s, eg, eu, ed, out,
                  rows_sem, plan_sem, w_sems, out_sems):
    count = eg.shape[0]
    ep, _, tokens = meta_ref.shape
    total_rows, dim = rows.shape
    cap = out.shape[0]
    me = lax.axis_index("ep")
    rows_copy = pltpu.make_async_copy(mall_hbm, rows, rows_sem)
    rows_copy.start()

    def weights(e):
        return [pltpu.make_async_copy(src.at[e], dst.at[e], w_sems.at[i, e])
                for i, (src, dst) in enumerate([(eg_hbm, eg), (eu_hbm, eu), (ed_hbm, ed)])]

    for e in range(count):
        for copy in weights(e):
            copy.start()
    sorted_out[...] = jnp.zeros_like(sorted_out)

    first = (me * count).astype(F32)
    before = (iota((tokens, tokens), 0) < iota((tokens, tokens), 1)).astype(F32).astype(BF16)
    expert = iota((count, tokens), 0).astype(F32)
    hots, ranks, local = [], [], []
    seen = jnp.zeros((count, 1), F32)
    for s in range(ep):
        block = meta_ref[s]
        one, two = block[0:1, :] - first, block[1:2, :] - first
        in_one = (one >= 0) & (one < count)
        in_two = (two >= 0) & (two < count)
        mine = jnp.where(in_one, one, jnp.where(in_two, two, -1.0))
        wt_row[s:s + 1, :] = jnp.where(in_one, block[2:3, :], jnp.where(in_two, block[3:4, :], 0.0))
        hot = (expert == mine).astype(F32)
        hots.append(hot)
        local.append(mine)
        ranks.append(mm(hot.astype(BF16), before) + seen)
        seen = seen + jnp.sum(hot, axis=1, keepdims=True)
    padded = jnp.floor((seen + (ALIGN - 1)) * (1.0 / ALIGN)) * ALIGN
    padded = jnp.broadcast_to(padded, (count, tokens))
    earlier = (iota((count, count), 1) < iota((count, count), 0)).astype(F32).astype(BF16)
    start = mm(earlier, padded.astype(BF16))
    for s in range(ep):
        at = jnp.sum(hots[s] * (start + ranks[s]), axis=0, keepdims=True)
        at = jnp.where(local[s] >= 0, at, -1.0)
        pos_row[s:s + 1, :] = at
        pos_col[pl.ds(s * tokens, tokens), :] = jnp.transpose(jnp.broadcast_to(at, (tokens, tokens)))
    plan[0:count, :] = jnp.broadcast_to(seen, (count, tokens)).astype(jnp.int32)
    plan[count:2 * count, :] = start.astype(jnp.int32)
    plan[2 * count:3 * count, :] = (start + padded).astype(jnp.int32)
    plan_copy = pltpu.make_async_copy(plan, plan_s, plan_sem)
    plan_copy.start()
    plan_copy.wait()
    used = plan_s[3 * count - 1, 0]
    chunks = (used + (CHUNK - 1)) // CHUNK
    rows_copy.wait()

    def gather(c, carry):
        base = pl.multiple_of(c * CHUNK, CHUNK)
        slot = (iota((CHUNK, tokens), 0) + base).astype(F32)
        picks = []
        wt = jnp.zeros((CHUNK, tokens), F32)
        for s in range(ep):
            hot = slot == pos_row[s:s + 1, :]
            wt = wt + jnp.where(hot, wt_row[s:s + 1, :], 0.0)
            picks.append(hot.astype(F32).astype(BF16))
        pick = jnp.concatenate(picks, axis=1)
        wt_slot[pl.ds(base, CHUNK), :] = jnp.broadcast_to(jnp.sum(wt, axis=1, keepdims=True), (CHUNK, tokens))
        for i in range(dim // 512):
            cols = slice(i * 512, (i + 1) * 512)
            sorted_in[pl.ds(base, CHUNK), cols] = mm(pick, rows[:, cols]).astype(BF16)
        return carry

    lax.fori_loop(0, chunks, gather, 0)

    def run_expert(e, carry):
        for copy in weights(e):
            copy.wait()
        passes = (plan_s[e, 0] + (WIN - 1)) // WIN
        begin = plan_s[count + e, 0]

        def one_pass(p, inner):
            at = pl.ds(pl.multiple_of(begin + p * WIN, ALIGN), WIN)
            x = sorted_in[at, :]
            gate = nt_dot(eg[e], x)
            up = nt_dot(eu[e], x)
            act = jnp.transpose(jax.nn.silu(gate) * up).astype(BF16)
            wt = wt_slot[at, :][:, 0:1]
            for i in range(dim // 512):
                cols = slice(i * 512, (i + 1) * 512)
                sorted_out[at, cols] = (mm(act, ed[e, :, cols]) * wt).astype(BF16)
            return inner

        lax.fori_loop(0, passes, one_pass, 0)
        return carry

    lax.fori_loop(0, count, run_expert, 0)

    block = total_rows // 2
    lane = iota((block, tokens), 1).astype(F32)
    for k in range(1, cap // CHUNK + 1):
        @pl.when(jnp.maximum(chunks, 1) == k)
        def _():
            for b in range(2):
                at = pl.ds(b * block, block)
                where = pos_col[at, :]
                pick = jnp.concatenate([(where == lane + float(j * tokens)).astype(F32).astype(BF16)
                                        for j in range(k * CHUNK // tokens)], axis=1)

                def cols_body(i, carry):
                    cols = pl.ds(pl.multiple_of(i * 512, 512), 512)
                    rows[at, cols] = mm(pick, sorted_out[0:k * CHUNK, cols]).astype(BF16)
                    return carry

                lax.fori_loop(0, dim // 512, cols_body, 0)
                pltpu.make_async_copy(rows.at[at], out_hbm.at[at], out_sems.at[b]).start()
    for b in range(2):
        at = pl.ds(b * block, block)
        pltpu.make_async_copy(rows.at[at], out_hbm.at[at], out_sems.at[b]).wait()


def experts(meta, mall, eg_t, eu_t, ed):
    ep, _, tokens = meta.shape
    dim = mall.shape[1]
    count = eg_t.shape[0]
    most = ep * tokens // 2 + count * (ALIGN - 1)
    cap = (most + CHUNK - 1) // CHUNK * CHUNK
    total = ep * tokens
    return pl.pallas_call(
        expert_kernel,
        name="experts",
        out_shape=jax.ShapeDtypeStruct((total, dim), BF16),
        in_specs=[VMEM] + [ANY] * 4,
        out_specs=ANY,
        scratch_shapes=[
            pltpu.VMEM((total, dim), BF16), pltpu.VMEM((cap + WIN, dim), BF16), pltpu.VMEM((cap + WIN, dim), BF16),
            pltpu.VMEM((ep, tokens), F32), pltpu.VMEM((total, tokens), F32), pltpu.VMEM((ep, tokens), F32),
            pltpu.VMEM((cap + WIN, tokens), F32), pltpu.VMEM((3 * count, tokens), jnp.int32),
            pltpu.SMEM((3 * count, tokens), jnp.int32),
            pltpu.VMEM(eg_t.shape, BF16), pltpu.VMEM(eu_t.shape, BF16), pltpu.VMEM(ed.shape, BF16),
            pltpu.VMEM((cap, 128), BF16),
            pltpu.SemaphoreType.DMA, pltpu.SemaphoreType.DMA, pltpu.SemaphoreType.DMA((3, count)),
            pltpu.SemaphoreType.DMA((2,))],
        compiler_params=pltpu.CompilerParams(vmem_limit_bytes=VMEM_LIMIT),
    )(meta, mall, eg_t, eu_t, ed)


def back_kernel(h_ref, gains_ref, moe_hbm, wg_hbm, wu_hbm, wd_hbm, out_ref,
                keep, give, take, ring, relay_x, got_x, swap, own, c_s, wg, wu, wd, part, relay, got, full,
                send_sems, recv_sems, load_sems):
    tokens, dim = h_ref.shape
    ep, me, core, partner, right, left, far = ring_ids()
    tp, mt = lax.axis_size("tp"), lax.axis_index("tp")
    halfd = dim // 2
    quart = halfd // 2
    pair = 2 * tokens
    mine = pl.ds(pl.multiple_of(core * halfd, halfd), halfd)
    other = pl.ds(pl.multiple_of((1 - core) * halfd, halfd), halfd)
    chips = [far // 2, right // 2, left // 2, me // 2]

    def rows_of(chip):
        return pl.ds(pl.multiple_of(chip * pair, pair), pair)

    give_loads = [pltpu.make_async_copy(moe_hbm.at[rows_of(chip), other], give.at[i], load_sems.at[i])
                  for i, chip in enumerate(chips)]
    keep_loads = [pltpu.make_async_copy(moe_hbm.at[rows_of(chip), mine], keep.at[i], load_sems.at[4 + i])
                  for i, chip in enumerate(chips)]
    w_loads = [pltpu.make_async_copy(s, d, load_sems.at[8 + i])
               for i, (s, d) in enumerate([(wg_hbm, wg), (wu_hbm, wu), (wd_hbm, wd)])]
    for load in give_loads + keep_loads + w_loads:
        load.start()
    meet([partner, right, left], [lax.rem(mt + 1, tp), lax.rem(mt + tp - 1, tp)])
    links = Links(send_sems, recv_sems)
    for i in range(4):
        give_loads[i].wait()
        links.send(i, give.at[i], take.at[i], {"ep": partner})

    def add_pair(i):
        keep_loads[i].wait()
        links.recv(i)
        ring[i] = (keep[i].astype(F32) + take[i].astype(F32)).astype(BF16)

    lo, hi = pl.ds(0, quart), pl.ds(quart, quart)
    to_right, to_left = {"ep": right}, {"ep": left}
    add_pair(0)
    links.send(4, ring.at[0, :, lo], relay_x.at[0], to_right)
    links.send(5, ring.at[0, :, hi], relay_x.at[1], to_left)
    add_pair(1)
    links.send(6, ring.at[1, :, hi], got_x.at[0, 1], to_right)
    add_pair(2)
    links.send(7, ring.at[2, :, lo], got_x.at[1, 0], to_left)
    add_pair(3)

    wide = h_ref[...].astype(F32)
    inv = lax.rsqrt(jnp.mean(wide * wide, axis=-1, keepdims=True) + NORM_EPS)
    c_s[...] = (wide * inv * gains_ref[1:2, :]).astype(BF16)
    w_loads[0].wait()
    w_loads[1].wait()
    acts = []
    for i in range(wg.shape[1] // 512):
        cols = slice(i * 512, (i + 1) * 512)
        gate = mm(c_s[...], wg[:, cols])
        up = mm(c_s[...], wu[:, cols])
        acts.append((jax.nn.silu(gate) * up).astype(BF16))
    act = jnp.concatenate(acts, axis=1)
    w_loads[2].wait()
    for i in range(dim // 512):
        cols = slice(i * 512, (i + 1) * 512)
        own[:, cols] = mm(act, wd[:, cols])

    links.recv(4)
    relay_x[2] = (ring[1, :, 0:quart].astype(F32) + relay_x[0].astype(F32)).astype(BF16)
    links.send(8, relay_x.at[2], got_x.at[0, 0], to_right)
    links.recv(5)
    relay_x[3] = (ring[2, :, quart:halfd].astype(F32) + relay_x[1].astype(F32)).astype(BF16)
    links.send(9, relay_x.at[3], got_x.at[1, 1], to_left)
    links.recv(6, 7, 8, 9)
    mine_rows = pl.ds(pl.multiple_of(core * tokens, tokens), tokens)
    give_rows = pl.ds(pl.multiple_of((1 - core) * tokens, tokens), tokens)

    def arrived(at):
        pieces = []
        for q in (0, 1):
            cols = slice(q * quart, (q + 1) * quart)
            pieces.append(ring[3, at, cols].astype(F32) + got_x[0, q, at, :].astype(F32)
                          + got_x[1, q, at, :].astype(F32))
        return jnp.concatenate(pieces, axis=1)

    swap[0] = arrived(give_rows).astype(BF16)
    links.send(10, swap.at[0], swap.at[1], {"ep": partner})
    own[:, mine] += arrived(mine_rows)
    part[:, mine] = own[:, mine].astype(BF16)
    links.recv(10)
    own[:, other] += swap[1].astype(F32)
    part[:, other] = own[:, other].astype(BF16)
    tp_sum = RowSum(links, 11, part, relay, got, full, "tp")
    tp_sum.start()
    tp_sum.pass_on()
    tp_sum.finish_sum(own, h_ref)
    tp_sum.forward()
    tp_sum.finish()
    out_ref[...] = full[...]
    links.drain()


def back(h, gains, moe, w_gate, w_up, w_down, tp):
    tokens, dim = h.shape
    pair, halfd, quart = 2 * tokens, dim // 2, dim // 4
    chips = moe.shape[0] // pair
    return pl.pallas_call(
        back_kernel,
        name="back",
        out_shape=jax.ShapeDtypeStruct((tokens, dim), BF16),
        in_specs=[VMEM, VMEM] + [ANY] * 4,
        out_specs=VMEM,
        scratch_shapes=[
            pltpu.VMEM((chips, pair, halfd), BF16), pltpu.VMEM((chips, pair, halfd), BF16),
            pltpu.VMEM((chips, pair, halfd), BF16), pltpu.VMEM((chips, pair, halfd), BF16),
            pltpu.VMEM((4, pair, quart), BF16), pltpu.VMEM((2, 2, pair, quart), BF16),
            pltpu.VMEM((2, tokens, halfd), BF16), pltpu.VMEM((tokens, dim), F32), pltpu.VMEM((tokens, dim), BF16),
            pltpu.VMEM(w_gate.shape, BF16), pltpu.VMEM(w_up.shape, BF16), pltpu.VMEM(w_down.shape, BF16),
            *row_sum_scratch(tokens, dim, tp),
            pltpu.SemaphoreType.DMA((23,)), pltpu.SemaphoreType.DMA((23,)), pltpu.SemaphoreType.DMA((11,))],
        compiler_params=pltpu.CompilerParams(collective_id=1, has_side_effects=True, vmem_limit_bytes=VMEM_LIMIT),
    )(h, gains, moe, w_gate, w_up, w_down)


def solution(mesh):
    ep, tp = mesh.shape['ep'], mesh.shape['tp']
    row_spec = P(('dp', 'ep'), None)
    cache_spec = P(('dp', 'ep'), None, 'tp', None)
    col_split = P(None, 'tp')
    row_split = P('tp', None)
    in_specs = (row_spec, P(('dp', 'ep')), row_spec, cache_spec, cache_spec, P(None), P(None), P(None), col_split, col_split, col_split, row_split, col_split, col_split, row_split, P(None, None), P('ep', None, 'tp'), P('ep', None, 'tp'), P('ep', 'tp', None))
    out_specs = (row_spec, cache_spec, cache_spec)

    def local_layer(hidden_in, positions, expert_ids, k_cache, v_cache, norm_in, norm_res, norm_post, w_q, w_k, w_v, w_o, w_gate, w_up, w_down, w_router, e_gate, e_up, e_down):
        tokens, dim = hidden_in.shape
        slots, head = k_cache.shape[1], k_cache.shape[3]
        freq = (1.0 / (ROPE_BASE ** (jnp.arange(0, head, 2, dtype=F32) / head)))[None, :]
        freq = jnp.concatenate([freq, freq], axis=1)
        gains = jnp.stack([norm_in, norm_res, norm_post]).astype(F32)
        h, k_new, v_new, meta, mall = front(
            hidden_in, expert_ids.T, positions, freq, gains, w_router,
            k_cache.reshape(tokens, slots, head), v_cache.reshape(tokens, slots, head), w_q, w_k, w_v, w_o, ep, tp)
        moe = experts(meta, mall.reshape(ep * tokens, dim), jnp.swapaxes(e_gate, 1, 2), jnp.swapaxes(e_up, 1, 2), e_down)
        slot_hit = (jnp.arange(slots)[None, :] == positions[:, None])[:, :, None, None]
        k_out = jnp.where(slot_hit, k_new[:, None, None, :], k_cache)
        v_out = jnp.where(slot_hit, v_new[:, None, None, :], v_cache)
        return back(h, gains, moe, w_gate, w_up, w_down, tp), k_out, v_out

    return jax.shard_map(local_layer, mesh=mesh, in_specs=in_specs, out_specs=out_specs, check_vma=False)
```

time: 315 us -> 128 us (0.41)
  waiting for transfers between devices: 99.7 us -> 0 us
  local copies, waits for them, and re-layouts: 66.1 us -> 2.9 us
  Pallas kernels: 57.4 us -> 116 us
  matrix products: 27.3 us -> 0 us
  other arithmetic: 31 us -> 6.13 us
  starting transfers between devices: 16.1 us -> 0 us
  between operations: 14.5 us -> 0.74 us
    pallas_call x0 -> x3, Pallas kernels: none -> 116 us  [the longest x1 45.9 us: back(): pl.pallas_call(back_kernel, name='back', out_shape=jax.ShapeDtypeStruct((...]
    psum x2 -> x0, waiting for transfers between devices: 64.1 us -> none  [the longest x1 64.1 us: local_layer(): expert_sum = lax.psum(expert_part, 'tp')]
    another operation x3 -> x0, Pallas kernels: 55.5 us -> none
    unnamed x28 -> x11, local copies, waits for them, and re-layouts: 44 us -> 0.82 us
    all_to_all x3 -> x0, waiting for transfers between devices: 35.5 us -> none  [the longest x1 21.9 us: local_layer(): returned = lax.all_to_all(expert_sum, 'ep', 0, 0, tiled=True)]
    dot_general x9 -> x0, matrix products: 27.3 us -> none  [the longest x1 7.67 us: dense_block(): return jnp.dot(act_val, w_down, preferred_element_type=jnp.float32)]
    all_to_all x3 -> x0, starting transfers between devices: 16 us -> none  [the longest x1 6.02 us: local_layer(): recv_expert = lax.all_to_all(send_expert, 'ep', 0, 0, tiled=True)]
    gather x9 -> x0, local copies, waits for them, and re-layouts: 14.7 us -> none  [the longest x1 3.32 us: local_layer(): send_rows = padded_rows[send_token]]
  transfers between devices with their start and end apart: 5 -> 0, of which waited for: 3 -> 0; matrix products, arithmetic and copies ran while one was open for 24% -> 0% of each run, Pallas kernels for 1% -> 0%
where the time goes in v1:
time: 128 us; the launch traced here: 126 us
  Pallas kernels  116 us (91%)
  other arithmetic  6.13 us (5%)
  local copies, waits for them, and re-layouts  2.9 us (2%)
    pallas_call x1, Pallas kernels, back(): pl.pallas_call(back_kernel, name='back', out_shape=jax.ShapeDtypeStruct((...  45.9 us
    pallas_call x1, Pallas kernels, front(): pl.pallas_call(front_kernel, name='front', out_shape=(shape((tokens, dim)...  37.6 us
    pallas_call x1, Pallas kernels, experts(): pl.pallas_call(expert_kernel, name='experts', out_shape=jax.ShapeDtypeStr...  32.8 us
    select_n x1, other arithmetic, local_layer(): v_out = jnp.where(slot_hit, v_new[:, None, None, :], v_cache)  4.8 us

profile of v1, /device:TPU:97, one launch (start us, length us, event | category | flops | bytes accessed | tf_op | source)
XLA Modules:
  0.0 126.1 jit_solution(15700366649288428114)
XLA Ops:
  0.6 0.7 stack.12
  1.3 0.7 stack.13
  2.0 0.7 stack.14
  2.7 0.6 maximum_convert_fusion.gains_ref
  3.4 0.6 pad_maximum_fusion.freq_ref
  4.0 37.6 %front.1 = (bf16[128,2048]{1,0:T(8,128)(2,1)}, bf16[128,128]{1,0:T(8,128)(2,1)}, bf16[128,128]{1,0:T(8,128)(2,1)}, f32[8,8,128]{2,1,0:T(8,128)}, bf16[8,128,2048]{2,1,0:T(8,128)(2,1)}) custom-call(bf16[128,2048]{1,0:T(8,128)(2,1)} %x_ref.1, s32[2,128]{1,0:T(2,128)} %bitcast.11, s32[128]{0:T(128)} %pos_ref.1, f32[1,128]{1,0:T(1,128)} %pad_maximum_fusion.freq_ref, ...), custom_call_target="tpu_custom_call" | custom-call | tf_op jit(solution)/shard_map/front/pallas_call | solution.py:324
  41.6 32.8 %experts.1.moe_hbm = bf16[1024,2048]{1,0:T(8,128)(2,1)} custom-call(f32[8,8,128]{2,1,0:T(8,128)} %get-tuple-element.9.meta_ref, bf16[1024,2048]{1,0:T(8,128)(2,1)} %bitcast.10, bf16[16,192,2048]{2,1,0:T(8,128)(2,1)} %bitcast.6, bf16[16,192,2048]{2,1,0:T(8,128)(2,1)} %bitcast.7, bf16[16,192,2048]{2,1,0:T(8,128)(2,1)} %ed_hbm.1), custom_call_target="tpu_custom_call" | custom-call | tf_op jit(solution)/shard_map/experts/pallas_call | solution.py:471
  74.4 0.0 copy-start.4
  74.4 0.0 copy-start
  74.4 0.0 copy-start.2
  74.5 0.0 copy-start.3
  74.5 45.9 %back.1 = bf16[128,2048]{1,0:T(8,128)(2,1)} custom-call(bf16[128,2048]{1,0:T(8,128)(2,1)} %get-tuple-element.8.h_ref, f32[3,2048]{1,0:T(4,128)} %maximum_convert_fusion.gains_ref, bf16[1024,2048]{1,0:T(8,128)(2,1)} %experts.1.moe_hbm, bf16[2048,1536]{1,0:T(8,128)(2,1)} %wg_hbm.1, bf16[2048,1536]{1,0:T(8,128)(2,1)} %wu_hbm.1, bf16[1536,2048]{1,0:T(8,128)(2,1)} %wd_hbm.1), custom_call_target="tpu_custom_call" | custom-call | tf_op jit(solution)/shard_map/back/pallas_call | solution.py:592
  120.3 0.0 copy-done.4
  120.3 0.1 iota_compare_fusion
  120.4 0.0 copy-done
  120.4 0.0 copy-done.2
  120.5 0.0 copy-done.3
  120.5 0.0 copy-start.1
  120.5 4.8 %broadcast_select_fusion = (bf16[128,64,1,128]{3,1,2,0:T(8,128)(2,1)}, bf16[128,64,1,128]{3,1,2,0:T(8,128)(2,1)}) fusion(bf16[128,64,1,128]{3,1,2,0:T(8,128)(2,1)} %param.23, pred[128,64]{1,0:T(8,128)(4,1)S(1)} %iota_compare_fusion, bf16[128,128]{1,0:T(8,128)(2,1)S(1)} %copy-done.3, bf16[128,64,1,128]{3,1,2,0:T(8,128)(2,1)S(1)} %copy-done, ...), kind=kLoop, calls=%fused_computation | loop fusion | flops 2097152 | bytes 8462336 | tf_op jit(solution)/shard_map/jit(_where)/select_n | solution.py:631
  125.3 0.0 copy-done.1
  125.3 0.8 copy.23
  (1 shorter events, 0.0 us)
Async XLA Ops:
  74.4 45.9 %copy-start.4 = (s32[128]{0:T(128)S(1)}, s32[128]{0:T(128)}, u32[]{:S(2)}) copy-start(s32[128]{0:T(128)} %pos_ref.1) | copy-start | bytes 1540
  74.4 46.0 %copy-start = (bf16[128,64,1,128]{3,1,2,0:T(8,128)(2,1)S(1)}, bf16[128,64,1,128]{3,1,2,0:T(8,128)(2,1)}, u32[]{:S(2)}) copy-start(bf16[128,64,1,128]{3,1,2,0:T(8,128)(2,1)} %param.22) | copy-start | bytes 6291460
  74.4 46.0 %copy-start.2 = (bf16[128,128]{1,0:T(8,128)(2,1)S(1)}, bf16[128,128]{1,0:T(8,128)(2,1)}, u32[]{:S(2)}) copy-start(bf16[128,128]{1,0:T(8,128)(2,1)} %get-tuple-element.11) | copy-start | bytes 98308
  74.5 46.0 %copy-start.3 = (bf16[128,128]{1,0:T(8,128)(2,1)S(1)}, bf16[128,128]{1,0:T(8,128)(2,1)}, u32[]{:S(2)}) copy-start(bf16[128,128]{1,0:T(8,128)(2,1)} %get-tuple-element.12) | copy-start | bytes 98308
  120.5 4.8 %copy-start.1 = (bf16[128,2048]{1,0:T(8,128)(2,1)S(1)}, bf16[128,2048]{1,0:T(8,128)(2,1)}, u32[]{:S(2)}) copy-start(bf16[128,2048]{1,0:T(8,128)(2,1)} %back.1) | copy-start | bytes 1572868

commit v2 on v1

--- a/solution.py
+++ b/solution.py
@@ -15,6 +15,8 @@
 BF16 = jnp.bfloat16
 WIN = 32
 ALIGN = 16
+AHEAD = 6
+COLS = 512
 CHUNK = 256
 VMEM_LIMIT = 60 * 1024 * 1024
 
@@ -31,8 +33,28 @@
     return jnp.dot(a, b, preferred_element_type=F32)
 
 
+def span(i, width):
+    return slice(i * width, (i + 1) * width)
+
+
+def total(v, axis):
+    return jnp.sum(v, axis=axis, keepdims=True)
+
+
+def exp_rows(v):
+    return jnp.exp(v - jnp.max(v, axis=-1, keepdims=True))
+
+
+def rms(wide):
+    return lax.rsqrt(jnp.mean(wide * wide, axis=-1, keepdims=True) + NORM_EPS)
+
+
 def iota(shape, dim):
     return lax.broadcasted_iota(jnp.int32, shape, dim)
+
+
+def gain_row(ref):
+    return ref[...].astype(F32).reshape(1, ref.shape[0])
 
 
 class Links:
@@ -56,9 +78,7 @@
 
 
 class RowSum:
-    sends = 12
-
-    def __init__(self, links, base, part, relay, got, full, axis):
+    def __init__(self, links, base, axis, full, part=None, relay=None, got=None):
         self.links, self.base, self.part, self.relay, self.got, self.full = links, base, part, relay, got, full
         self.size = lax.axis_size(axis)
         self.me = lax.axis_index(axis)
@@ -66,10 +86,12 @@
         self.left = lax.rem(self.me + self.size - 1, self.size)
         self.far = lax.rem(self.me + 2, self.size)
         self.to_right, self.to_left = {axis: self.right}, {axis: self.left}
-        self.block = part.shape[0] // self.size
+        self.block = full.shape[0] // self.size
         self.half = self.block // 2
 
     def rows(self, rank, half):
+        if half is None:
+            return pl.ds(pl.multiple_of(rank * self.block, self.block), self.block)
         return pl.ds(pl.multiple_of(rank * self.block + half * self.half, self.half), self.half)
 
     def send(self, i, src, dst, device):
@@ -94,13 +116,16 @@
         relay[3] = (part[self.rows(self.left, 1), :].astype(F32) + relay[1].astype(F32)).astype(BF16)
         self.send(5, relay.at[3], self.got.at[1, 1], self.to_left)
 
-    def finish_sum(self, own, rest):
+    def collect(self, own, rest):
         full = self.full
         self.recv(2, 3, 4, 5)
         for half in (0, 1):
             at = self.rows(self.me, half)
-            total = own[at, :] + self.got[0, half].astype(F32) + self.got[1, half].astype(F32)
-            full[at, :] = (rest[at, :].astype(F32) + total).astype(BF16)
+            acc = own[at, :] + self.got[0, half].astype(F32) + self.got[1, half].astype(F32)
+            full[at, :] = (rest[at, :].astype(F32) + acc).astype(BF16)
+
+    def spread(self):
+        full = self.full
         self.send(6, full.at[self.rows(self.me, 0)], full.at[self.rows(self.me, 0)], self.to_right)
         self.send(7, full.at[self.rows(self.me, 1)], full.at[self.rows(self.me, 1)], self.to_left)
         self.send(8, full.at[self.rows(self.me, 1)], full.at[self.rows(self.me, 1)], self.to_right)
@@ -140,8 +165,8 @@
     return ep, me, core, partner, lax.rem(me + 2, ep), lax.rem(me + ep - 2, ep), lax.rem(me + 4, ep)
 
 
-def front_kernel(x_ref, ids_ref, pos_ref, freq_ref, gains_ref, wr_ref, kc_hbm, vc_hbm, wq_hbm, wk_hbm, wv_hbm, wo_hbm,
-                 h_ref, knew_ref, vnew_ref, meta_ref, mall_hbm,
+def front_kernel(x_ref, ids_ref, pos_ref, gin_ref, gpost_ref, wr_ref, kc_hbm, vc_hbm, wq_hbm, wk_hbm, wv_hbm, wo_hbm,
+                 hsum_ref, knew_ref, vnew_ref, meta_ref, mall_hbm,
                  mall, meta, a_s, q_s, o_s, k_s, v_s, pcol, kc, vc, wq, wk, wv, wo, own, part, relay, got, full,
                  send_sems, recv_sems, load_sems, out_sems):
     tokens, dim = x_ref.shape
@@ -162,9 +187,9 @@
         pl.semaphore_signal(barrier, inc=1, device_id={"tp": peer}, device_id_type=MESH)
 
     wide = x_ref[...].astype(F32)
-    inv = lax.rsqrt(jnp.mean(wide * wide, axis=-1, keepdims=True) + NORM_EPS)
-    mall[me] = (wide * inv * gains_ref[2:3, :]).astype(BF16)
-    a_s[...] = (wide * inv * gains_ref[0:1, :]).astype(BF16)
+    inv = rms(wide)
+    mall[me] = (wide * inv * gain_row(gpost_ref)).astype(BF16)
+    a_s[...] = (wide * inv * gain_row(gin_ref)).astype(BF16)
 
     pl.semaphore_wait(barrier, len(peers) + 2)
     links = Links(send_sems, recv_sems)
@@ -189,15 +214,15 @@
 
     m_own = mall[me]
     logits = mm(m_own, wr_ref[...])
-    probs = jnp.exp(logits - jnp.max(logits, axis=-1, keepdims=True))
-    probs = probs / jnp.sum(probs, axis=-1, keepdims=True)
+    probs = exp_rows(logits)
+    probs = probs / total(probs, 1)
     experts = logits.shape[1]
     ids = ids_ref[...].astype(F32)
     lane = iota((tokens, experts), 1).astype(F32)
     picked = []
     for k in (0, 1):
         id_col = jnp.transpose(jnp.broadcast_to(ids[k:k + 1, :], (experts, tokens)))
-        picked.append(jnp.sum(jnp.where(id_col == lane, probs, 0.0), axis=-1, keepdims=True))
+        picked.append(total(jnp.where(id_col == lane, probs, 0.0), 1))
     both = picked[0] + picked[1]
     wt_rows = [jnp.transpose(jnp.broadcast_to(p / both, (tokens, 128)))[0:8, :] for p in picked]
     sub = iota((8, tokens), 0)
@@ -217,9 +242,12 @@
         return carry
 
     lax.fori_loop(0, tokens // 8, pos_body, 0)
-    angles = pcol[...].astype(F32) * freq_ref[...]
+    spot = iota((tokens, head), 1)
+    power = lax.rem(spot, head // 2).astype(F32) * (-np.log(ROPE_BASE) / (head // 2))
+    angles = pcol[...].astype(F32) * jnp.exp(power)
     cosine = jnp.cos(angles)
-    sine = jnp.where(iota((tokens, head), 1) < head // 2, -jnp.sin(angles), jnp.sin(angles))
+    sine = jnp.sin(angles)
+    sine = jnp.where(spot < head // 2, -sine, sine)
 
     def rope(v):
         return v * cosine + pltpu.roll(v, head // 2, 1) * sine
@@ -232,9 +260,9 @@
     knew_ref[...] = k_s[...].astype(BF16)
     vnew_ref[...] = v_s[...].astype(BF16)
     for i in range(heads // 2):
-        q2 = mm(normed, wq[:, i * 2 * head:(i + 1) * 2 * head])
+        q2 = mm(normed, wq[:, span(i, 2 * head)])
         for j in (0, 1):
-            q_s[2 * i + j] = rope(q2[:, j * head:(j + 1) * head]).astype(BF16).astype(F32)
+            q_s[2 * i + j] = rope(q2[:, span(j, head)]).astype(BF16).astype(F32)
 
     loads[3].wait()
     loads[4].wait()
@@ -252,13 +280,12 @@
         q8 = q_s[:, pl.ds(base, 8), :].reshape(heads * 8, head).astype(BF16)
         scores = nt_dot(q8, keys) * (head ** -0.5)
         col = iota((8, 8 * slots), 1)
-        mask = jnp.zeros((8, 8 * slots), jnp.bool_)
         row_pos = jnp.concatenate([pcol[pl.ds(base, 8), :]] * (8 * slots // head), axis=1)
         mask = (col // slots == iota((8, 8 * slots), 0)) & (lax.rem(col, slots) <= row_pos)
         mask = jnp.broadcast_to(mask[None], (heads, 8, 8 * slots)).reshape(heads * 8, 8 * slots)
         scores = jnp.where(mask, scores, -1e30)
-        e = jnp.exp(scores - jnp.max(scores, axis=-1, keepdims=True))
-        p = (e / jnp.sum(e, axis=-1, keepdims=True)).astype(BF16)
+        e = exp_rows(scores)
+        p = (e / total(e, 1)).astype(BF16)
         o8 = mm(p, vals)
         o_s[:, pl.ds(base, 8), :] = o8.reshape(heads, 8, head)
         return carry
@@ -266,48 +293,41 @@
     lax.fori_loop(0, tokens // 8, attend, 0)
     mix = jnp.concatenate([o_s[i].astype(BF16) for i in range(heads)], axis=1)
     loads[5].wait()
-    for i in range(dim // 512):
-        cols = slice(i * 512, (i + 1) * 512)
+    for i in range(dim // COLS):
+        cols = span(i, COLS)
         piece = mm(mix, wo[:, cols])
         own[:, cols] = piece
         part[:, cols] = piece.astype(BF16)
-    tp_sum = RowSum(links, 5, part, relay, got, full, "tp")
+    tp_sum = RowSum(links, 5, "tp", full, part, relay, got)
     tp_sum.start()
 
-    links.recv(0)
-    links.send(17, half(left, 0), half(left, 0), {"ep": right})
-    links.send(27, half(left, 0), half(left, 0), {"ep": partner})
-    links.recv(1)
-    links.send(18, half(right, 1), half(right, 1), {"ep": left})
-    links.send(28, half(right, 1), half(right, 1), {"ep": partner})
+    def twin(i):
+        return i + 1 - 2 * lax.rem(i, 2)
+
+    moves = [(0, 17, left, 0, right), (1, 18, right, 1, left)]
+    for n, (came, to, block, h, device) in enumerate(moves):
+        links.recv(came)
+        links.send(to, half(block, h), half(block, h), {"ep": device})
+        links.send(27 + n, half(block, h), half(block, h), {"ep": partner})
     tp_sum.pass_on()
     links.recv(4)
     put(partner)
-    tp_sum.finish_sum(own, x_ref)
-    links.recv(2)
-    links.send(29, half(left, 1), half(left, 1), {"ep": partner})
-    put(left)
-    links.recv(3)
-    links.send(30, half(right, 0), half(right, 0), {"ep": partner})
-    put(right)
-    tp_sum.forward()
-    tp_sum.finish()
-    h_ref[...] = full[...]
+    tp_sum.collect(own, x_ref)
+    hsum_ref[...] = full[tp_sum.rows(tp_sum.me, None), :]
+    for n, (came, block, h) in enumerate([(2, left, 1), (3, right, 0)]):
+        links.recv(came)
+        links.send(29 + n, half(block, h), half(block, h), {"ep": partner})
+        put(block)
     links.recv(*range(20, 20 + len(peers)))
     meta_ref[...] = meta[...]
-    links.recv(17)
-    links.send(31, half(far, 0), half(far, 0), {"ep": partner})
-    links.recv(18)
-    links.send(32, half(far, 1), half(far, 1), {"ep": partner})
+    links.recv(27, 29)
+    put(twin(left))
+    links.recv(28, 30)
+    put(twin(right))
+    for n, came in enumerate([17, 18]):
+        links.recv(came)
+        links.send(31 + n, half(far, n), half(far, n), {"ep": partner})
     put(far)
-
-    def twin(i):
-        return i + 1 - 2 * lax.rem(i, 2)
-
-    links.recv(27, 29)
-    links.recv(28, 30)
-    put(twin(left))
-    put(twin(right))
     links.recv(31, 32)
     put(twin(far))
     links.drain()
@@ -315,7 +335,7 @@
         copy.wait()
 
 
-def front(x, ids_t, pos, freq, gains, w_router, kc, vc, w_q, w_k, w_v, w_o, ep, tp):
+def front(x, ids_t, pos, g_in, g_post, w_router, kc, vc, w_q, w_k, w_v, w_o, ep, tp):
     tokens, dim = x.shape
     head = w_k.shape[1]
     heads = w_q.shape[1] // head
@@ -324,7 +344,7 @@
     return pl.pallas_call(
         front_kernel,
         name="front",
-        out_shape=(shape((tokens, dim), BF16), shape((tokens, head), BF16), shape((tokens, head), BF16),
+        out_shape=(shape((tokens // tp, dim), BF16), shape((tokens, head), BF16), shape((tokens, head), BF16),
                    shape((ep, 8, tokens), F32), shape((ep, tokens, dim), BF16)),
         in_specs=[VMEM, VMEM, SMEM, VMEM, VMEM, VMEM] + [ANY] * 6,
         out_specs=(VMEM, VMEM, VMEM, VMEM, ANY),
@@ -338,12 +358,13 @@
             pltpu.SemaphoreType.DMA((33,)), pltpu.SemaphoreType.DMA((33,)),
             pltpu.SemaphoreType.DMA((6,)), pltpu.SemaphoreType.DMA((8,))],
         compiler_params=pltpu.CompilerParams(collective_id=0, has_side_effects=True, vmem_limit_bytes=VMEM_LIMIT),
-    )(x, ids_t, pos, freq, gains, w_router, kc, vc, w_q, w_k, w_v, w_o)
-
-
-def expert_kernel(meta_ref, mall_hbm, eg_hbm, eu_hbm, ed_hbm, out_hbm,
-                  rows, sorted_in, sorted_out, pos_row, pos_col, wt_row, wt_slot, plan, plan_s, eg, eu, ed, out,
-                  rows_sem, plan_sem, w_sems, out_sems):
+    )(x, ids_t, pos, g_in, g_post, w_router, kc, vc, w_q, w_k, w_v, w_o)
+
+
+def expert_kernel(meta_ref, pos_ref, knew_ref, vnew_ref, kc_hbm, vc_hbm, mall_hbm, eg_hbm, eu_hbm, ed_hbm,
+                  out_hbm, ko_hbm, vo_hbm,
+                  kc, vc, k_s, v_s, rows, sorted_in, sorted_out, pos_row, pos_col, wt_row, wt_slot, plan, plan_s, eg, eu, ed, out,
+                  rows_sem, plan_sem, cache_sems, w_sems, out_sems):
     count = eg.shape[0]
     ep, _, tokens = meta_ref.shape
     total_rows, dim = rows.shape
@@ -356,9 +377,6 @@
         return [pltpu.make_async_copy(src.at[e], dst.at[e], w_sems.at[i, e])
                 for i, (src, dst) in enumerate([(eg_hbm, eg), (eu_hbm, eu), (ed_hbm, ed)])]
 
-    for e in range(count):
-        for copy in weights(e):
-            copy.start()
     sorted_out[...] = jnp.zeros_like(sorted_out)
 
     first = (me * count).astype(F32)
@@ -377,13 +395,13 @@
         hots.append(hot)
         local.append(mine)
         ranks.append(mm(hot.astype(BF16), before) + seen)
-        seen = seen + jnp.sum(hot, axis=1, keepdims=True)
+        seen = seen + total(hot, 1)
     padded = jnp.floor((seen + (ALIGN - 1)) * (1.0 / ALIGN)) * ALIGN
     padded = jnp.broadcast_to(padded, (count, tokens))
     earlier = (iota((count, count), 1) < iota((count, count), 0)).astype(F32).astype(BF16)
     start = mm(earlier, padded.astype(BF16))
     for s in range(ep):
-        at = jnp.sum(hots[s] * (start + ranks[s]), axis=0, keepdims=True)
+        at = total(hots[s] * (start + ranks[s]), 0)
         at = jnp.where(local[s] >= 0, at, -1.0)
         pos_row[s:s + 1, :] = at
         pos_col[pl.ds(s * tokens, tokens), :] = jnp.transpose(jnp.broadcast_to(at, (tokens, tokens)))
@@ -396,6 +414,14 @@
     used = plan_s[3 * count - 1, 0]
     chunks = (used + (CHUNK - 1)) // CHUNK
     rows_copy.wait()
+    for e in range(AHEAD):
+        for copy in weights(e):
+            copy.start()
+    caches = [(kc_hbm, kc, ko_hbm), (vc_hbm, vc, vo_hbm)]
+    cache_in = [pltpu.make_async_copy(src, buf, cache_sems.at[0, i]) for i, (src, buf, _) in enumerate(caches)]
+    cache_out = [pltpu.make_async_copy(buf, dst, cache_sems.at[1, i]) for i, (_, buf, dst) in enumerate(caches)]
+    for copy in cache_in:
+        copy.start()
 
     def gather(c, carry):
         base = pl.multiple_of(c * CHUNK, CHUNK)
@@ -407,15 +433,20 @@
             wt = wt + jnp.where(hot, wt_row[s:s + 1, :], 0.0)
             picks.append(hot.astype(F32).astype(BF16))
         pick = jnp.concatenate(picks, axis=1)
-        wt_slot[pl.ds(base, CHUNK), :] = jnp.broadcast_to(jnp.sum(wt, axis=1, keepdims=True), (CHUNK, tokens))
-        for i in range(dim // 512):
-            cols = slice(i * 512, (i + 1) * 512)
+        wt_slot[pl.ds(base, CHUNK), :] = jnp.broadcast_to(total(wt, 1), (CHUNK, tokens))
+        for i in range(dim // COLS):
+            cols = span(i, COLS)
             sorted_in[pl.ds(base, CHUNK), cols] = mm(pick, rows[:, cols]).astype(BF16)
         return carry
 
     lax.fori_loop(0, chunks, gather, 0)
 
     def run_expert(e, carry):
+        @pl.when(e + AHEAD < count)
+        def _():
+            for copy in weights(e + AHEAD):
+                copy.start()
+
         for copy in weights(e):
             copy.wait()
         passes = (plan_s[e, 0] + (WIN - 1)) // WIN
@@ -428,8 +459,8 @@
             up = nt_dot(eu[e], x)
             act = jnp.transpose(jax.nn.silu(gate) * up).astype(BF16)
             wt = wt_slot[at, :][:, 0:1]
-            for i in range(dim // 512):
-                cols = slice(i * 512, (i + 1) * 512)
+            for i in range(dim // COLS):
+                cols = span(i, COLS)
                 sorted_out[at, cols] = (mm(act, ed[e, :, cols]) * wt).astype(BF16)
             return inner
 
@@ -437,6 +468,27 @@
         return carry
 
     lax.fori_loop(0, count, run_expert, 0)
+
+    k_s[...] = knew_ref[...].astype(F32)
+    v_s[...] = vnew_ref[...].astype(F32)
+    for copy in cache_in:
+        copy.wait()
+    head = kc.shape[2]
+
+    def new_rows(g, carry):
+        for j in range(8):
+            b = g * 8 + j
+            spot = pos_ref[b]
+            base = pl.multiple_of(spot // ALIGN * ALIGN, ALIGN)
+            hit = iota((ALIGN, head), 0) == spot - base
+            for buf, new in ((kc, k_s), (vc, v_s)):
+                tile = buf[b, pl.ds(base, ALIGN), :].astype(F32)
+                buf[b, pl.ds(base, ALIGN), :] = jnp.where(hit, new[pl.ds(b, 1), :], tile).astype(BF16)
+        return carry
+
+    lax.fori_loop(0, tokens // 8, new_rows, 0)
+    for copy in cache_out:
+        copy.start()
 
     block = total_rows // 2
     lane = iota((block, tokens), 1).astype(F32)
@@ -450,7 +502,7 @@
                                         for j in range(k * CHUNK // tokens)], axis=1)
 
                 def cols_body(i, carry):
-                    cols = pl.ds(pl.multiple_of(i * 512, 512), 512)
+                    cols = pl.ds(pl.multiple_of(i * COLS, COLS), COLS)
                     rows[at, cols] = mm(pick, sorted_out[0:k * CHUNK, cols]).astype(BF16)
                     return carry
 
@@ -459,38 +511,44 @@
     for b in range(2):
         at = pl.ds(b * block, block)
         pltpu.make_async_copy(rows.at[at], out_hbm.at[at], out_sems.at[b]).wait()
-
-
-def experts(meta, mall, eg_t, eu_t, ed):
+    for copy in cache_out:
+        copy.wait()
+
+
+def experts(meta, pos, k_new, v_new, kc, vc, mall, eg_t, eu_t, ed):
     ep, _, tokens = meta.shape
     dim = mall.shape[1]
     count = eg_t.shape[0]
     most = ep * tokens // 2 + count * (ALIGN - 1)
     cap = (most + CHUNK - 1) // CHUNK * CHUNK
-    total = ep * tokens
+    every = ep * tokens
     return pl.pallas_call(
         expert_kernel,
         name="experts",
-        out_shape=jax.ShapeDtypeStruct((total, dim), BF16),
-        in_specs=[VMEM] + [ANY] * 4,
-        out_specs=ANY,
+        out_shape=(jax.ShapeDtypeStruct((every, dim), BF16), jax.ShapeDtypeStruct(kc.shape, BF16),
+                   jax.ShapeDtypeStruct(vc.shape, BF16)),
+        in_specs=[VMEM, SMEM, VMEM, VMEM] + [ANY] * 6,
+        out_specs=(ANY, ANY, ANY),
         scratch_shapes=[
-            pltpu.VMEM((total, dim), BF16), pltpu.VMEM((cap + WIN, dim), BF16), pltpu.VMEM((cap + WIN, dim), BF16),
-            pltpu.VMEM((ep, tokens), F32), pltpu.VMEM((total, tokens), F32), pltpu.VMEM((ep, tokens), F32),
+            pltpu.VMEM(kc.shape, BF16), pltpu.VMEM(vc.shape, BF16),
+            pltpu.VMEM(k_new.shape, F32), pltpu.VMEM(v_new.shape, F32),
+            pltpu.VMEM((every, dim), BF16), pltpu.VMEM((cap + WIN, dim), BF16), pltpu.VMEM((cap + WIN, dim), BF16),
+            pltpu.VMEM((ep, tokens), F32), pltpu.VMEM((every, tokens), F32), pltpu.VMEM((ep, tokens), F32),
             pltpu.VMEM((cap + WIN, tokens), F32), pltpu.VMEM((3 * count, tokens), jnp.int32),
             pltpu.SMEM((3 * count, tokens), jnp.int32),
             pltpu.VMEM(eg_t.shape, BF16), pltpu.VMEM(eu_t.shape, BF16), pltpu.VMEM(ed.shape, BF16),
             pltpu.VMEM((cap, 128), BF16),
-            pltpu.SemaphoreType.DMA, pltpu.SemaphoreType.DMA, pltpu.SemaphoreType.DMA((3, count)),
+            pltpu.SemaphoreType.DMA, pltpu.SemaphoreType.DMA, pltpu.SemaphoreType.DMA((2, 2)),
+            pltpu.SemaphoreType.DMA((3, count)),
             pltpu.SemaphoreType.DMA((2,))],
         compiler_params=pltpu.CompilerParams(vmem_limit_bytes=VMEM_LIMIT),
-    )(meta, mall, eg_t, eu_t, ed)
-
-
-def back_kernel(h_ref, gains_ref, moe_hbm, wg_hbm, wu_hbm, wd_hbm, out_ref,
-                keep, give, take, ring, relay_x, got_x, swap, own, c_s, wg, wu, wd, part, relay, got, full,
+    )(meta, pos, k_new, v_new, kc, vc, mall, eg_t, eu_t, ed)
+
+
+def back_kernel(hsum_ref, gres_ref, moe_hbm, wg_hbm, wu_hbm, wd_hbm, out_ref,
+                keep, give, take, ring, relay_x, got_x, swap, own, c_s, wg, wu, wd, hid, part, relay, got, full,
                 send_sems, recv_sems, load_sems):
-    tokens, dim = h_ref.shape
+    tokens, dim = hid.shape
     ep, me, core, partner, right, left, far = ring_ids()
     tp, mt = lax.axis_size("tp"), lax.axis_index("tp")
     halfd = dim // 2
@@ -513,6 +571,9 @@
         load.start()
     meet([partner, right, left], [lax.rem(mt + 1, tp), lax.rem(mt + tp - 1, tp)])
     links = Links(send_sems, recv_sems)
+    mid = RowSum(links, 17, "tp", hid)
+    hid[mid.rows(mid.me, None), :] = hsum_ref[...]
+    mid.spread()
     for i in range(4):
         give_loads[i].wait()
         links.send(i, give.at[i], take.at[i], {"ep": partner})
@@ -533,21 +594,23 @@
     links.send(7, ring.at[2, :, lo], got_x.at[1, 0], to_left)
     add_pair(3)
 
-    wide = h_ref[...].astype(F32)
-    inv = lax.rsqrt(jnp.mean(wide * wide, axis=-1, keepdims=True) + NORM_EPS)
-    c_s[...] = (wide * inv * gains_ref[1:2, :]).astype(BF16)
+    mid.forward()
+    mid.finish()
+    wide = hid[...].astype(F32)
+    inv = rms(wide)
+    c_s[...] = (wide * inv * gain_row(gres_ref)).astype(BF16)
     w_loads[0].wait()
     w_loads[1].wait()
     acts = []
-    for i in range(wg.shape[1] // 512):
-        cols = slice(i * 512, (i + 1) * 512)
+    for i in range(wg.shape[1] // COLS):
+        cols = span(i, COLS)
         gate = mm(c_s[...], wg[:, cols])
         up = mm(c_s[...], wu[:, cols])
         acts.append((jax.nn.silu(gate) * up).astype(BF16))
     act = jnp.concatenate(acts, axis=1)
     w_loads[2].wait()
-    for i in range(dim // 512):
-        cols = slice(i * 512, (i + 1) * 512)
+    for i in range(dim // COLS):
+        cols = span(i, COLS)
         own[:, cols] = mm(act, wd[:, cols])
 
     links.recv(4)
@@ -563,7 +626,7 @@
     def arrived(at):
         pieces = []
         for q in (0, 1):
-            cols = slice(q * quart, (q + 1) * quart)
+            cols = span(q, quart)
             pieces.append(ring[3, at, cols].astype(F32) + got_x[0, q, at, :].astype(F32)
                           + got_x[1, q, at, :].astype(F32))
         return jnp.concatenate(pieces, axis=1)
@@ -575,18 +638,19 @@
     links.recv(10)
     own[:, other] += swap[1].astype(F32)
     part[:, other] = own[:, other].astype(BF16)
-    tp_sum = RowSum(links, 11, part, relay, got, full, "tp")
+    tp_sum = RowSum(links, 11, "tp", full, part, relay, got)
     tp_sum.start()
     tp_sum.pass_on()
-    tp_sum.finish_sum(own, h_ref)
+    tp_sum.collect(own, hid)
+    tp_sum.spread()
     tp_sum.forward()
     tp_sum.finish()
     out_ref[...] = full[...]
     links.drain()
 
 
-def back(h, gains, moe, w_gate, w_up, w_down, tp):
-    tokens, dim = h.shape
+def back(h_sum, g_res, moe, w_gate, w_up, w_down, tp):
+    tokens, dim = h_sum.shape[0] * tp, h_sum.shape[1]
     pair, halfd, quart = 2 * tokens, dim // 2, dim // 4
     chips = moe.shape[0] // pair
     return pl.pallas_call(
@@ -601,10 +665,10 @@
             pltpu.VMEM((4, pair, quart), BF16), pltpu.VMEM((2, 2, pair, quart), BF16),
             pltpu.VMEM((2, tokens, halfd), BF16), pltpu.VMEM((tokens, dim), F32), pltpu.VMEM((tokens, dim), BF16),
             pltpu.VMEM(w_gate.shape, BF16), pltpu.VMEM(w_up.shape, BF16), pltpu.VMEM(w_down.shape, BF16),
-            *row_sum_scratch(tokens, dim, tp),
-            pltpu.SemaphoreType.DMA((23,)), pltpu.SemaphoreType.DMA((23,)), pltpu.SemaphoreType.DMA((11,))],
+            pltpu.VMEM((tokens, dim), BF16), *row_sum_scratch(tokens, dim, tp),
+            pltpu.SemaphoreType.DMA((29,)), pltpu.SemaphoreType.DMA((29,)), pltpu.SemaphoreType.DMA((11,))],
         compiler_params=pltpu.CompilerParams(collective_id=1, has_side_effects=True, vmem_limit_bytes=VMEM_LIMIT),
-    )(h, gains, moe, w_gate, w_up, w_down)
+    )(h_sum, g_res, moe, w_gate, w_up, w_down)
 
 
 def solution(mesh):
@@ -619,16 +683,13 @@
     def local_layer(hidden_in, positions, expert_ids, k_cache, v_cache, norm_in, norm_res, norm_post, w_q, w_k, w_v, w_o, w_gate, w_up, w_down, w_router, e_gate, e_up, e_down):
         tokens, dim = hidden_in.shape
         slots, head = k_cache.shape[1], k_cache.shape[3]
-        freq = (1.0 / (ROPE_BASE ** (jnp.arange(0, head, 2, dtype=F32) / head)))[None, :]
-        freq = jnp.concatenate([freq, freq], axis=1)
-        gains = jnp.stack([norm_in, norm_res, norm_post]).astype(F32)
-        h, k_new, v_new, meta, mall = front(
-            hidden_in, expert_ids.T, positions, freq, gains, w_router,
-            k_cache.reshape(tokens, slots, head), v_cache.reshape(tokens, slots, head), w_q, w_k, w_v, w_o, ep, tp)
-        moe = experts(meta, mall.reshape(ep * tokens, dim), jnp.swapaxes(e_gate, 1, 2), jnp.swapaxes(e_up, 1, 2), e_down)
-        slot_hit = (jnp.arange(slots)[None, :] == positions[:, None])[:, :, None, None]
-        k_out = jnp.where(slot_hit, k_new[:, None, None, :], k_cache)
-        v_out = jnp.where(slot_hit, v_new[:, None, None, :], v_cache)
-        return back(h, gains, moe, w_gate, w_up, w_down, tp), k_out, v_out
+        kc, vc = (cache.reshape(tokens, slots, head) for cache in (k_cache, v_cache))
+        h_sum, k_new, v_new, meta, mall = front(
+            hidden_in, expert_ids.T, positions, norm_in, norm_post, w_router, kc, vc, w_q, w_k, w_v, w_o, ep, tp)
+        moe, k_out, v_out = experts(
+            meta, positions, k_new, v_new, kc, vc, mall.reshape(ep * tokens, dim),
+            jnp.swapaxes(e_gate, 1, 2), jnp.swapaxes(e_up, 1, 2), e_down)
+        hidden_out = back(h_sum, norm_res, moe, w_gate, w_up, w_down, tp)
+        return hidden_out, k_out.reshape(k_cache.shape), v_out.reshape(v_cache.shape)
 
     return jax.shard_map(local_layer, mesh=mesh, in_specs=in_specs, out_specs=out_specs, check_vma=False)

time: 128 us -> 105 us (0.82); the launches traced: 126 us -> 105 us
  Pallas kernels: 116 us -> 102 us
  other arithmetic: 6.13 us -> 0 us
    pallas_call x2, Pallas kernels: 70.4 us -> 57.8 us  [the longest x1 32 us: front(): pl.pallas_call(front_kernel, name='front', out_shape=(shape((tokens // tp...]
    select_n x1 -> x0, other arithmetic: 4.8 us -> none  [local_layer(): v_out = jnp.where(slot_hit, v_new[:, None, None, :], v_cache)]
    another operation x3 -> x0, local copies, waits for them, and re-layouts: 2.08 us -> none  [local_layer(): gains = jnp.stack([norm_in, norm_res, norm_post]).astype(F32)]
    pallas_call x1, Pallas kernels: 45.9 us -> 44.4 us  [back(): pl.pallas_call(back_kernel, name='back', out_shape=jax.ShapeDtypeStruct((...]
where the time goes in v2:
time: 105 us
  Pallas kernels  102 us (97%)
  local copies, waits for them, and re-layouts  1.88 us (2%)
    pallas_call x1, Pallas kernels, back(): pl.pallas_call(back_kernel, name='back', out_shape=jax.ShapeDtypeStruct((...  44.4 us
    pallas_call x1, Pallas kernels, front(): pl.pallas_call(front_kernel, name='front', out_shape=(shape((tokens // tp...  32 us
    pallas_call x1, Pallas kernels, experts(): pl.pallas_call(expert_kernel, name='experts', out_shape=(jax.ShapeDtypeSt...  25.9 us

profile of v2, /device:TPU:97, one launch (start us, length us, event | category | flops | bytes accessed | tf_op | source)
XLA Modules:
  0.0 104.8 jit_solution(7197898167175111716)
XLA Ops:
  0.6 32.0 %front.1 = (bf16[32,2048]{1,0:T(8,128)(2,1)}, bf16[128,128]{1,0:T(8,128)(2,1)}, bf16[128,128]{1,0:T(8,128)(2,1)}, f32[8,8,128]{2,1,0:T(8,128)}, bf16[8,128,2048]{2,1,0:T(8,128)(2,1)}) custom-call(bf16[128,2048]{1,0:T(8,128)(2,1)} %x_ref.1, s32[2,128]{1,0:T(2,128)} %bitcast.19, s32[128]{0:T(128)} %pos_ref.3, bf16[2048]{0:T(1024)(128)(2,1)} %gin_ref.1, ...), custom_call_target="tpu_custom_call" | custom-call | tf_op jit(solution)/shard_map/front/pallas_call | solution.py:344
  32.6 25.9 %experts.1 = (bf16[1024,2048]{1,0:T(8,128)(2,1)}, bf16[128,64,128]{2,1,0:T(8,128)(2,1)}, bf16[128,64,128]{2,1,0:T(8,128)(2,1)}) custom-call(f32[8,8,128]{2,1,0:T(8,128)} %get-tuple-element.12.meta_ref, s32[128]{0:T(128)} %pos_ref.3, bf16[128,128]{1,0:T(8,128)(2,1)} %get-tuple-element.13.knew_ref, bf16[128,128]{1,0:T(8,128)(2,1)} %get-tuple-element.14.vnew_ref, ...), custom_call_target="tpu_custom_call" | custom-call | tf_op jit(solution)/shard_map/experts/pallas_call | solution.py:525
  58.5 44.4 %back.1 = bf16[128,2048]{1,0:T(8,128)(2,1)} custom-call(bf16[32,2048]{1,0:T(8,128)(2,1)} %get-tuple-element.11.hsum_ref, bf16[2048]{0:T(1024)(128)(2,1)} %gres_ref.1, bf16[1024,2048]{1,0:T(8,128)(2,1)} %get-tuple-element.16.moe_hbm, bf16[2048,1536]{1,0:T(8,128)(2,1)} %wg_hbm.1, bf16[2048,1536]{1,0:T(8,128)(2,1)} %wu_hbm.1, bf16[1536,2048]{1,0:T(8,128)(2,1)} %wd_hbm.1), custom_call_target="tpu_custom_call" | custom-call | tf_op jit(solution)/shard_map/back/pallas_call | solution.py:656
  102.9 1.9 %copy.25 = bf16[128,2048]{1,0:T(8,128)(2,1)} copy(bf16[128,2048]{1,0:T(8,128)(2,1)} %back.1) | data formatting | bytes 1048576

commit v3 on v0

v3 whole, which is shorter than its diff:
```python
import functools

import jax
import jax.numpy as jnp
import numpy as np
from jax import lax
from jax.experimental import pallas as pl
from jax.experimental.pallas import tpu as pltpu
from jax.sharding import PartitionSpec as P

NORM_EPS = 1e-5
ROPE_BASE = 10000.0
MESH = pl.DeviceIdType.MESH
F32 = jnp.float32
BF16 = jnp.bfloat16
WIN = 32
ALIGN = 16
COLS = 512
VMEM_LIMIT = 67000000

ANY = pl.BlockSpec(memory_space=pl.ANY)
VMEM = pl.BlockSpec(memory_space=pltpu.VMEM)
SMEM = pl.BlockSpec(memory_space=pltpu.SMEM)


def nt_dot(a, b):
    return lax.dot_general(a, b, (((1,), (1,)), ((), ())), preferred_element_type=F32)


def mm(a, b):
    return jnp.dot(a, b, preferred_element_type=F32)


def span(i, width):
    return slice(i * width, (i + 1) * width)


def total(v, axis):
    return jnp.sum(v, axis=axis, keepdims=True)


def exp_rows(v):
    return jnp.exp(v - jnp.max(v, axis=-1, keepdims=True))


def rms(wide):
    return lax.rsqrt(jnp.mean(wide * wide, axis=-1, keepdims=True) + NORM_EPS)


def iota(shape, dim):
    return lax.broadcasted_iota(jnp.int32, shape, dim)


def gain_row(ref):
    return ref[...].astype(F32).reshape(1, ref.shape[0])


class Links:
    def __init__(self, send_sems, recv_sems):
        self.send_sems, self.recv_sems, self.started, self.unsent = send_sems, recv_sems, {}, []

    def copy(self, i):
        src, dst, device = self.started[i]
        return pltpu.make_async_remote_copy(
            src_ref=src(), dst_ref=dst(), send_sem=self.send_sems.at[i], recv_sem=self.recv_sems.at[i],
            device_id=device, device_id_type=MESH)

    def send(self, i, src, device, dst=None):
        self.started[i] = (src, dst or src, device)
        self.copy(i).start()
        self.unsent.append(i)

    def recv(self, *ids):
        for i in ids:
            self.copy(i).wait_recv()

    def drain(self):
        for i in self.unsent:
            self.copy(i).wait_send()
        self.unsent = []


def at(ref, *index):
    return lambda: ref.at[index]


class RowSum:
    def __init__(self, links, base, axis, full, part=None, relay=None, got=None):
        self.links, self.base, self.part, self.relay, self.got, self.full = links, base, part, relay, got, full
        self.size = lax.axis_size(axis)
        self.me = lax.axis_index(axis)
        self.right = lax.rem(self.me + 1, self.size)
        self.left = lax.rem(self.me + self.size - 1, self.size)
        self.far = lax.rem(self.me + 2, self.size)
        self.to_right, self.to_left = {axis: self.right}, {axis: self.left}
        self.block = full.shape[0] // self.size
        self.half = self.block // 2

    def rows(self, rank, half):
        if half is None:
            return pl.ds(pl.multiple_of(rank * self.block, self.block), self.block)
        return pl.ds(pl.multiple_of(rank * self.block + half * self.half, self.half), self.half)

    def send(self, i, device, src, dst=None):
        buf, *rows = src
        self.links.send(self.base + i, (lambda: buf.at[self.rows(*rows)]) if rows else (lambda: buf), device, dst)

    def recv(self, *ids):
        self.links.recv(*[self.base + i for i in ids])

    def start(self):
        part, relay, got = self.part, self.relay, self.got
        self.send(0, self.to_right, (part, self.far, 0), at(relay, 0))
        self.send(1, self.to_left, (part, self.far, 1), at(relay, 1))
        self.send(2, self.to_right, (part, self.right, 1), at(got, 0, 1))
        self.send(3, self.to_left, (part, self.left, 0), at(got, 1, 0))

    def pass_on(self):
        part, relay = self.part, self.relay
        for n, (dest, device) in enumerate([(self.right, self.to_right), (self.left, self.to_left)]):
            self.recv(n)
            relay[2 + n] = (part[self.rows(dest, n), :].astype(F32) + relay[n].astype(F32)).astype(BF16)
            self.send(4 + n, device, (relay.at[2 + n],), at(self.got, n, n))

    def collect(self, own, rest):
        self.recv(2, 3, 4, 5)
        for half in range(2):
            here = self.rows(self.me, half)
            acc = own[here, :] + self.got[0, half].astype(F32) + self.got[1, half].astype(F32)
            self.full[here, :] = (rest[here, :].astype(F32) + acc).astype(BF16)

    def spread(self):
        for n, device in enumerate([self.to_right, self.to_left]):
            self.send(6 + n, device, (self.full, self.me, n))
        for n, device in enumerate([self.to_right, self.to_left]):
            self.send(8 + n, device, (self.full, self.me, 1 - n))

    def forward(self):
        for n, (block, device) in enumerate([(self.left, self.to_right), (self.right, self.to_left)]):
            self.recv(6 + n)
            self.send(10 + n, device, (self.full, block, n))

    def finish(self):
        self.recv(8, 9, 10, 11)


def row_sum_scratch(rows, cols, tp):
    half = rows // tp // 2
    return [pltpu.VMEM((rows, cols), BF16), pltpu.VMEM((4, half, cols), BF16),
            pltpu.VMEM((2, 2, half, cols), BF16), pltpu.VMEM((rows, cols), BF16)]


def ring_ids():
    ep = lax.axis_size("ep")
    me = lax.axis_index("ep")
    core = lax.rem(me, 2)
    partner = me + 1 - 2 * core
    return ep, me, core, partner, lax.rem(me + 2, ep), lax.rem(me + ep - 2, ep), lax.rem(me + 4, ep)


ROWS, ATT, FAR, META, TWIN, GIVE, RING, SWAP, LAST = 0, 5, 17, 20, 28, 34, 38, 44, 45
COPIES = 57


def layer_kernel(x_ref, ids_ref, pos_ref, gin_ref, gpost_ref, gres_ref, wr_ref, kc_hbm, vc_hbm, wq_hbm, wk_hbm, wv_hbm,
                 wo_hbm, eg_hbm, eu_hbm, ed_hbm, wg_hbm, wu_hbm, wd_hbm, out_ref, knew_ref, vnew_ref,
                 mall, meta, a_s, own, pos_row, pos_col, plan, plan_s, take, ring, relay_x, got_x, swap,
                 part, relay, got, hid, part_b, relay_b, got_b, full_b, send_sems, recv_sems, load_sems, plan_sem, w_sems):
    tokens, dim = x_ref.shape
    head = wk_hbm.shape[1]
    heads = wq_hbm.shape[1] // head
    slots = kc_hbm.shape[1]
    count, width = ed_hbm.shape[0], ed_hbm.shape[1]
    ep, me, core, partner, right, left, far = ring_ids()
    tp, mt = lax.axis_size("tp"), lax.axis_index("tp")
    to_right, to_left, to_partner = {"ep": right}, {"ep": left}, {"ep": partner}
    peers = [lax.rem(me + i, ep) for i in range(1, ep)]
    barrier = pltpu.get_barrier_semaphore()
    for peer in peers:
        pl.semaphore_signal(barrier, inc=1, device_id={"ep": peer}, device_id_type=MESH)
    for peer in (lax.rem(mt + 1, tp), lax.rem(mt + tp - 1, tp)):
        pl.semaphore_signal(barrier, inc=1, device_id={"tp": peer}, device_id_type=MESH)
    links = Links(send_sems, recv_sems)
    att_sum = RowSum(links, ATT, "tp", hid, part, relay, got)
    hrow = tokens // 2

    def half(i, h):
        return at(mall, i, pl.ds(h * hrow, hrow))

    def twin(i):
        return i + 1 - 2 * lax.rem(i, 2)

    def attention(kc, vc, wq, wk, wv, wo, q_s, o_s, k_s, v_s, pcol):
        loads = [pltpu.make_async_copy(src, dst, load_sems.at[i]) for i, (src, dst) in enumerate(
            [(wq_hbm, wq), (wk_hbm, wk), (wv_hbm, wv), (kc_hbm, kc), (vc_hbm, vc), (wo_hbm, wo)])]
        for load in loads:
            load.start()
        wide = x_ref[...].astype(F32)
        inv = rms(wide)
        mall[me] = (wide * inv * gain_row(gpost_ref)).astype(BF16)
        a_s[...] = (wide * inv * gain_row(gin_ref)).astype(BF16)
        pl.semaphore_wait(barrier, len(peers) + 2)
        first = [(0, right), (1, left), (1, right), (0, left)]
        for n, (h, device) in enumerate(first):
            links.send(ROWS + n, half(me, h), {"ep": device})
        links.send(ROWS + len(first), at(mall, me), to_partner)

        logits = mm(mall[me], wr_ref[...])
        probs = exp_rows(logits)
        probs = probs / total(probs, 1)
        experts = logits.shape[1]
        ids = ids_ref[...].astype(F32)
        lane = iota((tokens, experts), 1).astype(F32)
        id_rows = [ids[k:k + 1, :] for k in range(2)]
        picked = [total(jnp.where(jnp.transpose(jnp.broadcast_to(row, (experts, tokens))) == lane, probs, 0.0), 1)
                  for row in id_rows]
        both = picked[0] + picked[1]
        sub = iota((8, tokens), 0)
        block = jnp.zeros((8, tokens), F32)
        wts = [jnp.transpose(jnp.broadcast_to(p / both, (tokens, tokens)))[0:8, :] for p in picked]
        for n, row in enumerate(id_rows + wts):
            block = jnp.where(sub == n, row, block)
        meta[me] = block
        for n, peer in enumerate(peers):
            links.send(META + n, at(meta, me), {"ep": peer})

        def pos_body(g, carry):
            row = iota((8, head), 0)
            acc = jnp.zeros((8, head), jnp.int32)
            for j in range(8):
                acc = jnp.where(row == j, pos_ref[g * 8 + j], acc)
            pcol[pl.ds(pl.multiple_of(g * 8, 8), 8), :] = acc
            return carry

        lax.fori_loop(0, tokens // 8, pos_body, 0)
        spot = iota((tokens, head), 1)
        power = lax.rem(spot, head // 2).astype(F32) * (-np.log(ROPE_BASE) / (head // 2))
        angles = pcol[...].astype(F32) * jnp.exp(power)
        cosine = jnp.cos(angles)
        sine = jnp.sin(angles)
        sine = jnp.where(spot < head // 2, -sine, sine)

        def rope(v):
            return (v * cosine + pltpu.roll(v, head // 2, 1) * sine).astype(BF16).astype(F32)

        for load in loads[:3]:
            load.wait()
        normed = a_s[...]
        k_s[...] = rope(mm(normed, wk[...]))
        v_s[...] = mm(normed, wv[...]).astype(BF16).astype(F32)
        knew_ref[...] = k_s[...].astype(BF16)
        vnew_ref[...] = v_s[...].astype(BF16)
        for i in range(heads // 2):
            q2 = mm(normed, wq[:, span(i, 2 * head)])
            for j in range(2):
                q_s[2 * i + j] = rope(q2[:, span(j, head)])
        for load in loads[3:5]:
            load.wait()

        def attend(g, carry):
            base = pl.multiple_of(g * 8, 8)
            slot = iota((slots, head), 0)
            pairs = []
            for new, old in ((k_s, kc), (v_s, vc)):
                pieces = [jnp.where(slot == pos_ref[g * 8 + j], new[pl.ds(base + j, 1), :], old[base + j].astype(F32))
                          for j in range(8)]
                pairs.append(jnp.concatenate([piece.astype(BF16) for piece in pieces], axis=0))
            keys, vals = pairs
            q8 = q_s[:, pl.ds(base, 8), :].reshape(heads * 8, head).astype(BF16)
            scores = nt_dot(q8, keys) * (head ** -0.5)
            each = (8, 8 * slots)
            col = iota(each, 1)
            row_pos = jnp.concatenate([pcol[pl.ds(base, 8), :]] * (8 * slots // head), axis=1)
            mask = (col // slots == iota(each, 0)) & (lax.rem(col, slots) <= row_pos)
            mask = jnp.broadcast_to(mask[None], (heads, *each)).reshape(heads * 8, 8 * slots)
            e = exp_rows(jnp.where(mask, scores, -1e30))
            o8 = mm((e / total(e, 1)).astype(BF16), vals)
            o_s[:, pl.ds(base, 8), :] = o8.reshape(heads, 8, head)
            return carry

        lax.fori_loop(0, tokens // 8, attend, 0)
        mix = jnp.concatenate([o_s[i].astype(BF16) for i in range(heads)], axis=1)
        loads[5].wait()
        for i in range(dim // COLS):
            cols = span(i, COLS)
            piece = mm(mix, wo[:, cols])
            own[:, cols] = piece
            part[:, cols] = piece.astype(BF16)
        att_sum.start()

    kv = pltpu.VMEM((tokens, head), F32)
    each_head = pltpu.VMEM((heads, tokens, head), F32)
    pl.run_scoped(
        attention, *[pltpu.VMEM(ref.shape, BF16) for ref in (kc_hbm, vc_hbm, wq_hbm, wk_hbm, wv_hbm, wo_hbm)],
        each_head, each_head, kv, kv, pltpu.VMEM((tokens, head), jnp.int32))

    chips = [far // 2, right // 2, left // 2, me // 2]
    halfd = dim // 2
    quart = halfd // 2
    mine = pl.ds(pl.multiple_of(core * halfd, halfd), halfd)
    other = pl.ds(pl.multiple_of((1 - core) * halfd, halfd), halfd)
    lo, hi, full = pl.ds(0, quart), pl.ds(quart, quart), slice(None)

    def chip_rows(chip):
        return pl.ds(chip * 2, 2)

    def add_pair(i):
        links.recv(GIVE + i)
        for j in range(2):
            ring[i, j] = (mall[chips[i] * 2 + j, :, mine].astype(F32) + take[i, j].astype(F32)).astype(BF16)

    def moe(srt, wt_slot, eg, eu, ed):
        loads = []
        for i, (src, dst) in enumerate([(eg_hbm, eg), (eu_hbm, eu), (ed_hbm, ed)]):
            load = pltpu.make_async_copy(src, dst, w_sems.at[i])
            load.start()
            loads.append(load)
        cap = srt.shape[0]
        rows = min(cap, COLS)

        for n, (block, h, device) in enumerate([(left, 0, right), (right, 1, left)]):
            links.recv(ROWS + n)
            links.send(FAR + n, half(block, h), {"ep": device})
            links.send(TWIN + n, half(block, h), to_partner)

        links.recv(*range(META, META + len(peers)))
        begin = (me * count).astype(F32)
        before = (iota((tokens, tokens), 0) < iota((tokens, tokens), 1)).astype(F32).astype(BF16)
        expert = iota((count, tokens), 0).astype(F32)
        hots, ranks, local, wts = [], [], [], []
        seen = jnp.zeros((count, 1), F32)
        for s in range(ep):
            block = meta[s]
            one, two = block[0:1, :] - begin, block[1:2, :] - begin
            in_one = (one >= 0) & (one < count)
            in_two = (two >= 0) & (two < count)
            took = jnp.where(in_one, one, jnp.where(in_two, two, -1.0))
            wts.append(jnp.where(in_one, block[2:3, :], jnp.where(in_two, block[3:4, :], 0.0)))
            hot = (expert == took).astype(F32)
            hots.append(hot)
            local.append(took)
            ranks.append(mm(hot.astype(BF16), before) + seen)
            seen = seen + total(hot, 1)
        tiles = jnp.broadcast_to(jnp.floor((seen + (WIN - 1)) * (1.0 / WIN)), (count, tokens))
        earlier = (iota((count, count), 1) < iota((count, count), 0)).astype(F32).astype(BF16)
        start = mm(earlier, tiles.astype(BF16))
        ended = (start + tiles <= iota((count, tokens), 1).astype(F32)).astype(F32)
        plan[...] = jnp.broadcast_to(jnp.minimum(total(ended, 0), count - 1.0), plan.shape).astype(jnp.int32)
        plan_copy = pltpu.make_async_copy(plan, plan_s, plan_sem)
        plan_copy.start()
        for s in range(ep):
            place = total(hots[s] * (start * WIN + ranks[s]), 0)
            place = jnp.where(local[s] >= 0, place, -1.0)
            pos_row[s] = jnp.broadcast_to(place, (8, tokens))
            pos_col[s] = jnp.transpose(jnp.broadcast_to(place, (tokens, tokens)))
        plan_copy.wait()

        for c in range(cap // rows):
            slot = (iota((rows, tokens), 0) + c * rows).astype(F32)
            wt = jnp.zeros((rows, tokens), F32)
            for s in range(ep):
                wt = wt + jnp.where(slot == pos_row[s, 0:1, :], wts[s], 0.0)
            wt_slot[span(c, rows), :] = jnp.broadcast_to(total(wt, 1), (rows, tokens))

        def gather(one, fresh):
            two = twin(one)

            def body(c, carry):
                here = pl.ds(pl.multiple_of(c * rows, rows), rows)
                slot = (iota((rows, tokens), 0) + c * rows).astype(F32)
                pick = jnp.concatenate([(slot == pos_row[s, 0:1, :]).astype(F32).astype(BF16) for s in (one, two)], axis=1)
                for i in range(dim // COLS):
                    cols = span(i, COLS)
                    got_rows = mm(pick, jnp.concatenate([mall[one, :, cols], mall[two, :, cols]], axis=0))
                    if not fresh:
                        got_rows = got_rows + srt[here, cols].astype(F32)
                    srt[here, cols] = got_rows.astype(BF16)
                return carry

            lax.fori_loop(0, cap // rows, body, 0)

        links.recv(ROWS + 4)
        gather(me, True)
        att_sum.pass_on()
        att_sum.collect(own, x_ref)
        att_sum.spread()
        for n, (block, h) in enumerate([(left, 1), (right, 0)]):
            links.recv(ROWS + 2 + n)
            links.send(TWIN + 2 + n, half(block, h), to_partner)
        att_sum.forward()
        for n, block in enumerate([left, right]):
            links.recv(TWIN + n, TWIN + 2 + n)
            gather(block, False)
        for n in range(2):
            links.recv(FAR + n)
            links.send(TWIN + 4 + n, half(far, n), to_partner)
        att_sum.finish()
        links.recv(TWIN + 4, TWIN + 5)
        gather(far, False)
        for load in loads:
            load.wait()

        def tile(i, carry):
            e = jnp.minimum(jnp.maximum(plan_s[0, i], 0), count - 1)
            here = pl.ds(pl.multiple_of(i * WIN, WIN), WIN)
            x = srt[here, :]
            act = jnp.transpose(jax.nn.silu(nt_dot(eg[e], x)) * nt_dot(eu[e], x)).astype(BF16)
            wt = wt_slot[here, :][:, 0:1]
            for i in range(dim // COLS):
                cols = span(i, COLS)
                srt[here, cols] = (mm(act, ed[e, :, cols]) * wt).astype(BF16)
            return carry

        lax.fori_loop(0, cap // WIN, tile, 0)
        links.drain()

        lane = iota((2 * tokens, tokens), 1).astype(F32)

        def scatter(i):
            where = pos_col[chip_rows(chips[i])].reshape(2 * tokens, tokens)
            pick = jnp.concatenate([(where == lane + j * tokens).astype(F32).astype(BF16)
                                    for j in range(cap // tokens)], axis=1)
            for n in range(dim // COLS):
                cols = span(n, COLS)
                mall[chip_rows(chips[i]), :, cols] = mm(pick, srt[:, cols]).astype(BF16).reshape(2, tokens, COLS)
            links.send(GIVE + i, lambda: mall.at[chip_rows(chips[i]), :, other], to_partner, at(take, i))

        scatter(0)
        scatter(1)
        add_pair(0)
        links.send(RING, at(ring, 0, full, full, lo), to_right, at(relay_x, 0))
        links.send(RING + 1, at(ring, 0, full, full, hi), to_left, at(relay_x, 1))
        scatter(2)
        add_pair(1)
        links.send(RING + 2, at(ring, 1, full, full, hi), to_right, at(got_x, 0, 1))
        scatter(3)
        add_pair(2)
        links.send(RING + 3, at(ring, 2, full, full, lo), to_left, at(got_x, 1, 0))
        add_pair(3)

    cap = ep * tokens // 2 + count * WIN
    pl.run_scoped(
        moe, pltpu.VMEM((cap, dim), BF16), pltpu.VMEM((cap, tokens), F32),
        *[pltpu.VMEM(ref.shape, BF16) for ref in (eg_hbm, eu_hbm, ed_hbm)])

    def dense(wg, wu, wd):
        loads = [pltpu.make_async_copy(src, dst, load_sems.at[i])
                 for i, (src, dst) in enumerate([(wg_hbm, wg), (wu_hbm, wu), (wd_hbm, wd)])]
        for load in loads:
            load.start()
        wide = hid[...].astype(F32)
        a_s[...] = (wide * rms(wide) * gain_row(gres_ref)).astype(BF16)
        for load in loads[:2]:
            load.wait()
        acts = []
        for i in range(wg.shape[1] // COLS):
            cols = span(i, COLS)
            acts.append((jax.nn.silu(mm(a_s[...], wg[:, cols])) * mm(a_s[...], wu[:, cols])).astype(BF16))
        act = jnp.concatenate(acts, axis=1)
        loads[2].wait()
        for i in range(dim // COLS):
            cols = span(i, COLS)
            own[:, cols] = mm(act, wd[:, cols])

    pl.run_scoped(dense, *[pltpu.VMEM(ref.shape, BF16) for ref in (wg_hbm, wu_hbm, wd_hbm)])

    for n, (dest, cols, device, side) in enumerate([(1, span(0, quart), to_right, 0), (2, span(1, quart), to_left, 1)]):
        links.recv(RING + n)
        relay_x[2 + n] = (ring[dest, :, :, cols].astype(F32) + relay_x[n].astype(F32)).astype(BF16)
        links.send(RING + 4 + n, at(relay_x, 2 + n), device, at(got_x, side, n))
    links.recv(*range(RING + 2, SWAP))

    def arrived(j):
        return jnp.concatenate(
            [ring[3, j, :, span(q, quart)].astype(F32) + got_x[0, q, j].astype(F32) + got_x[1, q, j].astype(F32)
             for q in range(2)], axis=1)

    swap[0] = arrived(1 - core).astype(BF16)
    links.send(SWAP, at(swap, 0), to_partner, at(swap, 1))
    last = RowSum(links, LAST, "tp", full_b, part_b, relay_b, got_b)
    own[:, mine] += arrived(core)
    part_b[:, mine] = own[:, mine].astype(BF16)
    links.recv(SWAP)
    own[:, other] += swap[1].astype(F32)
    part_b[:, other] = own[:, other].astype(BF16)
    last.start()
    last.pass_on()
    last.collect(own, hid)
    last.spread()
    last.forward()
    last.finish()
    out_ref[...] = full_b[...]
    links.drain()


def layer(x, ids_t, pos, g_in, g_post, g_res, w_router, kc, vc, w_q, w_k, w_v, w_o, eg_t, eu_t, ed, w_gate, w_up, w_down, ep, tp):
    tokens, dim = x.shape
    head = w_k.shape[1]
    chips, halfd, quart = ep // 2, dim // 2, dim // 4
    shape = jax.ShapeDtypeStruct
    return pl.pallas_call(
        layer_kernel,
        name="layer",
        out_shape=(shape((tokens, dim), BF16), shape((tokens, head), BF16), shape((tokens, head), BF16)),
        in_specs=[VMEM, VMEM, SMEM] + [VMEM] * 4 + [ANY] * 12,
        out_specs=(VMEM, VMEM, VMEM),
        scratch_shapes=[
            pltpu.VMEM((ep, tokens, dim), BF16), pltpu.VMEM((ep, 8, tokens), F32), pltpu.VMEM((tokens, dim), BF16),
            pltpu.VMEM((tokens, dim), F32), pltpu.VMEM((ep, 8, tokens), F32), pltpu.VMEM((ep, tokens, tokens), F32),
            pltpu.VMEM((8, tokens), jnp.int32), pltpu.SMEM((8, tokens), jnp.int32),
            pltpu.VMEM((chips, 2, tokens, halfd), BF16), pltpu.VMEM((chips, 2, tokens, halfd), BF16),
            pltpu.VMEM((4, 2, tokens, quart), BF16), pltpu.VMEM((2, 2, 2, tokens, quart), BF16),
            pltpu.VMEM((2, tokens, halfd), BF16), *row_sum_scratch(tokens, dim, tp), *row_sum_scratch(tokens, dim, tp),
            pltpu.SemaphoreType.DMA((COPIES,)), pltpu.SemaphoreType.DMA((COPIES,)), pltpu.SemaphoreType.DMA((6,)),
            pltpu.SemaphoreType.DMA, pltpu.SemaphoreType.DMA((3,))],
        compiler_params=pltpu.CompilerParams(collective_id=0, has_side_effects=True, vmem_limit_bytes=VMEM_LIMIT),
    )(x, ids_t, pos, g_in, g_post, g_res, w_router, kc, vc, w_q, w_k, w_v, w_o, eg_t, eu_t, ed, w_gate, w_up, w_down)


def cache_kernel(pos_ref, knew_ref, vnew_ref, hid_ref, kc_hbm, vc_hbm, out_ref, ko_hbm, vo_hbm, kc, vc, k_s, v_s, sems):
    tokens, _, head = kc.shape
    caches = [(kc_hbm, kc, ko_hbm), (vc_hbm, vc, vo_hbm)]
    cache_in = [pltpu.make_async_copy(src, buf, sems.at[0, i]) for i, (src, buf, _) in enumerate(caches)]
    cache_out = [pltpu.make_async_copy(buf, dst, sems.at[1, i]) for i, (_, buf, dst) in enumerate(caches)]
    for copy in cache_in:
        copy.start()
    out_ref[...] = hid_ref[...]
    k_s[...] = knew_ref[...].astype(F32)
    v_s[...] = vnew_ref[...].astype(F32)
    for buf, new, came, goes in zip((kc, vc), (k_s, v_s), cache_in, cache_out):
        came.wait()

        def new_rows(g, carry):
            for j in range(8):
                b = g * 8 + j
                spot = pos_ref[b]
                base = pl.multiple_of(spot // ALIGN * ALIGN, ALIGN)
                hit = iota((ALIGN, head), 0) == spot - base
                tile = buf[b, pl.ds(base, ALIGN), :].astype(F32)
                buf[b, pl.ds(base, ALIGN), :] = jnp.where(hit, new[pl.ds(b, 1), :], tile).astype(BF16)
            return carry

        lax.fori_loop(0, tokens // 8, new_rows, 0)
        goes.start()
    for copy in cache_out:
        copy.wait()


def caches(pos, k_new, v_new, hid, kc, vc):
    shape = jax.ShapeDtypeStruct
    return pl.pallas_call(
        cache_kernel,
        name="caches",
        out_shape=(shape(hid.shape, BF16), shape(kc.shape, BF16), shape(vc.shape, BF16)),
        in_specs=[SMEM, VMEM, VMEM, VMEM, ANY, ANY],
        out_specs=(VMEM, ANY, ANY),
        scratch_shapes=[pltpu.VMEM(kc.shape, BF16), pltpu.VMEM(vc.shape, BF16), pltpu.VMEM(k_new.shape, F32),
                        pltpu.VMEM(v_new.shape, F32), pltpu.SemaphoreType.DMA((2, 2))],
    )(pos, k_new, v_new, hid, kc, vc)


def solution(mesh):
    ep, tp = mesh.shape['ep'], mesh.shape['tp']
    row_spec = P(('dp', 'ep'), None)
    cache_spec = P(('dp', 'ep'), None, 'tp', None)
    col_split = P(None, 'tp')
    row_split = P('tp', None)
    in_specs = (row_spec, P(('dp', 'ep')), row_spec, cache_spec, cache_spec, P(None), P(None), P(None), col_split, col_split, col_split, row_split, col_split, col_split, row_split, P(None, None), P('ep', None, 'tp'), P('ep', None, 'tp'), P('ep', 'tp', None))
    out_specs = (row_spec, cache_spec, cache_spec)

    def local_layer(hidden_in, positions, expert_ids, k_cache, v_cache, norm_in, norm_res, norm_post, w_q, w_k, w_v, w_o, w_gate, w_up, w_down, w_router, e_gate, e_up, e_down):
        tokens, dim = hidden_in.shape
        slots, head = k_cache.shape[1], k_cache.shape[3]
        kc, vc = (cache.reshape(tokens, slots, head) for cache in (k_cache, v_cache))
        hid, k_new, v_new = layer(
            hidden_in, expert_ids.T, positions, norm_in, norm_post, norm_res, w_router, kc, vc, w_q, w_k, w_v, w_o,
            jnp.swapaxes(e_gate, 1, 2), jnp.swapaxes(e_up, 1, 2), e_down, w_gate, w_up, w_down, ep, tp)
        hidden_out, k_out, v_out = caches(positions, k_new, v_new, hid, kc, vc)
        return hidden_out, k_out.reshape(k_cache.shape), v_out.reshape(v_cache.shape)

    return jax.shard_map(local_layer, mesh=mesh, in_specs=in_specs, out_specs=out_specs, check_vma=False)
```

time: 315 us -> 116 us (0.37)
  waiting for transfers between devices: 99.7 us -> 0 us
  local copies, waits for them, and re-layouts: 66.1 us -> 0 us
  Pallas kernels: 57.4 us -> 114 us
  other arithmetic: 31 us -> 0 us
  matrix products: 27.3 us -> 0 us
  starting transfers between devices: 16.1 us -> 0 us
  between operations: 14.5 us -> 0.81 us
    pallas_call x0 -> x2, Pallas kernels: none -> 114 us  [the longest x1 107 us: layer(): pl.pallas_call(layer_kernel, name='layer', out_shape=(shape((tokens, dim)...]
    psum x2 -> x0, waiting for transfers between devices: 64.1 us -> none  [the longest x1 64.1 us: local_layer(): expert_sum = lax.psum(expert_part, 'tp')]
    another operation x3 -> x0, Pallas kernels: 55.5 us -> none
    unnamed x28 -> x0, local copies, waits for them, and re-layouts: 44 us -> none
    all_to_all x3 -> x0, waiting for transfers between devices: 35.5 us -> none  [the longest x1 21.9 us: local_layer(): returned = lax.all_to_all(expert_sum, 'ep', 0, 0, tiled=True)]
    dot_general x9 -> x0, matrix products: 27.3 us -> none  [the longest x1 7.67 us: dense_block(): return jnp.dot(act_val, w_down, preferred_element_type=jnp.float32)]
    all_to_all x3 -> x0, starting transfers between devices: 16 us -> none  [the longest x1 6.02 us: local_layer(): recv_expert = lax.all_to_all(send_expert, 'ep', 0, 0, tiled=True)]
    gather x9 -> x0, local copies, waits for them, and re-layouts: 14.7 us -> none  [the longest x1 3.32 us: local_layer(): send_rows = padded_rows[send_token]]
  transfers between devices with their start and end apart: 5 -> 0, of which waited for: 3 -> 0; matrix products, arithmetic and copies ran while one was open for 24% -> 0% of each run, Pallas kernels for 1% -> 0%
where the time goes in v3:
time: 116 us; the launch traced here: 115 us
  Pallas kernels  114 us (98%)
    pallas_call x1, Pallas kernels, layer(): pl.pallas_call(layer_kernel, name='layer', out_shape=(shape((tokens, dim)...  107 us
    pallas_call x1, Pallas kernels, caches(): pl.pallas_call(cache_kernel, name='caches', out_shape=(shape(hid.shape, B...  6.74 us

profile of v3, /device:TPU:97, one launch (start us, length us, event | category | flops | bytes accessed | tf_op | source)
XLA Modules:
  0.0 114.5 jit_solution(570760960853020044)
XLA Ops:
  0.6 107.0 %layer.1 = (bf16[128,2048]{1,0:T(8,128)(2,1)}, bf16[128,128]{1,0:T(8,128)(2,1)}, bf16[128,128]{1,0:T(8,128)(2,1)}) custom-call(bf16[128,2048]{1,0:T(8,128)(2,1)} %x_ref.1, s32[2,128]{1,0:T(2,128)} %bitcast.17, s32[128]{0:T(128)} %pos_ref.3, bf16[2048]{0:T(1024)(128)(2,1)} %gin_ref.1, bf16[2048]{0:T(1024)(128)(2,1)} %gpost_ref.1, bf16[2048]{0:T(1024)(128)(2,1)} %gres_ref.1, ...), custom_call_target="tpu_custom_call" | custom-call | tf_op jit(solution)/shard_map/layer/pallas_call | solution.py:501
  107.6 6.7 %caches.1 = (bf16[128,2048]{1,0:T(8,128)(2,1)}, bf16[128,64,128]{2,1,0:T(8,128)(2,1)}, bf16[128,64,128]{2,1,0:T(8,128)(2,1)}) custom-call(s32[128]{0:T(128)} %pos_ref.3, bf16[128,128]{1,0:T(8,128)(2,1)} %get-tuple-element.9.knew_ref, bf16[128,128]{1,0:T(8,128)(2,1)} %get-tuple-element.10.vnew_ref, bf16[128,2048]{1,0:T(8,128)(2,1)} %get-tuple-element.11.hid_ref, ...), custom_call_target="tpu_custom_call" | custom-call | tf_op jit(solution)/shard_map/caches/pallas_call | solution.py:551

commit v4 on v3

v4 whole, which is shorter than its diff:
```python
import functools

import jax
import jax.numpy as jnp
import numpy as np
from jax import lax
from jax.experimental import pallas as pl
from jax.experimental.pallas import tpu as pltpu
from jax.sharding import PartitionSpec as P

NORM_EPS = 1e-5
ROPE_BASE = 10000.0
MESH = pl.DeviceIdType.MESH
F32 = jnp.float32
BF16 = jnp.bfloat16
WIN = 64
ALIGN = 16
AHEAD = 8
COLS = 512
PARTS = 4
VMEM_LIMIT = 67000000

ANY = pl.BlockSpec(memory_space=pl.ANY)
VMEM = pl.BlockSpec(memory_space=pltpu.VMEM)
SMEM = pl.BlockSpec(memory_space=pltpu.SMEM)


def nt_dot(a, b):
    return lax.dot_general(a, b, (((1,), (1,)), ((), ())), preferred_element_type=F32)


def mm(a, b):
    return jnp.dot(a, b, preferred_element_type=F32)


def span(i, width):
    return slice(i * width, (i + 1) * width)


def total(v, axis):
    return jnp.sum(v, axis=axis, keepdims=True)


def exp_rows(v):
    return jnp.exp(v - jnp.max(v, axis=-1, keepdims=True))


def rms(wide):
    return lax.rsqrt(jnp.mean(wide * wide, axis=-1, keepdims=True) + NORM_EPS)


def iota(shape, dim):
    return lax.broadcasted_iota(jnp.int32, shape, dim)


def gain_row(ref):
    return ref[...].astype(F32).reshape(1, ref.shape[0])


class Links:
    def __init__(self, send_sems, recv_sems):
        self.send_sems, self.recv_sems, self.started, self.unsent = send_sems, recv_sems, {}, []

    def copy(self, i):
        src, dst, device = self.started[i]
        return pltpu.make_async_remote_copy(
            src_ref=src(), dst_ref=dst(), send_sem=self.send_sems.at[i], recv_sem=self.recv_sems.at[i],
            device_id=device, device_id_type=MESH)

    def send(self, i, src, device, dst=None):
        self.started[i] = (src, dst or src, device)
        self.copy(i).start()
        self.unsent.append(i)

    def recv(self, *ids):
        for i in ids:
            self.copy(i).wait_recv()

    def drain(self):
        for i in self.unsent:
            self.copy(i).wait_send()
        self.unsent = []


def pieces_of(src, dst, sems, i, parts):
    size = src.shape[0] // parts
    copies = [pltpu.make_async_copy(src.at[pl.ds(n * size, size)], dst.at[pl.ds(n * size, size)], sems.at[i, n])
              for n in range(parts)]
    for copy in copies:
        copy.start()
    return copies


def finish(copies):
    for copy in copies:
        copy.wait()


def at(ref, *index):
    return lambda: ref.at[index]


class RowSum:
    def __init__(self, links, base, axis, full, part=None, relay=None, got=None):
        self.links, self.base, self.part, self.relay, self.got, self.full = links, base, part, relay, got, full
        self.size = lax.axis_size(axis)
        self.me = lax.axis_index(axis)
        self.right = lax.rem(self.me + 1, self.size)
        self.left = lax.rem(self.me + self.size - 1, self.size)
        self.far = lax.rem(self.me + 2, self.size)
        self.to_right, self.to_left = {axis: self.right}, {axis: self.left}
        self.block = full.shape[0] // self.size
        self.half = self.block // 2

    def rows(self, rank, half):
        if half is None:
            return pl.ds(pl.multiple_of(rank * self.block, self.block), self.block)
        return pl.ds(pl.multiple_of(rank * self.block + half * self.half, self.half), self.half)

    def send(self, i, device, src, dst=None):
        buf, *rows = src
        self.links.send(self.base + i, (lambda: buf.at[self.rows(*rows)]) if rows else (lambda: buf), device, dst)

    def recv(self, *ids):
        self.links.recv(*[self.base + i for i in ids])

    def start(self):
        part, relay, got = self.part, self.relay, self.got
        self.send(0, self.to_right, (part, self.far, 0), at(relay, 0))
        self.send(1, self.to_left, (part, self.far, 1), at(relay, 1))
        self.send(2, self.to_right, (part, self.right, 1), at(got, 0, 1))
        self.send(3, self.to_left, (part, self.left, 0), at(got, 1, 0))

    def pass_on(self):
        part, relay = self.part, self.relay
        for n, (dest, device) in enumerate([(self.right, self.to_right), (self.left, self.to_left)]):
            self.recv(n)
            relay[2 + n] = (part[self.rows(dest, n), :].astype(F32) + relay[n].astype(F32)).astype(BF16)
            self.send(4 + n, device, (relay.at[2 + n],), at(self.got, n, n))

    def collect(self, own, rest):
        self.recv(2, 3, 4, 5)
        for half in range(2):
            here = self.rows(self.me, half)
            acc = own[here, :] + self.got[0, half].astype(F32) + self.got[1, half].astype(F32)
            self.full[here, :] = (rest[here, :].astype(F32) + acc).astype(BF16)

    def spread(self):
        for n, device in enumerate([self.to_right, self.to_left]):
            self.send(6 + n, device, (self.full, self.me, n))
        for n, device in enumerate([self.to_right, self.to_left]):
            self.send(8 + n, device, (self.full, self.me, 1 - n))

    def forward(self):
        for n, (block, device) in enumerate([(self.left, self.to_right), (self.right, self.to_left)]):
            self.recv(6 + n)
            self.send(10 + n, device, (self.full, block, n))

    def finish(self):
        self.recv(8, 9, 10, 11)


def row_sum_scratch(rows, cols, tp):
    half = rows // tp // 2
    return [pltpu.VMEM((rows, cols), BF16), pltpu.VMEM((4, half, cols), BF16),
            pltpu.VMEM((2, 2, half, cols), BF16), pltpu.VMEM((rows, cols), BF16)]


def ring_ids():
    ep = lax.axis_size("ep")
    me = lax.axis_index("ep")
    core = lax.rem(me, 2)
    partner = me + 1 - 2 * core
    return ep, me, core, partner, lax.rem(me + 2, ep), lax.rem(me + ep - 2, ep), lax.rem(me + 4, ep)


ROWS, ATT, FAR, META, TWIN, FRONT_COPIES = 0, 5, 17, 20, 28, 34
GIVE, RING, SWAP, LAST, MID, BACK_COPIES = 0, 4, 10, 11, 23, 35


def front_kernel(x_ref, ids_ref, pos_ref, gin_ref, gpost_ref, wr_ref, kc_hbm, vc_hbm, wq_hbm, wk_hbm, wv_hbm, wo_hbm,
                 hsum_ref, knew_ref, vnew_ref, place_ref, plan_ref, wt_slot, srt,
                 mall, meta, a_s, own, pos_row, part, relay, got, hid, send_sems, recv_sems, load_sems):
    tokens, dim = x_ref.shape
    head = wk_hbm.shape[1]
    heads = wq_hbm.shape[1] // head
    slots = kc_hbm.shape[1]
    count = plan_ref.shape[0] // 2
    ep, me, core, partner, right, left, far = ring_ids()
    tp, mt = lax.axis_size("tp"), lax.axis_index("tp")
    to_right, to_left, to_partner = {"ep": right}, {"ep": left}, {"ep": partner}
    peers = [lax.rem(me + i, ep) for i in range(1, ep)]
    barrier = pltpu.get_barrier_semaphore()
    for peer in peers:
        pl.semaphore_signal(barrier, inc=1, device_id={"ep": peer}, device_id_type=MESH)
    for peer in (lax.rem(mt + 1, tp), lax.rem(mt + tp - 1, tp)):
        pl.semaphore_signal(barrier, inc=1, device_id={"tp": peer}, device_id_type=MESH)
    links = Links(send_sems, recv_sems)
    att_sum = RowSum(links, ATT, "tp", hid, part, relay, got)
    hrow = tokens // 2

    def half(i, h):
        return at(mall, i, pl.ds(h * hrow, hrow))

    def twin(i):
        return i + 1 - 2 * lax.rem(i, 2)

    def attention(kc, vc, wq, wk, wv, wo, q_s, o_s, k_s, v_s, pcol):
        loads = [pieces_of(src, dst, load_sems, i, PARTS) for i, (src, dst) in enumerate(
            [(wq_hbm, wq), (wk_hbm, wk), (wv_hbm, wv), (kc_hbm, kc), (vc_hbm, vc), (wo_hbm, wo)])]
        wide = x_ref[...].astype(F32)
        inv = rms(wide)
        mall[me] = (wide * inv * gain_row(gpost_ref)).astype(BF16)
        a_s[...] = (wide * inv * gain_row(gin_ref)).astype(BF16)
        pl.semaphore_wait(barrier, len(peers) + 2)
        first = [(0, right), (1, left), (1, right), (0, left)]
        for n, (h, device) in enumerate(first):
            links.send(ROWS + n, half(me, h), {"ep": device})
        links.send(ROWS + len(first), at(mall, me), to_partner)

        logits = mm(mall[me], wr_ref[...])
        probs = exp_rows(logits)
        probs = probs / total(probs, 1)
        experts = logits.shape[1]
        ids = ids_ref[...].astype(F32)
        lane = iota((tokens, experts), 1).astype(F32)
        id_rows = [ids[k:k + 1, :] for k in range(2)]
        picked = [total(jnp.where(jnp.transpose(jnp.broadcast_to(row, (experts, tokens))) == lane, probs, 0.0), 1)
                  for row in id_rows]
        both = picked[0] + picked[1]
        sub = iota((8, tokens), 0)
        block = jnp.zeros((8, tokens), F32)
        wts = [jnp.transpose(jnp.broadcast_to(p / both, (tokens, tokens)))[0:8, :] for p in picked]
        for n, row in enumerate(id_rows + wts):
            block = jnp.where(sub == n, row, block)
        meta[me] = block
        for n, peer in enumerate(peers):
            links.send(META + n, at(meta, me), {"ep": peer})

        def pos_body(g, carry):
            row = iota((8, head), 0)
            acc = jnp.zeros((8, head), jnp.int32)
            for j in range(8):
                acc = jnp.where(row == j, pos_ref[g * 8 + j], acc)
            pcol[pl.ds(pl.multiple_of(g * 8, 8), 8), :] = acc
            return carry

        lax.fori_loop(0, tokens // 8, pos_body, 0)
        spot = iota((tokens, head), 1)
        power = lax.rem(spot, head // 2).astype(F32) * (-np.log(ROPE_BASE) / (head // 2))
        angles = pcol[...].astype(F32) * jnp.exp(power)
        cosine = jnp.cos(angles)
        sine = jnp.sin(angles)
        sine = jnp.where(spot < head // 2, -sine, sine)

        def rope(v):
            return (v * cosine + pltpu.roll(v, head // 2, 1) * sine).astype(BF16).astype(F32)

        for load in loads[:3]:
            finish(load)
        normed = a_s[...]
        k_s[...] = rope(mm(normed, wk[...]))
        v_s[...] = mm(normed, wv[...]).astype(BF16).astype(F32)
        knew_ref[...] = k_s[...].astype(BF16)
        vnew_ref[...] = v_s[...].astype(BF16)
        for i in range(heads // 2):
            q2 = mm(normed, wq[:, span(i, 2 * head)])
            for j in range(2):
                q_s[2 * i + j] = rope(q2[:, span(j, head)])
        for load in loads[3:5]:
            finish(load)

        def attend(g, carry):
            base = pl.multiple_of(g * 8, 8)
            slot = iota((slots, head), 0)
            pairs = []
            for new, old in ((k_s, kc), (v_s, vc)):
                pieces = [jnp.where(slot == pos_ref[g * 8 + j], new[pl.ds(base + j, 1), :], old[base + j].astype(F32))
                          for j in range(8)]
                pairs.append(jnp.concatenate([piece.astype(BF16) for piece in pieces], axis=0))
            keys, vals = pairs
            q8 = q_s[:, pl.ds(base, 8), :].reshape(heads * 8, head).astype(BF16)
            scores = nt_dot(q8, keys) * (head ** -0.5)
            each = (8, 8 * slots)
            col = iota(each, 1)
            row_pos = jnp.concatenate([pcol[pl.ds(base, 8), :]] * (8 * slots // head), axis=1)
            mask = (col // slots == iota(each, 0)) & (lax.rem(col, slots) <= row_pos)
            mask = jnp.broadcast_to(mask[None], (heads, *each)).reshape(heads * 8, 8 * slots)
            e = exp_rows(jnp.where(mask, scores, -1e30))
            o8 = mm((e / total(e, 1)).astype(BF16), vals)
            o_s[:, pl.ds(base, 8), :] = o8.reshape(heads, 8, head)
            return carry

        lax.fori_loop(0, tokens // 8, attend, 0)
        mix = jnp.concatenate([o_s[i].astype(BF16) for i in range(heads)], axis=1)
        finish(loads[5])
        for i in range(dim // COLS):
            cols = span(i, COLS)
            piece = mm(mix, wo[:, cols])
            own[:, cols] = piece
            part[:, cols] = piece.astype(BF16)
        att_sum.start()

    kv = pltpu.VMEM((tokens, head), F32)
    each_head = pltpu.VMEM((heads, tokens, head), F32)
    pl.run_scoped(
        attention, *[pltpu.VMEM(ref.shape, BF16) for ref in (kc_hbm, vc_hbm, wq_hbm, wk_hbm, wv_hbm, wo_hbm)],
        each_head, each_head, kv, kv, pltpu.VMEM((tokens, head), jnp.int32))

    cap = srt.shape[0]
    rows = cap // 2

    for n, (block, h, device) in enumerate([(left, 0, right), (right, 1, left)]):
        links.recv(ROWS + n)
        links.send(FAR + n, half(block, h), {"ep": device})
        links.send(TWIN + n, half(block, h), to_partner)

    links.recv(*range(META, META + len(peers)))
    begin = (me * count).astype(F32)
    before = (iota((tokens, tokens), 0) < iota((tokens, tokens), 1)).astype(F32).astype(BF16)
    expert = iota((count, tokens), 0).astype(F32)
    hots, ranks, local, wts = [], [], [], []
    seen = jnp.zeros((count, 1), F32)
    for s in range(ep):
        block = meta[s]
        one, two = block[0:1, :] - begin, block[1:2, :] - begin
        in_one = (one >= 0) & (one < count)
        in_two = (two >= 0) & (two < count)
        took = jnp.where(in_one, one, jnp.where(in_two, two, -1.0))
        wts.append(jnp.where(in_one, block[2:3, :], jnp.where(in_two, block[3:4, :], 0.0)))
        hot = (expert == took).astype(F32)
        hots.append(hot)
        local.append(took)
        ranks.append(mm(hot.astype(BF16), before) + seen)
        seen = seen + total(hot, 1)
    padded = jnp.broadcast_to(jnp.floor((seen + (ALIGN - 1)) * (1.0 / ALIGN)) * ALIGN, (count, tokens))
    earlier = (iota((count, count), 1) < iota((count, count), 0)).astype(F32).astype(BF16)
    start = mm(earlier, padded.astype(BF16))
    plan_ref[0:count, :] = jnp.broadcast_to(seen, (count, tokens)).astype(jnp.int32)
    plan_ref[count:, :] = start.astype(jnp.int32)
    for s in range(ep):
        place = total(hots[s] * (start + ranks[s]), 0)
        place = jnp.where(local[s] >= 0, place, -1.0)
        pos_row[s] = jnp.broadcast_to(place, (8, tokens))
        place_ref[s:s + 1, :] = place

    wt_slot[cap:, :] = jnp.zeros((WIN, tokens), F32)
    for c in range(cap // rows):
        slot = (iota((rows, tokens), 0) + c * rows).astype(F32)
        wt = jnp.zeros((rows, tokens), F32)
        for s in range(ep):
            wt = wt + jnp.where(slot == pos_row[s, 0:1, :], wts[s], 0.0)
        wt_slot[span(c, rows), :] = jnp.broadcast_to(total(wt, 1), (rows, tokens))

    def gather(one, fresh):
        two = twin(one)

        def body(c, carry):
            here = pl.ds(pl.multiple_of(c * rows, rows), rows)
            slot = (iota((rows, tokens), 0) + c * rows).astype(F32)
            pick = jnp.concatenate([(slot == pos_row[s, 0:1, :]).astype(F32).astype(BF16) for s in (one, two)], axis=1)
            for i in range(dim // COLS):
                cols = span(i, COLS)
                got_rows = mm(pick, jnp.concatenate([mall[one, :, cols], mall[two, :, cols]], axis=0))
                if not fresh:
                    got_rows = got_rows + srt[here, cols].astype(F32)
                srt[here, cols] = got_rows.astype(BF16)
            return carry

        lax.fori_loop(0, cap // rows, body, 0)

    links.recv(ROWS + 4)
    gather(me, True)
    att_sum.pass_on()
    for n, (block, h) in enumerate([(left, 1), (right, 0)]):
        links.recv(ROWS + 2 + n)
        links.send(TWIN + 2 + n, half(block, h), to_partner)
    att_sum.collect(own, x_ref)
    hsum_ref[...] = hid[att_sum.rows(mt, None), :]
    for n, block in enumerate([left, right]):
        links.recv(TWIN + n, TWIN + 2 + n)
        gather(block, False)
    for n in range(2):
        links.recv(FAR + n)
        links.send(TWIN + 4 + n, half(far, n), to_partner)
    links.recv(TWIN + 4, TWIN + 5)
    gather(far, False)
    links.drain()


def sorted_rows(ep, tokens, count):
    most = ep * tokens // 2 + count * (ALIGN - 1)
    return -(-most // (2 * tokens)) * 2 * tokens


def front(x, ids_t, pos, g_in, g_post, w_router, kc, vc, w_q, w_k, w_v, w_o, count, ep, tp):
    tokens, dim = x.shape
    head = w_k.shape[1]
    cap = sorted_rows(ep, tokens, count)
    shape = jax.ShapeDtypeStruct
    return pl.pallas_call(
        front_kernel,
        name="front",
        out_shape=(shape((tokens // tp, dim), BF16), shape((tokens, head), BF16), shape((tokens, head), BF16),
                   shape((ep, tokens), F32), shape((2 * count, tokens), jnp.int32), shape((cap + WIN, tokens), F32),
                   shape((cap, dim), BF16)),
        in_specs=[VMEM, VMEM, SMEM] + [VMEM] * 3 + [ANY] * 6,
        out_specs=(VMEM,) * 7,
        scratch_shapes=[
            pltpu.VMEM((ep, tokens, dim), BF16), pltpu.VMEM((ep, 8, tokens), F32), pltpu.VMEM((tokens, dim), BF16),
            pltpu.VMEM((tokens, dim), F32), pltpu.VMEM((ep, 8, tokens), F32), *row_sum_scratch(tokens, dim, tp),
            pltpu.SemaphoreType.DMA((FRONT_COPIES,)), pltpu.SemaphoreType.DMA((FRONT_COPIES,)),
            pltpu.SemaphoreType.DMA((6, PARTS))],
        compiler_params=pltpu.CompilerParams(collective_id=0, has_side_effects=True, vmem_limit_bytes=VMEM_LIMIT),
    )(x, ids_t, pos, g_in, g_post, w_router, kc, vc, w_q, w_k, w_v, w_o)


def expert_kernel(plan_ref, pos_ref, wt_slot, knew_ref, vnew_ref, kc_hbm, vc_hbm, srt_hbm, eg_hbm, eu_hbm, ed_hbm,
                  out_hbm, ko_hbm, vo_hbm, kc, vc, k_s, v_s, rows, out, eg, eu, ed, rows_sem, cache_sems, w_sems):
    count = eg.shape[0]
    tokens, _, head = kc.shape
    cap, dim = srt_hbm.shape

    def weights(e):
        return [pltpu.make_async_copy(src.at[e], dst.at[e], w_sems.at[i, e])
                for i, (src, dst) in enumerate([(eg_hbm, eg), (eu_hbm, eu), (ed_hbm, ed)])]

    news = ((k_s, kc, kc_hbm, ko_hbm), (v_s, vc, vc_hbm, vo_hbm))
    rows_copy = pltpu.make_async_copy(srt_hbm, rows.at[pl.ds(0, cap)], rows_sem.at[0])
    rows_copy.start()
    came = [pieces_of(src, buf, cache_sems, i, PARTS) for i, (_, buf, src, _) in enumerate(news)]
    for e in range(AHEAD):
        for copy in weights(e):
            copy.start()
    k_s[...] = knew_ref[...].astype(F32)
    v_s[...] = vnew_ref[...].astype(F32)
    out[...] = jnp.zeros_like(out)
    step = tokens // PARTS
    goes = []
    for n in range(PARTS):
        for i, (new, buf, _, dst) in enumerate(news):
            came[i][n].wait()

            def new_rows(g, carry):
                for j in range(8):
                    b = n * step + g * 8 + j
                    spot = pos_ref[b]
                    base = pl.multiple_of(spot // ALIGN * ALIGN, ALIGN)
                    hit = iota((ALIGN, head), 0) == spot - base
                    tile = buf[b, pl.ds(base, ALIGN), :].astype(F32)
                    buf[b, pl.ds(base, ALIGN), :] = jnp.where(hit, new[pl.ds(b, 1), :], tile).astype(BF16)
                return carry

            lax.fori_loop(0, step // 8, new_rows, 0)
            part = pl.ds(n * step, step)
            goes.append(pltpu.make_async_copy(buf.at[part], dst.at[part], cache_sems.at[2 + i, n]))
            goes[-1].start()
    rows_copy.wait()

    def run_expert(e, carry):
        @pl.when(e + AHEAD < count)
        def _():
            for copy in weights(e + AHEAD):
                copy.start()

        for copy in weights(e):
            copy.wait()
        passes = (plan_ref[e, 0] + (WIN - 1)) // WIN
        begin = plan_ref[count + e, 0]

        def one_pass(p, inner):
            here = pl.ds(pl.multiple_of(begin + p * WIN, ALIGN), WIN)
            x = rows[here, :]
            act = jnp.transpose(jax.nn.silu(nt_dot(eg[e], x)) * nt_dot(eu[e], x)).astype(BF16)
            wt = wt_slot[here, :][:, 0:1]
            for i in range(dim // COLS):
                cols = span(i, COLS)
                out[here, cols] = (mm(act, ed[e, :, cols]) * wt).astype(BF16)
            return inner

        lax.fori_loop(0, passes, one_pass, 0)
        return carry

    lax.fori_loop(0, count, run_expert, 0)
    out_copy = pltpu.make_async_copy(out.at[pl.ds(0, cap)], out_hbm, rows_sem.at[1])
    out_copy.start()
    out_copy.wait()
    finish(goes)


def experts(plan, pos, wt_slot, k_new, v_new, kc, vc, srt, eg_t, eu_t, ed):
    shape = jax.ShapeDtypeStruct
    count = ed.shape[0]
    room = (srt.shape[0] + WIN, srt.shape[1])
    return pl.pallas_call(
        expert_kernel,
        name="experts",
        out_shape=(shape(srt.shape, BF16), shape(kc.shape, BF16), shape(vc.shape, BF16)),
        in_specs=[SMEM, SMEM, VMEM, VMEM, VMEM] + [ANY] * 6,
        out_specs=(ANY, ANY, ANY),
        scratch_shapes=[
            pltpu.VMEM(kc.shape, BF16), pltpu.VMEM(vc.shape, BF16), pltpu.VMEM(k_new.shape, F32),
            pltpu.VMEM(v_new.shape, F32), pltpu.VMEM(room, BF16), pltpu.VMEM(room, BF16),
            *[pltpu.VMEM(w.shape, BF16) for w in (eg_t, eu_t, ed)],
            pltpu.SemaphoreType.DMA((2,)), pltpu.SemaphoreType.DMA((4, PARTS)), pltpu.SemaphoreType.DMA((3, count))],
        compiler_params=pltpu.CompilerParams(vmem_limit_bytes=VMEM_LIMIT),
    )(plan, pos, wt_slot, k_new, v_new, kc, vc, srt, eg_t, eu_t, ed)


def back_kernel(hsum_ref, gres_ref, place_ref, srt_hbm, wg_hbm, wu_hbm, wd_hbm, out_ref,
                srt, mall, pos_col, wg, wu, wd, a_s, own, take, ring, relay_x, got_x, swap, hid,
                part_b, relay_b, got_b, full_b, send_sems, recv_sems, load_sems):
    ep, tokens, dim = mall.shape
    cap = srt.shape[0]
    ep, me, core, partner, right, left, far = ring_ids()
    tp, mt = lax.axis_size("tp"), lax.axis_index("tp")
    to_right, to_left, to_partner = {"ep": right}, {"ep": left}, {"ep": partner}
    rows_in = pieces_of(srt_hbm, srt, load_sems, 3, 1)
    loads = [pieces_of(src, dst, load_sems, i, PARTS) for i, (src, dst) in enumerate(
        [(wg_hbm, wg), (wu_hbm, wu), (wd_hbm, wd)])]
    barrier = pltpu.get_barrier_semaphore()
    peers = [{"ep": i} for i in (partner, right, left)] + [{"tp": lax.rem(mt + i, tp)} for i in (1, tp - 1)]
    for peer in peers:
        pl.semaphore_signal(barrier, inc=1, device_id=peer, device_id_type=MESH)
    for s in range(ep):
        pos_col[s] = jnp.transpose(jnp.broadcast_to(place_ref[s:s + 1, :], (tokens, tokens)))
    pl.semaphore_wait(barrier, len(peers))
    links = Links(send_sems, recv_sems)
    mid = RowSum(links, MID, "tp", hid)
    hid[mid.rows(mt, None), :] = hsum_ref[...]
    mid.spread()
    chips = [far // 2, right // 2, left // 2, me // 2]
    halfd = dim // 2
    quart = halfd // 2
    mine = pl.ds(pl.multiple_of(core * halfd, halfd), halfd)
    other = pl.ds(pl.multiple_of((1 - core) * halfd, halfd), halfd)
    lo, hi, full = pl.ds(0, quart), pl.ds(quart, quart), slice(None)

    def chip_rows(chip):
        return pl.ds(chip * 2, 2)

    def add_pair(i):
        links.recv(GIVE + i)
        for j in range(2):
            ring[i, j] = (mall[chips[i] * 2 + j, :, mine].astype(F32) + take[i, j].astype(F32)).astype(BF16)

    lane = iota((2 * tokens, tokens), 1).astype(F32)

    def scatter(i):
        where = pos_col[chip_rows(chips[i])].reshape(2 * tokens, tokens)
        pick = jnp.concatenate([(where == lane + j * tokens).astype(F32).astype(BF16)
                                for j in range(cap // tokens)], axis=1)
        for n in range(dim // COLS):
            cols = span(n, COLS)
            mall[chip_rows(chips[i]), :, cols] = mm(pick, srt[:, cols]).astype(BF16).reshape(2, tokens, COLS)
        links.send(GIVE + i, lambda: mall.at[chip_rows(chips[i]), :, other], to_partner, at(take, i))

    finish(rows_in[0:1])
    scatter(0)
    scatter(1)
    add_pair(0)
    links.send(RING, at(ring, 0, full, full, lo), to_right, at(relay_x, 0))
    links.send(RING + 1, at(ring, 0, full, full, hi), to_left, at(relay_x, 1))
    scatter(2)
    add_pair(1)
    links.send(RING + 2, at(ring, 1, full, full, hi), to_right, at(got_x, 0, 1))
    scatter(3)
    add_pair(2)
    links.send(RING + 3, at(ring, 2, full, full, lo), to_left, at(got_x, 1, 0))
    add_pair(3)
    mid.forward()
    mid.finish()
    wide = hid[...].astype(F32)
    a_s[...] = (wide * rms(wide) * gain_row(gres_ref)).astype(BF16)
    for load in loads[:2]:
        finish(load)
    acts = []
    for i in range(wg.shape[1] // COLS):
        cols = span(i, COLS)
        acts.append((jax.nn.silu(mm(a_s[...], wg[:, cols])) * mm(a_s[...], wu[:, cols])).astype(BF16))
    act = jnp.concatenate(acts, axis=1)
    finish(loads[2])
    for i in range(dim // COLS):
        cols = span(i, COLS)
        own[:, cols] = mm(act, wd[:, cols])

    for n, (dest, cols, device, side) in enumerate([(1, span(0, quart), to_right, 0), (2, span(1, quart), to_left, 1)]):
        links.recv(RING + n)
        relay_x[2 + n] = (ring[dest, :, :, cols].astype(F32) + relay_x[n].astype(F32)).astype(BF16)
        links.send(RING + 4 + n, at(relay_x, 2 + n), device, at(got_x, side, n))
    links.recv(*range(RING + 2, SWAP))

    def arrived(j):
        return jnp.concatenate(
            [ring[3, j, :, span(q, quart)].astype(F32) + got_x[0, q, j].astype(F32) + got_x[1, q, j].astype(F32)
             for q in range(2)], axis=1)

    swap[0] = arrived(1 - core).astype(BF16)
    links.send(SWAP, at(swap, 0), to_partner, at(swap, 1))
    last = RowSum(links, LAST, "tp", full_b, part_b, relay_b, got_b)
    own[:, mine] += arrived(core)
    part_b[:, mine] = own[:, mine].astype(BF16)
    links.recv(SWAP)
    own[:, other] += swap[1].astype(F32)
    part_b[:, other] = own[:, other].astype(BF16)
    last.start()
    last.pass_on()
    last.collect(own, hid)
    last.spread()
    last.forward()
    last.finish()
    out_ref[...] = full_b[...]
    links.drain()


def back(h_sum, g_res, place, srt, w_gate, w_up, w_down, tp):
    tokens, dim = h_sum.shape[0] * tp, h_sum.shape[1]
    ep = place.shape[0]
    chips, halfd, quart = ep // 2, dim // 2, dim // 4
    return pl.pallas_call(
        back_kernel,
        name="back",
        out_shape=jax.ShapeDtypeStruct((tokens, dim), BF16),
        in_specs=[VMEM, VMEM, VMEM] + [ANY] * 4,
        out_specs=VMEM,
        scratch_shapes=[
            pltpu.VMEM(srt.shape, BF16), pltpu.VMEM((ep, tokens, dim), BF16), pltpu.VMEM((ep, tokens, tokens), F32),
            *[pltpu.VMEM(w.shape, BF16) for w in (w_gate, w_up, w_down)],
            pltpu.VMEM((tokens, dim), BF16), pltpu.VMEM((tokens, dim), F32),
            pltpu.VMEM((chips, 2, tokens, halfd), BF16), pltpu.VMEM((chips, 2, tokens, halfd), BF16),
            pltpu.VMEM((4, 2, tokens, quart), BF16), pltpu.VMEM((2, 2, 2, tokens, quart), BF16),
            pltpu.VMEM((2, tokens, halfd), BF16), pltpu.VMEM((tokens, dim), BF16), *row_sum_scratch(tokens, dim, tp),
            pltpu.SemaphoreType.DMA((BACK_COPIES,)), pltpu.SemaphoreType.DMA((BACK_COPIES,)),
            pltpu.SemaphoreType.DMA((4, PARTS))],
        compiler_params=pltpu.CompilerParams(collective_id=1, has_side_effects=True, vmem_limit_bytes=VMEM_LIMIT),
    )(h_sum, g_res, place, srt, w_gate, w_up, w_down)


def solution(mesh):
    ep, tp = mesh.shape['ep'], mesh.shape['tp']
    row_spec = P(('dp', 'ep'), None)
    cache_spec = P(('dp', 'ep'), None, 'tp', None)
    col_split = P(None, 'tp')
    row_split = P('tp', None)
    in_specs = (row_spec, P(('dp', 'ep')), row_spec, cache_spec, cache_spec, P(None), P(None), P(None), col_split, col_split, col_split, row_split, col_split, col_split, row_split, P(None, None), P('ep', None, 'tp'), P('ep', None, 'tp'), P('ep', 'tp', None))
    out_specs = (row_spec, cache_spec, cache_spec)

    def local_layer(hidden_in, positions, expert_ids, k_cache, v_cache, norm_in, norm_res, norm_post, w_q, w_k, w_v, w_o, w_gate, w_up, w_down, w_router, e_gate, e_up, e_down):
        tokens, dim = hidden_in.shape
        slots, head = k_cache.shape[1], k_cache.shape[3]
        kc, vc = (cache.reshape(tokens, slots, head) for cache in (k_cache, v_cache))
        h_sum, k_new, v_new, place, plan, wt_slot, srt = front(
            hidden_in, expert_ids.T, positions, norm_in, norm_post, w_router, kc, vc, w_q, w_k, w_v, w_o,
            e_down.shape[0], ep, tp)
        out, k_out, v_out = experts(
            plan, positions, wt_slot, k_new, v_new, kc, vc, srt, jnp.swapaxes(e_gate, 1, 2), jnp.swapaxes(e_up, 1, 2), e_down)
        hidden_out = back(h_sum, norm_res, place, out, w_gate, w_up, w_down, tp)
        return hidden_out, k_out.reshape(k_cache.shape), v_out.reshape(v_cache.shape)

    return jax.shard_map(local_layer, mesh=mesh, in_specs=in_specs, out_specs=out_specs, check_vma=False)
```

time: 116 us -> 109 us (0.940); the launches traced: 115 us -> 109 us
  Pallas kernels: 114 us -> 106 us
  local copies, waits for them, and re-layouts: 0 us -> 1.88 us
    pallas_call x2 -> x3, Pallas kernels: 114 us -> 106 us  [the longest x1 41.9 us: back(): pl.pallas_call(back_kernel, name='back', out_shape=jax.ShapeDtypeStruct((...]
    unnamed x0 -> x1, local copies, waits for them, and re-layouts: none -> 1.88 us
where the time goes in v4:
time: 109 us
  Pallas kernels  106 us (97%)
  local copies, waits for them, and re-layouts  1.88 us (2%)
    pallas_call x1, Pallas kernels, back(): pl.pallas_call(back_kernel, name='back', out_shape=jax.ShapeDtypeStruct((...  41.9 us
    pallas_call x1, Pallas kernels, front(): pl.pallas_call(front_kernel, name='front', out_shape=(shape((tokens // tp...  37.2 us
    pallas_call x1, Pallas kernels, experts(): pl.pallas_call(expert_kernel, name='experts', out_shape=(shape(srt.shape,...  27.3 us

profile of v4, /device:TPU:97, one launch (start us, length us, event | category | flops | bytes accessed | tf_op | source)
XLA Modules:
  0.0 108.9 jit_solution(4328373825563736884)
XLA Ops:
  0.6 37.2 %front.1 = (bf16[32,2048]{1,0:T(8,128)(2,1)}, bf16[128,128]{1,0:T(8,128)(2,1)}, bf16[128,128]{1,0:T(8,128)(2,1)}, f32[8,128]{1,0:T(8,128)}, s32[32,128]{1,0:T(8,...) custom-call(bf16[128,2048]{1,0:T(8,128)(2,1)} %x_ref.1, s32[2,128]{1,0:T(2,128)} %bitcast.17, s32[128]{0:T(128)} %pos_ref.3, ...), custom_call_target="tpu_custom_call" | custom-call | tf_op jit(solution)/shard_map/front/pallas_call | solution.py:401
  37.8 27.3 %experts.1 = (bf16[768,2048]{1,0:T(8,128)(2,1)}, bf16[128,64,128]{2,1,0:T(8,128)(2,1)}, bf16[128,64,128]{2,1,0:T(8,128)(2,1)}) custom-call(s32[32,128]{1,0:T(8,128)} %get-tuple-element.15.plan_ref, s32[128]{0:T(128)} %pos_ref.3, f32[832,128]{1,0:T(8,128)} %get-tuple-element.16.wt_slot, bf16[128,128]{1,0:T(8,128)(2,1)} %get-tuple-element.17.knew_ref, ...), custom_call_target="tpu_custom_call" | custom-call | tf_op jit(solution)/shard_map/experts/pallas_call | solution.py:495
  65.1 41.9 %back.1 = bf16[128,2048]{1,0:T(8,128)(2,1)} custom-call(bf16[32,2048]{1,0:T(8,128)(2,1)} %get-tuple-element.13.hsum_ref, bf16[2048]{0:T(1024)(128)(2,1)} %gres_ref.1, f32[8,128]{1,0:T(8,128)} %get-tuple-element.14.place_ref, bf16[768,2048]{1,0:T(8,128)(2,1)} %get-tuple-element.20.srt_hbm, bf16[2048,1536]{1,0:T(8,128)(2,1)} %wg_hbm.1, ...), custom_call_target="tpu_custom_call" | custom-call | tf_op jit(solution)/shard_map/back/pallas_call | solution.py:620
  107.0 1.9 %copy.25 = bf16[128,2048]{1,0:T(8,128)(2,1)} copy(bf16[128,2048]{1,0:T(8,128)(2,1)} %back.1) | data formatting | bytes 1048576

commit v5 on v4

--- a/solution.py
+++ b/solution.py
@@ -15,7 +15,7 @@
 BF16 = jnp.bfloat16
 WIN = 64
 ALIGN = 16
-AHEAD = 8
+AHEAD = 6
 COLS = 512
 PARTS = 4
 VMEM_LIMIT = 67000000
@@ -416,76 +416,102 @@
 
 
 def expert_kernel(plan_ref, pos_ref, wt_slot, knew_ref, vnew_ref, kc_hbm, vc_hbm, srt_hbm, eg_hbm, eu_hbm, ed_hbm,
-                  out_hbm, ko_hbm, vo_hbm, kc, vc, k_s, v_s, rows, out, eg, eu, ed, rows_sem, cache_sems, w_sems):
+                  out_hbm, ko_hbm, vo_hbm, kc, vc, k_s, v_s, rows, out, gate_s, up_s, eg, eu, ed, rows_sem, cache_sems, w_sems):
     count = eg.shape[0]
     tokens, _, head = kc.shape
     cap, dim = srt_hbm.shape
-
-    def weights(e):
-        return [pltpu.make_async_copy(src.at[e], dst.at[e], w_sems.at[i, e])
-                for i, (src, dst) in enumerate([(eg_hbm, eg), (eu_hbm, eu), (ed_hbm, ed)])]
-
+    step = tokens // count
     news = ((k_s, kc, kc_hbm, ko_hbm), (v_s, vc, vc_hbm, vo_hbm))
+
+    def some(e):
+        return pl.ds(e * step, step)
+
+    def comes(e):
+        copies = [pltpu.make_async_copy(src.at[e], dst.at[e], w_sems.at[i, e])
+                  for i, (src, dst) in enumerate([(eg_hbm, eg), (eu_hbm, eu), (ed_hbm, ed)])]
+        return copies + [pltpu.make_async_copy(src.at[some(e)], buf.at[some(e)], cache_sems.at[i, e])
+                         for i, (_, buf, src, _) in enumerate(news)]
+
+    def goes(e):
+        return [pltpu.make_async_copy(buf.at[some(e)], dst.at[some(e)], cache_sems.at[2 + i, e])
+                for i, (_, buf, _, dst) in enumerate(news)]
+
     rows_copy = pltpu.make_async_copy(srt_hbm, rows.at[pl.ds(0, cap)], rows_sem.at[0])
     rows_copy.start()
-    came = [pieces_of(src, buf, cache_sems, i, PARTS) for i, (_, buf, src, _) in enumerate(news)]
     for e in range(AHEAD):
-        for copy in weights(e):
+        for copy in comes(e):
             copy.start()
     k_s[...] = knew_ref[...].astype(F32)
     v_s[...] = vnew_ref[...].astype(F32)
     out[...] = jnp.zeros_like(out)
-    step = tokens // PARTS
-    goes = []
-    for n in range(PARTS):
-        for i, (new, buf, _, dst) in enumerate(news):
-            came[i][n].wait()
-
-            def new_rows(g, carry):
-                for j in range(8):
-                    b = n * step + g * 8 + j
-                    spot = pos_ref[b]
-                    base = pl.multiple_of(spot // ALIGN * ALIGN, ALIGN)
-                    hit = iota((ALIGN, head), 0) == spot - base
-                    tile = buf[b, pl.ds(base, ALIGN), :].astype(F32)
-                    buf[b, pl.ds(base, ALIGN), :] = jnp.where(hit, new[pl.ds(b, 1), :], tile).astype(BF16)
-                return carry
-
-            lax.fori_loop(0, step // 8, new_rows, 0)
-            part = pl.ds(n * step, step)
-            goes.append(pltpu.make_async_copy(buf.at[part], dst.at[part], cache_sems.at[2 + i, n]))
-            goes[-1].start()
     rows_copy.wait()
 
-    def run_expert(e, carry):
-        @pl.when(e + AHEAD < count)
+    def new_rows(e):
+        for new, buf, _, _ in news:
+            for j in range(step):
+                b = e * step + j
+                spot = pos_ref[b]
+                base = pl.multiple_of(spot // ALIGN * ALIGN, ALIGN)
+                hit = iota((ALIGN, head), 0) == spot - base
+                tile = buf[b, pl.ds(base, ALIGN), :].astype(F32)
+                buf[b, pl.ds(base, ALIGN), :] = jnp.where(hit, new[pl.ds(b, 1), :], tile).astype(BF16)
+
+    def window(e, p):
+        return pl.ds(pl.multiple_of(plan_ref[count + e, 0] + p * WIN, ALIGN), WIN)
+
+    def widen(e, here):
+        x = rows[here, :]
+        return nt_dot(eg[e], x), nt_dot(eu[e], x)
+
+    def narrow(e, here, gate, up):
+        act = jnp.transpose(jax.nn.silu(gate) * up).astype(BF16)
+        wt = wt_slot[here, :][:, 0:1]
+        for i in range(dim // COLS):
+            cols = span(i, COLS)
+            out[here, cols] = (mm(act, ed[e, :, cols]) * wt).astype(BF16)
+
+    def others(e):
+        def one(p, carry):
+            narrow(e, window(e, p), *widen(e, window(e, p)))
+            return carry
+
+        lax.fori_loop(1, (plan_ref[e, 0] + (WIN - 1)) // WIN, one, 0)
+
+    def begin(e):
+        gate, up = widen(e, window(e, 0))
+        gate_s[...] = gate
+        up_s[...] = up
+
+    finish(comes(0))
+    begin(0)
+    new_rows(0)
+    for copy in goes(0):
+        copy.start()
+
+    def run(e, carry):
+        @pl.when(e + (AHEAD - 1) < count)
         def _():
-            for copy in weights(e + AHEAD):
+            for copy in comes(e + (AHEAD - 1)):
                 copy.start()
 
-        for copy in weights(e):
-            copy.wait()
-        passes = (plan_ref[e, 0] + (WIN - 1)) // WIN
-        begin = plan_ref[count + e, 0]
-
-        def one_pass(p, inner):
-            here = pl.ds(pl.multiple_of(begin + p * WIN, ALIGN), WIN)
-            x = rows[here, :]
-            act = jnp.transpose(jax.nn.silu(nt_dot(eg[e], x)) * nt_dot(eu[e], x)).astype(BF16)
-            wt = wt_slot[here, :][:, 0:1]
-            for i in range(dim // COLS):
-                cols = span(i, COLS)
-                out[here, cols] = (mm(act, ed[e, :, cols]) * wt).astype(BF16)
-            return inner
-
-        lax.fori_loop(0, passes, one_pass, 0)
+        finish(comes(e))
+        narrow(e - 1, window(e - 1, 0), gate_s[...], up_s[...])
+        begin(e)
+        new_rows(e)
+        for copy in goes(e):
+            copy.start()
+        others(e - 1)
         return carry
 
-    lax.fori_loop(0, count, run_expert, 0)
+    lax.fori_loop(1, count, run, 0)
+    last = count - 1
+    narrow(last, window(last, 0), gate_s[...], up_s[...])
+    others(last)
     out_copy = pltpu.make_async_copy(out.at[pl.ds(0, cap)], out_hbm, rows_sem.at[1])
     out_copy.start()
     out_copy.wait()
-    finish(goes)
+    for e in range(count):
+        finish(goes(e))
 
 
 def experts(plan, pos, wt_slot, k_new, v_new, kc, vc, srt, eg_t, eu_t, ed):
@@ -501,8 +527,9 @@
         scratch_shapes=[
             pltpu.VMEM(kc.shape, BF16), pltpu.VMEM(vc.shape, BF16), pltpu.VMEM(k_new.shape, F32),
             pltpu.VMEM(v_new.shape, F32), pltpu.VMEM(room, BF16), pltpu.VMEM(room, BF16),
+            pltpu.VMEM((eg_t.shape[1], WIN), F32), pltpu.VMEM((eg_t.shape[1], WIN), F32),
             *[pltpu.VMEM(w.shape, BF16) for w in (eg_t, eu_t, ed)],
-            pltpu.SemaphoreType.DMA((2,)), pltpu.SemaphoreType.DMA((4, PARTS)), pltpu.SemaphoreType.DMA((3, count))],
+            pltpu.SemaphoreType.DMA((2,)), pltpu.SemaphoreType.DMA((4, count)), pltpu.SemaphoreType.DMA((3, count))],
         compiler_params=pltpu.CompilerParams(vmem_limit_bytes=VMEM_LIMIT),
     )(plan, pos, wt_slot, k_new, v_new, kc, vc, srt, eg_t, eu_t, ed)
 

time: 109 us -> 105 us (0.963)
  Pallas kernels: 106 us -> 102 us
    pallas_call x1, Pallas kernels: 27.3 us -> 22.7 us  [experts(): pl.pallas_call(expert_kernel, name='experts', out_shape=(shape(srt.shape,...]
where the time goes in v5:
time: 105 us; the launch traced here: 104 us
  Pallas kernels  102 us (97%)
  local copies, waits for them, and re-layouts  1.88 us (2%)
    pallas_call x1, Pallas kernels, back(): pl.pallas_call(back_kernel, name='back', out_shape=jax.ShapeDtypeStruct((...  41.9 us
    pallas_call x1, Pallas kernels, front(): pl.pallas_call(front_kernel, name='front', out_shape=(shape((tokens // tp...  37.2 us
    pallas_call x1, Pallas kernels, experts(): pl.pallas_call(expert_kernel, name='experts', out_shape=(shape(srt.shape,...  22.7 us

profile of v5, /device:TPU:97, one launch (start us, length us, event | category | flops | bytes accessed | tf_op | source)
XLA Modules:
  0.0 104.4 jit_solution(9771243346510420802)
XLA Ops:
  0.6 37.2 %front.1 = (bf16[32,2048]{1,0:T(8,128)(2,1)}, bf16[128,128]{1,0:T(8,128)(2,1)}, bf16[128,128]{1,0:T(8,128)(2,1)}, f32[8,128]{1,0:T(8,128)}, s32[32,128]{1,0:T(8,...) custom-call(bf16[128,2048]{1,0:T(8,128)(2,1)} %x_ref.1, s32[2,128]{1,0:T(2,128)} %bitcast.17, s32[128]{0:T(128)} %pos_ref.3, ...), custom_call_target="tpu_custom_call" | custom-call | tf_op jit(solution)/shard_map/front/pallas_call | solution.py:401
  37.8 22.7 %experts.1 = (bf16[768,2048]{1,0:T(8,128)(2,1)}, bf16[128,64,128]{2,1,0:T(8,128)(2,1)}, bf16[128,64,128]{2,1,0:T(8,128)(2,1)}) custom-call(s32[32,128]{1,0:T(8,128)} %get-tuple-element.15.plan_ref, s32[128]{0:T(128)} %pos_ref.3, f32[832,128]{1,0:T(8,128)} %get-tuple-element.16.wt_slot, bf16[128,128]{1,0:T(8,128)(2,1)} %get-tuple-element.17.knew_ref, ...), custom_call_target="tpu_custom_call" | custom-call | tf_op jit(solution)/shard_map/experts/pallas_call | solution.py:521
  60.5 41.9 %back.1 = bf16[128,2048]{1,0:T(8,128)(2,1)} custom-call(bf16[32,2048]{1,0:T(8,128)(2,1)} %get-tuple-element.13.hsum_ref, bf16[2048]{0:T(1024)(128)(2,1)} %gres_ref.1, f32[8,128]{1,0:T(8,128)} %get-tuple-element.14.place_ref, bf16[768,2048]{1,0:T(8,128)(2,1)} %get-tuple-element.20.srt_hbm, bf16[2048,1536]{1,0:T(8,128)(2,1)} %wg_hbm.1, ...), custom_call_target="tpu_custom_call" | custom-call | tf_op jit(solution)/shard_map/back/pallas_call | solution.py:647
  102.5 1.9 %copy.25 = bf16[128,2048]{1,0:T(8,128)(2,1)} copy(bf16[128,2048]{1,0:T(8,128)(2,1)} %back.1) | data formatting | bytes 1048576

commit v6 on v5

--- a/solution.py
+++ b/solution.py
@@ -13,7 +13,7 @@
 MESH = pl.DeviceIdType.MESH
 F32 = jnp.float32
 BF16 = jnp.bfloat16
-WIN = 64
+WIN = 48
 ALIGN = 16
 AHEAD = 6
 COLS = 512
@@ -142,8 +142,8 @@
         self.recv(2, 3, 4, 5)
         for half in range(2):
             here = self.rows(self.me, half)
-            acc = own[here, :] + self.got[0, half].astype(F32) + self.got[1, half].astype(F32)
-            self.full[here, :] = (rest[here, :].astype(F32) + acc).astype(BF16)
+            acc = own(here) + self.got[0, half].astype(F32) + self.got[1, half].astype(F32)
+            self.full[here, :] = (rest(here).astype(F32) + acc).astype(BF16)
 
     def spread(self):
         for n, device in enumerate([self.to_right, self.to_left]):
@@ -175,7 +175,8 @@
 
 
 ROWS, ATT, FAR, META, TWIN, FRONT_COPIES = 0, 5, 17, 20, 28, 34
-GIVE, RING, SWAP, LAST, MID, BACK_COPIES = 0, 4, 10, 11, 23, 35
+GIVE, RING, SWAP, LAST, MID, BACK_COPIES = 0, 4, 16, 18, 42, 54
+GROUPS = 2
 
 
 def front_kernel(x_ref, ids_ref, pos_ref, gin_ref, gpost_ref, wr_ref, kc_hbm, vc_hbm, wq_hbm, wk_hbm, wv_hbm, wo_hbm,
@@ -375,7 +376,7 @@
     for n, (block, h) in enumerate([(left, 1), (right, 0)]):
         links.recv(ROWS + 2 + n)
         links.send(TWIN + 2 + n, half(block, h), to_partner)
-    att_sum.collect(own, x_ref)
+    att_sum.collect(lambda here: own[here, :], lambda here: x_ref[here, :])
     hsum_ref[...] = hid[att_sum.rows(mt, None), :]
     for n, block in enumerate([left, right]):
         links.recv(TWIN + n, TWIN + 2 + n)
@@ -536,7 +537,7 @@
 
 def back_kernel(hsum_ref, gres_ref, place_ref, srt_hbm, wg_hbm, wu_hbm, wd_hbm, out_ref,
                 srt, mall, pos_col, wg, wu, wd, a_s, own, take, ring, relay_x, got_x, swap, hid,
-                part_b, relay_b, got_b, full_b, send_sems, recv_sems, load_sems):
+                part_a, relay_a, got_a, full_a, part_b, relay_b, got_b, full_b, send_sems, recv_sems, load_sems):
     ep, tokens, dim = mall.shape
     cap = srt.shape[0]
     ep, me, core, partner, right, left, far = ring_ids()
@@ -558,10 +559,14 @@
     mid.spread()
     chips = [far // 2, right // 2, left // 2, me // 2]
     halfd = dim // 2
-    quart = halfd // 2
+    width = halfd // GROUPS
+    piece = width // 2
     mine = pl.ds(pl.multiple_of(core * halfd, halfd), halfd)
     other = pl.ds(pl.multiple_of((1 - core) * halfd, halfd), halfd)
-    lo, hi, full = pl.ds(0, quart), pl.ds(quart, quart), slice(None)
+    full = slice(None)
+
+    def part_of(g, q):
+        return pl.ds(g * width + q * piece, piece)
 
     def chip_rows(chip):
         return pl.ds(chip * 2, 2)
@@ -586,14 +591,21 @@
     scatter(0)
     scatter(1)
     add_pair(0)
-    links.send(RING, at(ring, 0, full, full, lo), to_right, at(relay_x, 0))
-    links.send(RING + 1, at(ring, 0, full, full, hi), to_left, at(relay_x, 1))
+    for g in range(GROUPS):
+        for q, device in enumerate([to_right, to_left]):
+            links.send(RING + 6 * g + q, at(ring, 0, full, full, part_of(g, q)), device, at(relay_x, g, q))
+
+    def direct(g, side):
+        q = 1 - side
+        links.send(RING + 6 * g + 2 + side, at(ring, 1 + side, full, full, part_of(g, q)), (to_right, to_left)[side],
+                   at(got_x, g, side, q))
+
     scatter(2)
     add_pair(1)
-    links.send(RING + 2, at(ring, 1, full, full, hi), to_right, at(got_x, 0, 1))
+    direct(0, 0)
     scatter(3)
     add_pair(2)
-    links.send(RING + 3, at(ring, 2, full, full, lo), to_left, at(got_x, 1, 0))
+    direct(0, 1)
     add_pair(3)
     mid.forward()
     mid.finish()
@@ -611,39 +623,71 @@
         cols = span(i, COLS)
         own[:, cols] = mm(act, wd[:, cols])
 
-    for n, (dest, cols, device, side) in enumerate([(1, span(0, quart), to_right, 0), (2, span(1, quart), to_left, 1)]):
-        links.recv(RING + n)
-        relay_x[2 + n] = (ring[dest, :, :, cols].astype(F32) + relay_x[n].astype(F32)).astype(BF16)
-        links.send(RING + 4 + n, at(relay_x, 2 + n), device, at(got_x, side, n))
-    links.recv(*range(RING + 2, SWAP))
-
-    def arrived(j):
+    for g in range(GROUPS):
+        for q, device in enumerate([to_right, to_left]):
+            links.recv(RING + 6 * g + q)
+            relay_x[g, 2 + q] = (ring[1 + q, :, :, part_of(g, q)].astype(F32) + relay_x[g, q].astype(F32)).astype(BF16)
+            links.send(RING + 6 * g + 4 + q, at(relay_x, g, 2 + q), device, at(got_x, g, q, q))
+        if g + 1 < GROUPS:
+            for side in range(2):
+                direct(g + 1, side)
+
+    def arrived(g, j):
         return jnp.concatenate(
-            [ring[3, j, :, span(q, quart)].astype(F32) + got_x[0, q, j].astype(F32) + got_x[1, q, j].astype(F32)
+            [ring[3, j, :, part_of(g, q)].astype(F32) + got_x[g, 0, q, j].astype(F32) + got_x[g, 1, q, j].astype(F32)
              for q in range(2)], axis=1)
 
-    swap[0] = arrived(1 - core).astype(BF16)
-    links.send(SWAP, at(swap, 0), to_partner, at(swap, 1))
-    last = RowSum(links, LAST, "tp", full_b, part_b, relay_b, got_b)
-    own[:, mine] += arrived(core)
-    part_b[:, mine] = own[:, mine].astype(BF16)
-    links.recv(SWAP)
-    own[:, other] += swap[1].astype(F32)
-    part_b[:, other] = own[:, other].astype(BF16)
-    last.start()
-    last.pass_on()
-    last.collect(own, hid)
-    last.spread()
-    last.forward()
-    last.finish()
-    out_ref[...] = full_b[...]
+    def columns(half, g):
+        return pl.ds(pl.multiple_of(half * halfd + g * width, width), width)
+
+    def view(ref, g):
+        return lambda here: jnp.concatenate([ref[here, columns(half, g)] for half in range(2)], axis=1)
+
+    buffers = [(full_a, part_a, relay_a, got_a), (full_b, part_b, relay_b, got_b)]
+    last = [RowSum(links, LAST + 12 * g, "tp", *buffers[g]) for g in range(GROUPS)]
+
+    def add_half(g, half, value):
+        own[:, columns(half, g)] += value
+        buffers[g][1][:, pl.ds(pl.multiple_of(half * width, width), width)] = own[:, columns(half, g)].astype(BF16)
+
+    def come(g):
+        links.recv(*range(RING + 6 * g + 2, RING + 6 * g + 6))
+        swap[g, 0] = arrived(g, 1 - core).astype(BF16)
+        links.send(SWAP + g, at(swap, g, 0), to_partner, at(swap, g, 1))
+        add_half(g, core, arrived(g, core))
+
+    def go(g):
+        links.recv(SWAP + g)
+        add_half(g, 1 - core, swap[g, 1].astype(F32))
+        last[g].start()
+
+    def collect(g):
+        last[g].collect(view(own, g), view(hid, g))
+        last[g].spread()
+
+    come(0)
+    go(0)
+    last[0].pass_on()
+    come(1)
+    collect(0)
+    go(1)
+    last[0].forward()
+    last[1].pass_on()
+    last[0].finish()
+    collect(1)
+    last[1].forward()
+    last[1].finish()
+    for g in range(GROUPS):
+        for half in range(2):
+            out_ref[:, columns(half, g)] = buffers[g][0][:, span(half, width)]
     links.drain()
 
 
 def back(h_sum, g_res, place, srt, w_gate, w_up, w_down, tp):
     tokens, dim = h_sum.shape[0] * tp, h_sum.shape[1]
     ep = place.shape[0]
-    chips, halfd, quart = ep // 2, dim // 2, dim // 4
+    chips, halfd = ep // 2, dim // 2
+    width = halfd // GROUPS
     return pl.pallas_call(
         back_kernel,
         name="back",
@@ -655,8 +699,9 @@
             *[pltpu.VMEM(w.shape, BF16) for w in (w_gate, w_up, w_down)],
             pltpu.VMEM((tokens, dim), BF16), pltpu.VMEM((tokens, dim), F32),
             pltpu.VMEM((chips, 2, tokens, halfd), BF16), pltpu.VMEM((chips, 2, tokens, halfd), BF16),
-            pltpu.VMEM((4, 2, tokens, quart), BF16), pltpu.VMEM((2, 2, 2, tokens, quart), BF16),
-            pltpu.VMEM((2, tokens, halfd), BF16), pltpu.VMEM((tokens, dim), BF16), *row_sum_scratch(tokens, dim, tp),
+            pltpu.VMEM((GROUPS, 4, 2, tokens, width // 2), BF16), pltpu.VMEM((GROUPS, 2, 2, 2, tokens, width // 2), BF16),
+            pltpu.VMEM((GROUPS, 2, tokens, width), BF16), pltpu.VMEM((tokens, dim), BF16),
+            *row_sum_scratch(tokens, 2 * width, tp), *row_sum_scratch(tokens, 2 * width, tp),
             pltpu.SemaphoreType.DMA((BACK_COPIES,)), pltpu.SemaphoreType.DMA((BACK_COPIES,)),
             pltpu.SemaphoreType.DMA((4, PARTS))],
         compiler_params=pltpu.CompilerParams(collective_id=1, has_side_effects=True, vmem_limit_bytes=VMEM_LIMIT),

time: 105 us -> 108 us (1.029)
  the two profiles are of different devices: /device:TPU:97 before, /device:TPU:104 now
where the time goes in v6:
time: 108 us
  Pallas kernels  105 us (97%)
  local copies, waits for them, and re-layouts  1.88 us (2%)
    pallas_call x1, Pallas kernels, back(): pl.pallas_call(back_kernel, name='back', out_shape=jax.ShapeDtypeStruct((...  48.9 us
    pallas_call x1, Pallas kernels, front(): pl.pallas_call(front_kernel, name='front', out_shape=(shape((tokens // tp...  33.6 us
    pallas_call x1, Pallas kernels, experts(): pl.pallas_call(expert_kernel, name='experts', out_shape=(shape(srt.shape,...  22.5 us

profile of v6, /device:TPU:104, one launch (start us, length us, event | category | flops | bytes accessed | tf_op | source)
XLA Modules:
  0.0 107.6 jit_solution(7020092404471426653)
XLA Ops:
  0.6 33.6 %front.1 = (bf16[32,2048]{1,0:T(8,128)(2,1)}, bf16[128,128]{1,0:T(8,128)(2,1)}, bf16[128,128]{1,0:T(8,128)(2,1)}, f32[8,128]{1,0:T(8,128)}, s32[32,128]{1,0:T(8,...) custom-call(bf16[128,2048]{1,0:T(8,128)(2,1)} %x_ref.1, s32[2,128]{1,0:T(2,128)} %bitcast.17, s32[128]{0:T(128)} %pos_ref.3, ...), custom_call_target="tpu_custom_call" | custom-call | tf_op jit(solution)/shard_map/front/pallas_call | solution.py:402
  34.2 22.5 %experts.1 = (bf16[768,2048]{1,0:T(8,128)(2,1)}, bf16[128,64,128]{2,1,0:T(8,128)(2,1)}, bf16[128,64,128]{2,1,0:T(8,128)(2,1)}) custom-call(s32[32,128]{1,0:T(8,128)} %get-tuple-element.15.plan_ref, s32[128]{0:T(128)} %pos_ref.3, f32[816,128]{1,0:T(8,128)} %get-tuple-element.16.wt_slot, bf16[128,128]{1,0:T(8,128)(2,1)} %get-tuple-element.17.knew_ref, ...), custom_call_target="tpu_custom_call" | custom-call | tf_op jit(solution)/shard_map/experts/pallas_call | solution.py:522
  56.8 48.9 %back.1 = bf16[128,2048]{1,0:T(8,128)(2,1)} custom-call(bf16[32,2048]{1,0:T(8,128)(2,1)} %get-tuple-element.13.hsum_ref, bf16[2048]{0:T(1024)(128)(2,1)} %gres_ref.1, f32[8,128]{1,0:T(8,128)} %get-tuple-element.14.place_ref, bf16[768,2048]{1,0:T(8,128)(2,1)} %get-tuple-element.20.srt_hbm, bf16[2048,1536]{1,0:T(8,128)(2,1)} %wg_hbm.1, ...), custom_call_target="tpu_custom_call" | custom-call | tf_op jit(solution)/shard_map/back/pallas_call | solution.py:691
  105.7 1.9 %copy.25 = bf16[128,2048]{1,0:T(8,128)(2,1)} copy(bf16[128,2048]{1,0:T(8,128)(2,1)} %back.1) | data formatting | bytes 1048576

commit v7 on v5

--- a/solution.py
+++ b/solution.py
@@ -535,9 +535,9 @@
 
 
 def back_kernel(hsum_ref, gres_ref, place_ref, srt_hbm, wg_hbm, wu_hbm, wd_hbm, out_ref,
-                srt, mall, pos_col, wg, wu, wd, a_s, own, take, ring, relay_x, got_x, swap, hid,
+                srt, sums, pos_col, wg, wu, wd, a_s, own, take, ring, relay_x, got_x, swap, hid,
                 part_b, relay_b, got_b, full_b, send_sems, recv_sems, load_sems):
-    ep, tokens, dim = mall.shape
+    tokens, dim = hid.shape
     cap = srt.shape[0]
     ep, me, core, partner, right, left, far = ring_ids()
     tp, mt = lax.axis_size("tp"), lax.axis_index("tp")
@@ -561,15 +561,15 @@
     quart = halfd // 2
     mine = pl.ds(pl.multiple_of(core * halfd, halfd), halfd)
     other = pl.ds(pl.multiple_of((1 - core) * halfd, halfd), halfd)
-    lo, hi, full = pl.ds(0, quart), pl.ds(quart, quart), slice(None)
 
     def chip_rows(chip):
         return pl.ds(chip * 2, 2)
 
     def add_pair(i):
         links.recv(GIVE + i)
-        for j in range(2):
-            ring[i, j] = (mall[chips[i] * 2 + j, :, mine].astype(F32) + take[i, j].astype(F32)).astype(BF16)
+        for q in range(2):
+            cols = span(q, quart)
+            ring[i, q] = (sums[i, core, :, :, cols].astype(F32) + take[i, :, :, cols].astype(F32)).astype(BF16)
 
     lane = iota((2 * tokens, tokens), 1).astype(F32)
 
@@ -579,21 +579,22 @@
                                 for j in range(cap // tokens)], axis=1)
         for n in range(dim // COLS):
             cols = span(n, COLS)
-            mall[chip_rows(chips[i]), :, cols] = mm(pick, srt[:, cols]).astype(BF16).reshape(2, tokens, COLS)
-        links.send(GIVE + i, lambda: mall.at[chip_rows(chips[i]), :, other], to_partner, at(take, i))
+            side, part = divmod(n, halfd // COLS)
+            sums[i, side, :, :, span(part, COLS)] = mm(pick, srt[:, cols]).astype(BF16).reshape(2, tokens, COLS)
+        links.send(GIVE + i, at(sums, i, 1 - core), to_partner, at(take, i))
 
     finish(rows_in[0:1])
     scatter(0)
     scatter(1)
     add_pair(0)
-    links.send(RING, at(ring, 0, full, full, lo), to_right, at(relay_x, 0))
-    links.send(RING + 1, at(ring, 0, full, full, hi), to_left, at(relay_x, 1))
+    links.send(RING, at(ring, 0, 0), to_right, at(relay_x, 0))
+    links.send(RING + 1, at(ring, 0, 1), to_left, at(relay_x, 1))
     scatter(2)
     add_pair(1)
-    links.send(RING + 2, at(ring, 1, full, full, hi), to_right, at(got_x, 0, 1))
+    links.send(RING + 2, at(ring, 1, 1), to_right, at(got_x, 0, 1))
     scatter(3)
     add_pair(2)
-    links.send(RING + 3, at(ring, 2, full, full, lo), to_left, at(got_x, 1, 0))
+    links.send(RING + 3, at(ring, 2, 0), to_left, at(got_x, 1, 0))
     add_pair(3)
     mid.forward()
     mid.finish()
@@ -611,15 +612,15 @@
         cols = span(i, COLS)
         own[:, cols] = mm(act, wd[:, cols])
 
-    for n, (dest, cols, device, side) in enumerate([(1, span(0, quart), to_right, 0), (2, span(1, quart), to_left, 1)]):
+    for n, (dest, device, side) in enumerate([(1, to_right, 0), (2, to_left, 1)]):
         links.recv(RING + n)
-        relay_x[2 + n] = (ring[dest, :, :, cols].astype(F32) + relay_x[n].astype(F32)).astype(BF16)
+        relay_x[2 + n] = (ring[dest, n].astype(F32) + relay_x[n].astype(F32)).astype(BF16)
         links.send(RING + 4 + n, at(relay_x, 2 + n), device, at(got_x, side, n))
     links.recv(*range(RING + 2, SWAP))
 
     def arrived(j):
         return jnp.concatenate(
-            [ring[3, j, :, span(q, quart)].astype(F32) + got_x[0, q, j].astype(F32) + got_x[1, q, j].astype(F32)
+            [ring[3, q, j].astype(F32) + got_x[0, q, j].astype(F32) + got_x[1, q, j].astype(F32)
              for q in range(2)], axis=1)
 
     swap[0] = arrived(1 - core).astype(BF16)
@@ -651,10 +652,10 @@
         in_specs=[VMEM, VMEM, VMEM] + [ANY] * 4,
         out_specs=VMEM,
         scratch_shapes=[
-            pltpu.VMEM(srt.shape, BF16), pltpu.VMEM((ep, tokens, dim), BF16), pltpu.VMEM((ep, tokens, tokens), F32),
+            pltpu.VMEM(srt.shape, BF16), pltpu.VMEM((chips, 2, 2, tokens, halfd), BF16), pltpu.VMEM((ep, tokens, tokens), F32),
             *[pltpu.VMEM(w.shape, BF16) for w in (w_gate, w_up, w_down)],
             pltpu.VMEM((tokens, dim), BF16), pltpu.VMEM((tokens, dim), F32),
-            pltpu.VMEM((chips, 2, tokens, halfd), BF16), pltpu.VMEM((chips, 2, tokens, halfd), BF16),
+            pltpu.VMEM((chips, 2, tokens, halfd), BF16), pltpu.VMEM((chips, 2, 2, tokens, quart), BF16),
             pltpu.VMEM((4, 2, tokens, quart), BF16), pltpu.VMEM((2, 2, 2, tokens, quart), BF16),
             pltpu.VMEM((2, tokens, halfd), BF16), pltpu.VMEM((tokens, dim), BF16), *row_sum_scratch(tokens, dim, tp),
             pltpu.SemaphoreType.DMA((BACK_COPIES,)), pltpu.SemaphoreType.DMA((BACK_COPIES,)),

time: 105 us -> 105 us (level)
  no operation moved by 1% of the time
where the time goes in v7:
time: 105 us; the launch traced here: 104 us
  Pallas kernels  102 us (97%)
  local copies, waits for them, and re-layouts  1.88 us (2%)
    pallas_call x1, Pallas kernels, back(): pl.pallas_call(back_kernel, name='back', out_shape=jax.ShapeDtypeStruct((...  41.8 us
    pallas_call x1, Pallas kernels, front(): pl.pallas_call(front_kernel, name='front', out_shape=(shape((tokens // tp...  37.2 us
    pallas_call x1, Pallas kernels, experts(): pl.pallas_call(expert_kernel, name='experts', out_shape=(shape(srt.shape,...  22.7 us

profile of v7, /device:TPU:97, one launch (start us, length us, event | category | flops | bytes accessed | tf_op | source)
XLA Modules:
  0.0 104.2 jit_solution(1670872914853476614)
XLA Ops:
  0.6 37.2 %front.1 = (bf16[32,2048]{1,0:T(8,128)(2,1)}, bf16[128,128]{1,0:T(8,128)(2,1)}, bf16[128,128]{1,0:T(8,128)(2,1)}, f32[8,128]{1,0:T(8,128)}, s32[32,128]{1,0:T(8,...) custom-call(bf16[128,2048]{1,0:T(8,128)(2,1)} %x_ref.1, s32[2,128]{1,0:T(2,128)} %bitcast.17, s32[128]{0:T(128)} %pos_ref.3, ...), custom_call_target="tpu_custom_call" | custom-call | tf_op jit(solution)/shard_map/front/pallas_call | solution.py:401
  37.8 22.7 %experts.1 = (bf16[768,2048]{1,0:T(8,128)(2,1)}, bf16[128,64,128]{2,1,0:T(8,128)(2,1)}, bf16[128,64,128]{2,1,0:T(8,128)(2,1)}) custom-call(s32[32,128]{1,0:T(8,128)} %get-tuple-element.15.plan_ref, s32[128]{0:T(128)} %pos_ref.3, f32[832,128]{1,0:T(8,128)} %get-tuple-element.16.wt_slot, bf16[128,128]{1,0:T(8,128)(2,1)} %get-tuple-element.17.knew_ref, ...), custom_call_target="tpu_custom_call" | custom-call | tf_op jit(solution)/shard_map/experts/pallas_call | solution.py:521
  60.5 41.8 %back.1 = bf16[128,2048]{1,0:T(8,128)(2,1)} custom-call(bf16[32,2048]{1,0:T(8,128)(2,1)} %get-tuple-element.13.hsum_ref, bf16[2048]{0:T(1024)(128)(2,1)} %gres_ref.1, f32[8,128]{1,0:T(8,128)} %get-tuple-element.14.place_ref, bf16[768,2048]{1,0:T(8,128)(2,1)} %get-tuple-element.20.srt_hbm, bf16[2048,1536]{1,0:T(8,128)(2,1)} %wg_hbm.1, ...), custom_call_target="tpu_custom_call" | custom-call | tf_op jit(solution)/shard_map/back/pallas_call | solution.py:648
  102.3 1.9 %copy.25 = bf16[128,2048]{1,0:T(8,128)(2,1)} copy(bf16[128,2048]{1,0:T(8,128)(2,1)} %back.1) | data formatting | bytes 1048576
